TPU v7x, 256 devices: a whole 4x4x8 slice. The times are simulated.
256 devices in a mesh: seq: 16 (over z, core), tp: 16 (over y, x).
Axes of the slice: x: 4, y: 4, z: 8, core: 2. Of those that a mesh axis runs over, the one named last changes fastest.
Arguments:
- latents: bfloat16 [16, 8192, 512], P(None, ('seq', 'tp')), may hold values from -6 to 6
- rotary_rows: bfloat16 [16, 8192, 64], P(None, ('seq', 'tp')), may hold values from -6 to 6
- latent_gain: float32 [512], replicated, may hold values from 0.25 to 1.75
- key_up: bfloat16 [512, 16, 128], P(None, 'tp'), may hold values from -0.25 to 0.25
- value_up: bfloat16 [512, 16, 128], P(None, 'tp'), may hold values from -0.25 to 0.25
Outputs:
- decode_keys: bfloat16 [16, 16, 192, 8192], P('seq', 'tp')
- decode_values: bfloat16 [16, 8192, 16, 128], P('seq', None, 'tp')
All inputs are finite; a program needn't handle non-finite values.
Results may differ from a plain program's by a relative error of at most 0.0049.
Values may be sent and summed in bfloat16 or wider, within the bound.
No kernel may reach another device: no remote copies, remote signals or barrier semaphores. Data moves between devices by JAX's collectives and lax.ppermute only.
A program may use at most 64 MiB of HBM per device.

v0:
```python
import jax
import jax.numpy as jnp
from jax import lax
from jax.sharding import PartitionSpec as P


def in_one_piece(arrays, axis, split_dim, concat_dim, along):
    both = jnp.concatenate(arrays, axis=along)
    filled, at, done = (
        lax.all_to_all(both, axis, split_axis=split_dim, concat_axis=concat_dim, tiled=True),
        0,
        [],
    )
    for a in arrays:
        done.append(lax.slice_in_dim(filled, at, at + a.shape[along], axis=along))
        at += a.shape[along]
    return tuple(done)


def in_one_piece_2(arrays, axis, dim, along):
    both = jnp.concatenate(arrays, axis=along)
    filled, at, done = (lax.all_gather(both, axis, axis=dim, tiled=True), 0, [])
    for a in arrays:
        done.append(lax.slice_in_dim(filled, at, at + a.shape[along], axis=along))
        at += a.shape[along]
    return tuple(done)


def expand_rows(rows, rotary, key_up, value_up):
    wide_keys = jnp.einsum(
        "btr,rhk->bthk", rows, key_up, preferred_element_type=jnp.float32
    ).astype(jnp.bfloat16)
    shared = rotary[:, :, None]
    wide_values = jnp.einsum(
        "btr,rhk->bthk", rows, value_up, preferred_element_type=jnp.float32
    ).astype(jnp.bfloat16)
    return (jnp.concatenate([wide_keys, shared], axis=-1), wide_values)


def root_norm(vectors, row_gain):
    return (
        vectors * lax.rsqrt(jnp.mean(vectors * vectors, axis=-1, keepdims=True) + 1e-06) * row_gain
    )


def shards(latents, rotary_rows, latent_gain, key_up, value_up):
    rows_ready = root_norm(latents.astype(jnp.float32), latent_gain).astype(jnp.bfloat16)
    rows_moved, rotary_moved = in_one_piece((rows_ready, rotary_rows), "seq", 0, 1, 2)
    rows_cut = rows_moved.reshape(
        rows_moved.shape[0], lax.axis_size("seq"), -1, rows_moved.shape[2]
    )
    rotary_cut = rotary_moved.reshape(
        rotary_moved.shape[0], lax.axis_size("seq"), -1, rotary_moved.shape[2]
    )
    rows_joined, rotary_joined = in_one_piece_2((rows_cut, rotary_cut), "tp", 2, 3)
    rows_whole = rows_joined.reshape(rows_joined.shape[0], -1, rows_joined.shape[3])
    rotary_whole = rotary_joined.reshape(rotary_joined.shape[0], -1, rotary_joined.shape[3])
    decode_keys, decode_values = expand_rows(rows_whole, rotary_whole, key_up, value_up)
    decode_keys = jnp.transpose(decode_keys, (0, 2, 3, 1))
    return (decode_keys, decode_values)


def solution(mesh):
    return jax.shard_map(
        shards,
        mesh=mesh,
        in_specs=(
            P(None, ("seq", "tp"), None),
            P(None, ("seq", "tp"), None),
            P(),
            P(None, "tp", None),
            P(None, "tp", None),
        ),
        out_specs=(P("seq", "tp", None, None), P("seq", None, "tp", None)),
        check_vma=False,
    )
```

profile of v0, /device:TPU:1, one launch (start us, length us, event | category | flops | bytes accessed | tf_op | source)
XLA Modules:
  0.0 152.4 jit_solution(16020864475576484220)
XLA Ops:
  7.2 0.0 copy-start
  7.2 0.0 all-gather.2.cloned.1.call-start
  7.2 1.2 fusion.2
  8.5 1.2 fusion.4
  9.7 1.0 pad_maximum_fusion
  10.7 30.0 %all_to_all.12 = bf16[16,32,576]{2,1,0:T(8,128)(2,1)S(1)} all-to-all(bf16[16,32,576]{2,1,0:T(8,128)(2,1)S(1)} %pad_maximum_fusion), channel_id=1, replica_groups=mesh['seq'=16,'tp'=16] {'seq'}, dimensions={0} | all-to-all | bytes 1179648 | tf_op jit(solution)/shard_map/all_to_all | solution.py:10
  40.7 0.9 pad_maximum_fusion.1
  41.6 0.0 all-gather.2.cloned.1.call-update
  41.7 82.0 %all-gather.2.cloned.1.call-done = bf16[1,16,512,576]{3,2,1,0:T(8,128)(2,1)} async-done(((bf16[1,16,32,576]{3,2,1,0:T(8,128)(2,1)}), bf16[1,16,512,576]{3,2,1,0:T(8,128)(2,1)}) %all-gather.2.cloned.1.call-update) | async-done | bytes 9437200 | tf_op jit(solution)/shard_map/all_gather | solution.py:22
  123.7 0.0 slice-start
  123.7 1.6 %slice-done = bf16[1,16,512,64]{3,2,1,0:T(8,128)(2,1)S(1)} async-done(((bf16[1,16,512,576]{3,2,1,0:T(8,128)(2,1)}), bf16[1,16,512,64]{3,2,1,0:T(8,128)(2,1)S(1)}, s32[]{:S(2)}) %slice-start) | async-done | bytes 1048600 | tf_op jit(solution)/shard_map/slice | solution.py:24
  125.3 0.8 copy.10
  126.1 7.4 %slice.18 = bf16[1,16,512,512]{3,2,1,0:T(8,128)(2,1)} slice(bf16[1,16,512,576]{3,2,1,0:T(8,128)(2,1)} %all-gather.2.cloned.1.call-done), slice={[0:1], [0:16], [0:512], [0:512]} | slice | bytes 16777216 | tf_op jit(solution)/shard_map/slice | solution.py:24
  133.5 0.0 copy-done
  133.5 0.0 copy-start.1
  133.5 0.0 copy-start.2
  133.5 6.4 %fusion = bf16[1,8192,1,128]{1,3,2,0:T(8,128)(2,1)S(1)} fusion(bf16[8192,512]{1,0:T(8,128)(2,1)} %bitcast.19, bf16[512,1,128]{2,0,1:T(8,128)(2,1)S(1)} %copy-done), kind=kOutput, calls=%fused_computation.2 | convolution fusion | flops 1074790400 | bytes 10616832 | tf_op jit(solution)/shard_map/btr,rhk->bthk/dot_general | solution.py:30
  139.9 0.0 copy-done.1
  139.9 0.0 copy-done.2
  139.9 3.7 %fusion.1 = bf16[1,8192,1,128]{3,1,2,0:T(8,128)(2,1)} fusion(bf16[8192,512]{1,0:T(8,128)(2,1)S(1)} %bitcast.20, bf16[512,1,128]{2,0,1:T(8,128)(2,1)S(1)} %copy-done.2), kind=kOutput, calls=%fused_computation.3 | convolution fusion | flops 1074790400 | bytes 10616832 | tf_op jit(solution)/shard_map/btr,rhk->bthk/dot_general | solution.py:34
  143.6 1.9 %maximum_bitcast_fusion = bf16[1,1,192,8192]{3,2,1,0:T(8,128)(2,1)} fusion(bf16[1,8192,1,64]{1,3,2,0:T(8,128)(2,1)S(1)} %copy.10, bf16[1,8192,1,128]{1,3,2,0:T(8,128)(2,1)S(1)} %fusion), kind=kLoop, calls=%fused_computation.4 | loop fusion | flops 6291456 | bytes 6291456 | tf_op jit(solution)/shard_map/transpose | solution.py:59
  (3 shorter events, 0.1 us)
Async XLA Ops:
  7.2 126.4 %copy-start = (bf16[512,1,128]{2,0,1:T(8,128)(2,1)S(1)}, bf16[512,1,128]{2,0,1:T(8,128)(2,1)}, u32[]{:S(2)}) copy-start(bf16[512,1,128]{2,0,1:T(8,128)(2,1)} %param.8) | copy-start | bytes 393220
  7.2 116.5 %all-gather.2.cloned.1.call-start = ((), (), s32[]{:S(2)}) async-start(), calls=%async_computation.1 | async-start | bytes 11141120 | tf_op jit(solution)/shard_map/all_gather | solution.py:22
  123.7 1.6 %slice-start = ((bf16[1,16,512,576]{3,2,1,0:T(8,128)(2,1)}), bf16[1,16,512,64]{3,2,1,0:T(8,128)(2,1)S(1)}, s32[]{:S(2)}) async-start(bf16[1,16,512,576]{3,2,1,0:T(8,128)(2,1)} %all-gather.2.cloned.1.call-done), calls=%async_computation.2 | async-start | bytes 4194304 | tf_op jit(solution)/shard_map/slice | solution.py:24
  133.5 6.4 %copy-start.1 = (bf16[1,16,512,512]{3,2,1,0:T(8,128)(2,1)S(1)}, bf16[1,16,512,512]{3,2,1,0:T(8,128)(2,1)}, u32[]{:S(2)}) copy-start(bf16[1,16,512,512]{3,2,1,0:T(8,128)(2,1)} %slice.18) | copy-start | bytes 25165828
  133.5 6.4 %copy-start.2 = (bf16[512,1,128]{2,0,1:T(8,128)(2,1)S(1)}, bf16[512,1,128]{2,0,1:T(8,128)(2,1)}, u32[]{:S(2)}) copy-start(bf16[512,1,128]{2,0,1:T(8,128)(2,1)} %param.9) | copy-start | bytes 393220
Sparse Core Ops, SparseCore 0:
  41.8 81.8 all-gather.1
where the time goes:
time: 153 us; the launch traced here: 152 us
  waiting for transfers between devices  82 us (54%)
  blocking collectives  30 us (20%)
  between operations  14.1 us (9%)
  matrix products  10 us (7%)
  local copies, waits for them, and re-layouts  9.92 us (6%)
  other arithmetic  6.3 us (4%)
    all_gather x1, waiting for transfers between devices, in_one_piece_2(): filled, at, done = (lax.all_gather(both, axis, axis=dim, tiled=True), 0, [])  82 us
    all_to_all x1, blocking collectives, in_one_piece(): lax.all_to_all(both, axis, split_axis=split_dim, concat_axis=concat_dim,...  30 us
    slice x3, local copies, waits for them, and re-layouts, in_one_piece_2(): done.append(lax.slice_in_dim(filled, at, at + a.shape[along], axis=along))  9.04 us
    dot_general x1, matrix products, expand_rows(): jnp.einsum('btr,rhk->bthk', rows, key_up, preferred_element_type=jnp.floa...  6.37 us
    dot_general x1, matrix products, expand_rows(): jnp.einsum('btr,rhk->bthk', rows, value_up, preferred_element_type=jnp.fl...  3.66 us
  transfers between devices with their start and end apart: 1, of which 1 were waited for; matrix products, arithmetic and copies ran while one was open for 0% of the time, Pallas kernels for 0%

commit v1 on v0

v1 whole, which is shorter than its diff:
```python
import functools

import jax
import jax.numpy as jnp
from jax import lax
from jax.experimental import pallas as pl
from jax.experimental.pallas import tpu as pltpu
from jax.sharding import PartitionSpec as P


SIDE = 4
HOPS = (0, 1, -1, 2)
VMEM = pltpu.VMEM
MIB = 1 << 20
BF16 = jnp.bfloat16
OTHER = {"x": "y", "y": "x"}


def move(array, along, hop):
    pairs = []
    for y in range(SIDE):
        for x in range(SIDE):
            to = (y, (x + hop) % SIDE) if along == "x" else ((y + hop) % SIDE, x)
            pairs.append((y * SIDE + x, to[0] * SIDE + to[1]))
    return lax.ppermute(array, "tp", pairs)


def sender(along, hop):
    t = lax.axis_index("tp")
    mine = t % SIDE if along == "x" else t // SIDE
    return (mine - hop + SIDE) % SIDE


def whole(n, space=VMEM):
    return [pl.BlockSpec(memory_space=space)] * n


def shape(*dims):
    return jax.ShapeDtypeStruct(dims, BF16)


def call(kernel, outs, args, out_space=VMEM, in_specs=None, limit=24 * MIB, scratch=(), alias=None, flops=0, nbytes=MIB):
    return pl.pallas_call(
        kernel,
        out_shape=outs,
        in_specs=in_specs or whole(len(args)),
        out_specs=jax.tree.map(lambda _: pl.BlockSpec(memory_space=out_space), outs),
        scratch_shapes=list(scratch),
        input_output_aliases=alias or {},
        compiler_params=pltpu.CompilerParams(vmem_limit_bytes=limit),
        cost_estimate=pl.CostEstimate(flops=flops, bytes_accessed=nbytes, transcendentals=0),
    )(*args)


def run_all(copies):
    for copy in copies:
        copy.start()
    for copy in copies:
        copy.wait()


def pack_kernel(rot_in, key_in, value_in, rotary, weights, rot, sems):
    copies = [
        pltpu.make_async_copy(rot_in, rot, sems.at[0]),
        pltpu.make_async_copy(key_in, weights.at[0:512, :], sems.at[1]),
        pltpu.make_async_copy(value_in, weights.at[512:1024, :], sems.at[2]),
    ]
    for copy in copies:
        copy.start()
    copies[0].wait()
    pairs = rot.shape[0] // 2
    for b in range(pairs):
        both = [rot[b].astype(jnp.float32), rot[b + pairs].astype(jnp.float32)]
        rotary[b] = jnp.concatenate(both, axis=-1).astype(BF16)
    copies[1].wait()
    copies[2].wait()


def pack(rotary, key_up, value_up):
    b = rotary.shape[0]
    return call(
        pack_kernel,
        (shape(b // 2, 32, 128), shape(1024, 128)),
        (rotary, key_up.reshape(512, 128), value_up.reshape(512, 128)),
        in_specs=whole(3, pltpu.HBM),
        limit=67043328,
        scratch=[VMEM(rotary.shape, BF16), pltpu.SemaphoreType.DMA((3,))],
    )


def rotary_row_kernel(*refs):
    got, out, block = refs[:4], refs[4], refs[5]
    pairs = got[0].shape[0]
    for i, hop in enumerate(HOPS):
        at = pl.multiple_of(sender("x", hop) * 32, 32)
        for b in range(pairs):
            block[b, pl.ds(at, 32), :] = got[i][b]
    for b in range(pairs):
        turned = block[b].T
        out[b] = turned[0:64]
        out[b + pairs] = turned[64:128]


def rotary_row(got):
    pairs = got[0].shape[0]
    return call(
        rotary_row_kernel,
        shape(2 * pairs, 64, 128),
        got,
        limit=4 * MIB,
        scratch=[VMEM((pairs, 128, 128), BF16)],
    )


def rotary_plane_kernel(*refs):
    got, out = refs[:4], refs[4]
    for i, hop in enumerate(HOPS):
        out[:, pl.ds(sender("y", hop), 1), :, :] = got[i][...][:, None]


def rotary_plane(got):
    return call(rotary_plane_kernel, shape(got[0].shape[0], SIDE, 64, 128), got, limit=4 * MIB)


def norm_kernel(rows, gain, low, high):
    gains = gain[...]
    half = low.shape[0]
    for b in range(rows.shape[0]):
        v = rows[b].astype(jnp.float32)
        v = v * lax.rsqrt(jnp.mean(v * v, axis=-1, keepdims=True) + 1e-06) * gains
        (low if b < half else high)[b % half] = v.astype(BF16)


def norm(rows, gain):
    n = rows.shape[0]
    outs = (shape(n // 2, 32, 512),) * 2
    return call(norm_kernel, outs, (rows, gain.reshape(1, -1)), limit=4 * MIB)


def expand_kernel(along, *refs):
    rows, head, out, block = refs[:4], refs[4], refs[5], refs[6]
    s = block.shape[0]
    for i, hop in enumerate(HOPS):
        at = pl.multiple_of(sender(along, hop) * 32, 32)
        for b in range(s):
            block[b, pl.ds(at, 32), :] = rows[i][b]
    w = jnp.concatenate([head[0:512, :], head[512:1024, :]], axis=-1)
    for b in range(0, s, 2):
        wide = jnp.dot(
            block[b : b + 2].reshape(256, 512), w, preferred_element_type=jnp.float32
        ).astype(BF16)
        for k in range(2):
            part = wide[128 * k : 128 * k + 128]
            out[b + k, 0] = part[:, 0:128].T
            out[b + k, 1] = part[:, 128:256]


def expand(rows, head, along):
    s = rows[0].shape[0]
    return call(
        functools.partial(expand_kernel, along),
        shape(s, 2, 128, 128),
        (*rows, head),
        limit=8 * MIB,
        scratch=[VMEM((s, 128, 512), BF16)],
        flops=s * 128 * 512 * 256 * 2,
    )


def join_x_kernel(first, *refs):
    got, keys, values, sems = refs[:4], refs[-3], refs[-2], refs[-1]
    s = got[0].shape[0]
    copies = []
    for i, hop in enumerate(HOPS):
        y = sender("y", hop)
        sem = lambda: sems.at[len(copies)]
        copies.append(pltpu.make_async_copy(got[i].at[:, 1], values.at[first : first + s, y], sem()))
        for b in range(s):
            lanes = pl.ds(pl.multiple_of((first + b) * 512 + y * 128, 128), 128)
            copies.append(pltpu.make_async_copy(got[i].at[b, 0], keys.at[0:128, lanes], sem()))
    run_all(copies)


def join_y_kernel(first, *refs):
    got, keys, values, sorted_, lined, sems = refs[:4], *refs[-5:]
    s = got[0].shape[0]
    copies = []
    sem = lambda: sems.at[len(copies)]
    for i, hop in enumerate(HOPS):
        x = sender("x", hop)
        rows = pl.ds(pl.multiple_of(x * 32, 32), 32)
        for y in range(SIDE):
            copies.append(
                pltpu.make_async_copy(
                    got[i].at[:, 1, 32 * y : 32 * y + 32],
                    values.at[first : first + s, y, rows],
                    sem(),
                )
            )
    for copy in copies:
        copy.start()
    for i, hop in enumerate(HOPS):
        x = sender("x", hop)
        for b in range(s):
            sorted_[x, b] = got[i][b, 0]
    for b in range(s):
        for y in range(SIDE):
            parts = [sorted_[x, b][:, 32 * y : 32 * y + 32] for x in range(SIDE)]
            lined[b, :, 128 * y : 128 * y + 128] = jnp.concatenate(parts, axis=-1)
        at = (first + b) * 512
        copies.append(pltpu.make_async_copy(lined.at[b], keys.at[0:128, at : at + 512], sem()))
        copies[-1].start()
    for copy in copies:
        copy.wait()


def join_rotary_kernel(got, keys_in, keys, sems):
    del keys_in
    copies = []
    for b in range(got.shape[0]):
        for y in range(SIDE):
            at = b * 512 + y * 128
            copies.append(
                pltpu.make_async_copy(
                    got.at[b, y], keys.at[128:192, at : at + 128], sems.at[len(copies)]
                )
            )
    run_all(copies)


def joins(x_got, y_got, rotary):
    n = rotary.shape[0]
    s = n // 2
    outs = (shape(192, n * 512), shape(n, SIDE, 128, 128))
    sems = lambda k: pltpu.SemaphoreType.DMA((k,))
    keys, values = call(
        functools.partial(join_x_kernel, 0),
        outs,
        x_got,
        out_space=pltpu.HBM,
        limit=8 * MIB,
        scratch=[sems(SIDE * (s + 1))],
        nbytes=4 * MIB,
    )
    keys, values = call(
        functools.partial(join_y_kernel, s),
        outs,
        (*y_got, keys, values),
        out_space=pltpu.HBM,
        in_specs=whole(4) + whole(2, pltpu.HBM),
        limit=8 * MIB,
        scratch=[
            VMEM((SIDE, s, 128, 128), BF16),
            VMEM((s, 128, 512), BF16),
            sems(SIDE * SIDE + s),
        ],
        alias={4: 0, 5: 1},
        nbytes=4 * MIB,
    )
    keys = call(
        join_rotary_kernel,
        outs[0],
        (rotary, keys),
        out_space=pltpu.HBM,
        in_specs=whole(1) + whole(1, pltpu.HBM),
        limit=4 * MIB,
        scratch=[sems(n * SIDE)],
        alias={1: 0},
        nbytes=2 * MIB,
    )
    return keys, values


def named_move(array, along, i, back=False):
    return move(array, along, -HOPS[i] if back else HOPS[i])


def shards(latents, rotary_rows, latent_gain, key_up, value_up):
    mine = lax.all_to_all(latents, "seq", split_axis=0, concat_axis=0, tiled=True)
    rotary, head = pack(rotary_rows, key_up, value_up)
    row = rotary_row([rotary] + [named_move(rotary, "x", i) for i in (1, 2, 3)])
    plane = [row] + [named_move(row, "y", i) for i in (1, 2, 3)]
    heads = {a: [head] + [named_move(head, a, i, back=True) for i in (1, 2, 3)] for a in "xy"}
    mine, _ = lax.optimization_barrier((mine, row))
    halves = dict(zip("xy", norm(mine, latent_gain)))
    near = {a: [halves[a]] for a in "xy"}
    for i in (1, 2, 3):
        for a in "xy":
            near[a].append(named_move(halves[a], a, i))
    plane = rotary_plane(plane)
    far = lax.all_to_all(plane, "seq", split_axis=0, concat_axis=0, tiled=True)
    got = {"x": [None] * 4, "y": [None] * 4}
    for i in (3, 1, 2, 0):
        for a in "xy":
            piece = expand(near[a], heads[OTHER[a]][i], a)
            got[a][i] = named_move(piece, OTHER[a], i) if i else piece
    keys, values = joins(got["x"], got["y"], far)
    return keys[None, None], values.reshape(1, -1, 1, 128)


def solution(mesh):
    return jax.shard_map(
        shards,
        mesh=mesh,
        in_specs=(
            P(None, ("seq", "tp"), None),
            P(None, ("seq", "tp"), None),
            P(),
            P(None, "tp", None),
            P(None, "tp", None),
        ),
        out_specs=(P("seq", "tp", None, None), P("seq", None, "tp", None)),
        check_vma=False,
    )
```

time: 153 us -> 117 us (0.76)
  the two profiles are of different devices: /device:TPU:1 before, /device:TPU:2 now
where the time goes in v1:
time: 117 us
  starting transfers between devices  60.7 us (52%)
  waiting for transfers between devices  40.3 us (34%)
  Pallas kernels  13.7 us (12%)
    ppermute x24, starting transfers between devices, move(): return lax.ppermute(array, 'tp', pairs)  45 us
    ppermute x24, waiting for transfers between devices, move(): return lax.ppermute(array, 'tp', pairs)  40.3 us
    pallas_call x15, Pallas kernels, call(): pl.pallas_call(kernel, out_shape=outs, in_specs=in_specs or whole(len(arg...  13.7 us
    all_to_all x1, starting transfers between devices, shards(): lax.all_to_all(latents, 'seq', split_axis=0, concat_axis=0, tiled=True)  8.63 us
    all_to_all x1, starting transfers between devices, shards(): far = lax.all_to_all(plane, 'seq', split_axis=0, concat_axis=0, tiled=True)  7.14 us
  transfers between devices with their start and end apart: 26, of which 14 were waited for; matrix products, arithmetic and copies ran while one was open for 0% of the time, Pallas kernels for 10%

profile of v1, /device:TPU:2, one launch (start us, length us, event | category | flops | bytes accessed | tf_op | source)
XLA Modules:
  0.0 116.6 jit_solution(15924740555618015972)
XLA Ops:
  0.6 8.6 %all-to-all-start.1 = ((bf16[16,32,512]{2,1,0:T(8,128)(2,1)}), bf16[16,32,512]{2,1,0:T(8,128)(2,1)}, u32[]{:S(2)}, u32[]{:S(2)}) async-start(bf16[16,32,512]{2,1,0:T(8,128)(2,1)} %param.5), calls=%async_computation.1 | async-start | bytes 1048576 | tf_op jit(solution)/shard_map/all_to_all | solution.py:279
  9.3 1.8 %shard_map.68 = (bf16[8,32,128]{2,1,0:T(8,128)(2,1)}, bf16[1024,128]{1,0:T(8,128)(2,1)}) custom-call(bf16[16,32,64]{2,1,0:T(8,128)(2,1)} %rot_in.1, bf16[512,128]{1,0:T(8,128)(2,1)} %bitcast.8, bf16[512,128]{1,0:T(8,128)(2,1)} %bitcast.9), custom_call_target="tpu_custom_call" | custom-call | bytes 1048576 | tf_op jit(solution)/shard_map/pallas_call | solution.py:43
  13.2 2.1 %collective-permute-start.2 = (bf16[8,32,128]{2,1,0:T(8,128)(2,1)}, bf16[8,32,128]{2,1,0:T(8,128)(2,1)S(1)}, u32[]{:S(2)}, u32[]{:S(2)}) collective-permute-start(bf16[8,32,128]{2,1,0:T(8,128)(2,1)} %get-tuple-element.11.refs_0_), channel_id=1, source_target_pairs={{0,2},{1,3},{2,0},{3,1},{4,6},{5,7},{6,4},{7,5},{8,10},{9,11},{10,... | collective-permute-start | bytes 196616 | tf_op jit(solution)/shard_map/ppermute | solution.py:25
  17.1 2.0 %collective-permute-done.2.refs_3_ = bf16[8,32,128]{2,1,0:T(8,128)(2,1)S(1)} collective-permute-done((bf16[8,32,128]{2,1,0:T(8,128)(2,1)}, bf16[8,32,128]{2,1,0:T(8,128)(2,1)S(1)}, u32[]{:S(2)}, u32[]{:S(2)}) %collective-permute-start.2) | collective-permute-done | bytes 65568 | tf_op jit(solution)/shard_map/ppermute | solution.py:25
  21.8 1.7 %collective-permute-start.4 = (bf16[16,64,128]{2,1,0:T(8,128)(2,1)S(1)}, bf16[16,64,128]{2,1,0:T(8,128)(2,1)S(1)}, u32[]{:S(2)}, u32[]{:S(2)}) collective-permute-start(bf16[16,64,128]{2,1,0:T(8,128)(2,1)S(1)} %shard_map.69.refs_0_), channel_id=1, source_target_pairs={{0,12},{1,13},{2,14},{3,15},{4,0},{5,1},{6,2},{7,3},{8,4},{9,5},{1... | collective-permute-start | bytes 786440 | tf_op jit(solution)/shard_map/ppermute | solution.py:25
  23.5 2.0 %collective-permute-start.5 = (bf16[16,64,128]{2,1,0:T(8,128)(2,1)S(1)}, bf16[16,64,128]{2,1,0:T(8,128)(2,1)S(1)}, u32[]{:S(2)}, u32[]{:S(2)}) collective-permute-start(bf16[16,64,128]{2,1,0:T(8,128)(2,1)S(1)} %shard_map.69.refs_0_), channel_id=1, source_target_pairs={{0,8},{1,9},{2,10},{3,11},{4,12},{5,13},{6,14},{7,15},{8,0},{9,1},... | collective-permute-start | bytes 786440 | tf_op jit(solution)/shard_map/ppermute | solution.py:25
  25.5 4.0 %collective-permute-done.3.refs_1_ = bf16[16,64,128]{2,1,0:T(8,128)(2,1)S(1)} collective-permute-done((bf16[16,64,128]{2,1,0:T(8,128)(2,1)S(1)}, bf16[16,64,128]{2,1,0:T(8,128)(2,1)S(1)}, u32[]{:S(2)}, u32[]{:S(2)}) %collective-permute-start.3) | collective-permute-done | bytes 262176 | tf_op jit(solution)/shard_map/ppermute | solution.py:25
  29.5 4.7 %collective-permute-done.4.refs_2_ = bf16[16,64,128]{2,1,0:T(8,128)(2,1)S(1)} collective-permute-done((bf16[16,64,128]{2,1,0:T(8,128)(2,1)S(1)}, bf16[16,64,128]{2,1,0:T(8,128)(2,1)S(1)}, u32[]{:S(2)}, u32[]{:S(2)}) %collective-permute-start.4) | collective-permute-done | bytes 262176 | tf_op jit(solution)/shard_map/ppermute | solution.py:25
  34.2 1.8 %collective-permute-done.5.refs_3_ = bf16[16,64,128]{2,1,0:T(8,128)(2,1)S(1)} collective-permute-done((bf16[16,64,128]{2,1,0:T(8,128)(2,1)S(1)}, bf16[16,64,128]{2,1,0:T(8,128)(2,1)S(1)}, u32[]{:S(2)}, u32[]{:S(2)}) %collective-permute-start.5) | collective-permute-done | bytes 262176 | tf_op jit(solution)/shard_map/ppermute | solution.py:25
  37.1 7.1 %all-to-all-start = ((bf16[16,4,64,128]{3,2,1,0:T(8,128)(2,1)}), bf16[16,4,64,128]{3,2,1,0:T(8,128)(2,1)S(1)}, u32[]{:S(2)}, u32[]{:S(2)}) async-start(bf16[16,4,64,128]{3,2,1,0:T(8,128)(2,1)} %shard_map.70), calls=%async_computation | async-start | bytes 2097152 | tf_op jit(solution)/shard_map/all_to_all | solution.py:291
  44.3 1.9 %collective-permute-start.18 = (bf16[1024,128]{1,0:T(8,128)(2,1)S(1)}, bf16[1024,128]{1,0:T(8,128)(2,1)S(1)}, u32[]{:S(2)}, u32[]{:S(2)}) collective-permute-start(bf16[1024,128]{1,0:T(8,128)(2,1)S(1)} %copy-done), channel_id=1, source_target_pairs={{0,12},{1,13},{2,14},{3,15},{4,0},{5,1},{6,2},{7,3},{8,4},{9,5},{1... | collective-permute-start | bytes 786440 | tf_op jit(solution)/shard_map/ppermute | solution.py:25
  51.2 1.8 %collective-permute-done.18.refs_4_ = bf16[1024,128]{1,0:T(8,128)(2,1)S(1)} collective-permute-done((bf16[1024,128]{1,0:T(8,128)(2,1)S(1)}, bf16[1024,128]{1,0:T(8,128)(2,1)S(1)}, u32[]{:S(2)}, u32[]{:S(2)}) %collective-permute-start.18) | collective-permute-done | bytes 262176 | tf_op jit(solution)/shard_map/ppermute | solution.py:25
  54.6 2.2 %collective-permute-done.15.refs_1_ = bf16[8,32,512]{2,1,0:T(8,128)(2,1)S(1)} collective-permute-done((bf16[8,32,512]{2,1,0:T(8,128)(2,1)S(1)}, bf16[8,32,512]{2,1,0:T(8,128)(2,1)S(1)}, u32[]{:S(2)}, u32[]{:S(2)}) %collective-permute-start.15) | collective-permute-done | bytes 262176 | tf_op jit(solution)/shard_map/ppermute | solution.py:25
  58.3 5.4 %collective-permute-done.17.refs_3_ = bf16[8,32,512]{2,1,0:T(8,128)(2,1)S(1)} collective-permute-done((bf16[8,32,512]{2,1,0:T(8,128)(2,1)S(1)}, bf16[8,32,512]{2,1,0:T(8,128)(2,1)S(1)}, u32[]{:S(2)}, u32[]{:S(2)}) %collective-permute-start.17) | collective-permute-done | bytes 262176 | tf_op jit(solution)/shard_map/ppermute | solution.py:25
  64.6 2.1 %collective-permute-done.20.refs_4_ = bf16[1024,128]{1,0:T(8,128)(2,1)S(1)} collective-permute-done((bf16[1024,128]{1,0:T(8,128)(2,1)S(1)}, bf16[1024,128]{1,0:T(8,128)(2,1)S(1)}, u32[]{:S(2)}, u32[]{:S(2)}) %collective-permute-start.20) | collective-permute-done | bytes 262176 | tf_op jit(solution)/shard_map/ppermute | solution.py:25
  68.3 5.5 %collective-permute-start.11 = (bf16[1024,128]{1,0:T(8,128)(2,1)S(1)}, bf16[1024,128]{1,0:T(8,128)(2,1)S(1)}, u32[]{:S(2)}, u32[]{:S(2)}) collective-permute-start(bf16[1024,128]{1,0:T(8,128)(2,1)S(1)} %copy-done), channel_id=1, source_target_pairs={{0,1},{1,2},{2,3},{3,0},{4,5},{5,6},{6,7},{7,4},{8,9},{9,10},{10,1... | collective-permute-start | bytes 786440 | tf_op jit(solution)/shard_map/ppermute | solution.py:25
  73.8 6.6 %collective-permute-start.9 = (bf16[1024,128]{1,0:T(8,128)(2,1)S(1)}, bf16[1024,128]{1,0:T(8,128)(2,1)S(1)}, u32[]{:S(2)}, u32[]{:S(2)}) collective-permute-start(bf16[1024,128]{1,0:T(8,128)(2,1)S(1)} %copy-done), channel_id=1, source_target_pairs={{0,3},{1,0},{2,1},{3,2},{4,7},{5,4},{6,5},{7,6},{8,11},{9,8},{10,9... | collective-permute-start | bytes 786440 | tf_op jit(solution)/shard_map/ppermute | solution.py:25
  81.6 4.8 %collective-permute-done.8.refs_3_ = bf16[8,32,512]{2,1,0:T(8,128)(2,1)S(1)} collective-permute-done((bf16[8,32,512]{2,1,0:T(8,128)(2,1)S(1)}, bf16[8,32,512]{2,1,0:T(8,128)(2,1)S(1)}, u32[]{:S(2)}, u32[]{:S(2)}) %collective-permute-start.8) | collective-permute-done | bytes 262176 | tf_op jit(solution)/shard_map/ppermute | solution.py:25
  86.5 1.9 %collective-permute-start.23 = (bf16[8,2,128,128]{3,2,1,0:T(8,128)(2,1)S(1)}, bf16[8,2,128,128]{3,2,1,0:T(8,128)(2,1)S(1)}, u32[]{:S(2)}, u32[]{:S(2)}) collective-permute-start(bf16[8,2,128,128]{3,2,1,0:T(8,128)(2,1)S(1)} %shard_map.79), channel_id=1, source_target_pairs={{0,8},{1,9},{2,10},{3,11},{4,12},{5,13},{6,14},{7,15},{8,0},{9,1},... | collective-permute-start | bytes 1572872 | tf_op jit(solution)/shard_map/ppermute | solution.py:25
  89.0 6.6 %collective-permute-start.14 = (bf16[8,2,128,128]{3,2,1,0:T(8,128)(2,1)S(1)}, bf16[8,2,128,128]{3,2,1,0:T(8,128)(2,1)S(1)}, u32[]{:S(2)}, u32[]{:S(2)}) collective-permute-start(bf16[8,2,128,128]{3,2,1,0:T(8,128)(2,1)S(1)} %shard_map.75), channel_id=1, source_target_pairs={{0,2},{1,3},{2,0},{3,1},{4,6},{5,7},{6,4},{7,5},{8,10},{9,11},{10,... | collective-permute-start | bytes 1572872 | tf_op jit(solution)/shard_map/ppermute | solution.py:25
  96.8 4.5 %collective-permute-start.10 = (bf16[8,2,128,128]{3,2,1,0:T(8,128)(2,1)S(1)}, bf16[8,2,128,128]{3,2,1,0:T(8,128)(2,1)S(1)}, u32[]{:S(2)}, u32[]{:S(2)}) collective-permute-start(bf16[8,2,128,128]{3,2,1,0:T(8,128)(2,1)S(1)} %shard_map.73), channel_id=1, source_target_pairs={{0,1},{1,2},{2,3},{3,0},{4,5},{5,6},{6,7},{7,4},{8,9},{9,10},{10,1... | collective-permute-start | bytes 1572872 | tf_op jit(solution)/shard_map/ppermute | solution.py:25
  104.1 4.3 %collective-permute-done.14.refs_3_ = bf16[8,2,128,128]{3,2,1,0:T(8,128)(2,1)S(1)} collective-permute-done((bf16[8,2,128,128]{3,2,1,0:T(8,128)(2,1)S(1)}, bf16[8,2,128,128]{3,2,1,0:T(8,128)(2,1)S(1)}, u32[]{:S(2)}, u32[]{:S(2)}) %collective-permute-start.14) | collective-permute-done | bytes 524320 | tf_op jit(solution)/shard_map/ppermute | solution.py:25
  108.3 4.8 %collective-permute-done.12.refs_2_ = bf16[8,2,128,128]{3,2,1,0:T(8,128)(2,1)S(1)} collective-permute-done((bf16[8,2,128,128]{3,2,1,0:T(8,128)(2,1)S(1)}, bf16[8,2,128,128]{3,2,1,0:T(8,128)(2,1)S(1)}, u32[]{:S(2)}, u32[]{:S(2)}) %collective-permute-start.12) | collective-permute-done | bytes 524320 | tf_op jit(solution)/shard_map/ppermute | solution.py:25
  113.1 1.8 %shard_map.81 = (bf16[192,8192]{1,0:T(8,128)(2,1)}, bf16[16,4,128,128]{3,2,1,0:T(8,128)(2,1)}) custom-call(bf16[8,2,128,128]{3,2,1,0:T(8,128)(2,1)S(1)} %shard_map.72.refs_0_, bf16[8,2,128,128]{3,2,1,0:T(8,128)(2,1)S(1)} %collective-permute-done.10.refs_1_, ...), custom_call_target="tpu_custom_call", output_to_operand_aliasing={{0}: (4, {}), {1}: (5, {})} | custom-call | bytes 4194304 | tf_op jit(solution)/shard_map/pallas_call | solution.py:43
  (49 shorter events, 25.4 us)
Async XLA Ops:
  0.6 36.5 %all-to-all-start.1 = ((bf16[16,32,512]{2,1,0:T(8,128)(2,1)}), bf16[16,32,512]{2,1,0:T(8,128)(2,1)}, u32[]{:S(2)}, u32[]{:S(2)}) async-start(bf16[16,32,512]{2,1,0:T(8,128)(2,1)} %param.5), calls=%async_computation.1 | async-start | bytes 1048576 | tf_op jit(solution)/shard_map/all_to_all | solution.py:279
  13.2 6.0 %collective-permute-start.2 = (bf16[8,32,128]{2,1,0:T(8,128)(2,1)}, bf16[8,32,128]{2,1,0:T(8,128)(2,1)S(1)}, u32[]{:S(2)}, u32[]{:S(2)}) collective-permute-start(bf16[8,32,128]{2,1,0:T(8,128)(2,1)} %get-tuple-element.11.refs_0_), channel_id=1, source_target_pairs={{0,2},{1,3},{2,0},{3,1},{4,6},{5,7},{6,4},{7,5},{8,10},{9,11},{10,... | collective-permute-start | bytes 196616 | tf_op jit(solution)/shard_map/ppermute | solution.py:25
  20.2 9.3 %collective-permute-start.3 = (bf16[16,64,128]{2,1,0:T(8,128)(2,1)S(1)}, bf16[16,64,128]{2,1,0:T(8,128)(2,1)S(1)}, u32[]{:S(2)}, u32[]{:S(2)}) collective-permute-start(bf16[16,64,128]{2,1,0:T(8,128)(2,1)S(1)} %shard_map.69.refs_0_), channel_id=1, source_target_pairs={{0,4},{1,5},{2,6},{3,7},{4,8},{5,9},{6,10},{7,11},{8,12},{9,13},{1... | collective-permute-start | bytes 786440 | tf_op jit(solution)/shard_map/ppermute | solution.py:25
  21.8 12.4 %collective-permute-start.4 = (bf16[16,64,128]{2,1,0:T(8,128)(2,1)S(1)}, bf16[16,64,128]{2,1,0:T(8,128)(2,1)S(1)}, u32[]{:S(2)}, u32[]{:S(2)}) collective-permute-start(bf16[16,64,128]{2,1,0:T(8,128)(2,1)S(1)} %shard_map.69.refs_0_), channel_id=1, source_target_pairs={{0,12},{1,13},{2,14},{3,15},{4,0},{5,1},{6,2},{7,3},{8,4},{9,5},{1... | collective-permute-start | bytes 786440 | tf_op jit(solution)/shard_map/ppermute | solution.py:25
  23.5 12.6 %collective-permute-start.5 = (bf16[16,64,128]{2,1,0:T(8,128)(2,1)S(1)}, bf16[16,64,128]{2,1,0:T(8,128)(2,1)S(1)}, u32[]{:S(2)}, u32[]{:S(2)}) collective-permute-start(bf16[16,64,128]{2,1,0:T(8,128)(2,1)S(1)} %shard_map.69.refs_0_), channel_id=1, source_target_pairs={{0,8},{1,9},{2,10},{3,11},{4,12},{5,13},{6,14},{7,15},{8,0},{9,1},... | collective-permute-start | bytes 786440 | tf_op jit(solution)/shard_map/ppermute | solution.py:25
  37.1 77.9 %all-to-all-start = ((bf16[16,4,64,128]{3,2,1,0:T(8,128)(2,1)}), bf16[16,4,64,128]{3,2,1,0:T(8,128)(2,1)S(1)}, u32[]{:S(2)}, u32[]{:S(2)}) async-start(bf16[16,4,64,128]{3,2,1,0:T(8,128)(2,1)} %shard_map.70), calls=%async_computation | async-start | bytes 2097152 | tf_op jit(solution)/shard_map/all_to_all | solution.py:291
  44.3 8.7 %collective-permute-start.18 = (bf16[1024,128]{1,0:T(8,128)(2,1)S(1)}, bf16[1024,128]{1,0:T(8,128)(2,1)S(1)}, u32[]{:S(2)}, u32[]{:S(2)}) collective-permute-start(bf16[1024,128]{1,0:T(8,128)(2,1)S(1)} %copy-done), channel_id=1, source_target_pairs={{0,12},{1,13},{2,14},{3,15},{4,0},{5,1},{6,2},{7,3},{8,4},{9,5},{1... | collective-permute-start | bytes 786440 | tf_op jit(solution)/shard_map/ppermute | solution.py:25
  47.5 9.3 %collective-permute-start.15 = (bf16[8,32,512]{2,1,0:T(8,128)(2,1)S(1)}, bf16[8,32,512]{2,1,0:T(8,128)(2,1)S(1)}, u32[]{:S(2)}, u32[]{:S(2)}) collective-permute-start(bf16[8,32,512]{2,1,0:T(8,128)(2,1)S(1)} %get-tuple-element.15.refs_0_), channel_id=1, source_target_pairs={{0,1},{1,2},{2,3},{3,0},{4,5},{5,6},{6,7},{7,4},{8,9},{9,10},{10,1... | collective-permute-start | bytes 786440 | tf_op jit(solution)/shard_map/ppermute | solution.py:25
  48.3 9.8 %collective-permute-start.16 = (bf16[8,32,512]{2,1,0:T(8,128)(2,1)S(1)}, bf16[8,32,512]{2,1,0:T(8,128)(2,1)S(1)}, u32[]{:S(2)}, u32[]{:S(2)}) collective-permute-start(bf16[8,32,512]{2,1,0:T(8,128)(2,1)S(1)} %get-tuple-element.15.refs_0_), channel_id=1, source_target_pairs={{0,3},{1,0},{2,1},{3,2},{4,7},{5,4},{6,5},{7,6},{8,11},{9,8},{10,9... | collective-permute-start | bytes 786440 | tf_op jit(solution)/shard_map/ppermute | solution.py:25
  49.6 14.2 %collective-permute-start.17 = (bf16[8,32,512]{2,1,0:T(8,128)(2,1)S(1)}, bf16[8,32,512]{2,1,0:T(8,128)(2,1)S(1)}, u32[]{:S(2)}, u32[]{:S(2)}) collective-permute-start(bf16[8,32,512]{2,1,0:T(8,128)(2,1)S(1)} %get-tuple-element.15.refs_0_), channel_id=1, source_target_pairs={{0,2},{1,3},{2,0},{3,1},{4,6},{5,7},{6,4},{7,5},{8,10},{9,11},{10,... | collective-permute-start | bytes 786440 | tf_op jit(solution)/shard_map/ppermute | solution.py:25
  51.0 15.7 %collective-permute-start.20 = (bf16[1024,128]{1,0:T(8,128)(2,1)S(1)}, bf16[1024,128]{1,0:T(8,128)(2,1)S(1)}, u32[]{:S(2)}, u32[]{:S(2)}) collective-permute-start(bf16[1024,128]{1,0:T(8,128)(2,1)S(1)} %copy-done), channel_id=1, source_target_pairs={{0,4},{1,5},{2,6},{3,7},{4,8},{5,9},{6,10},{7,11},{8,12},{9,13},{1... | collective-permute-start | bytes 786440 | tf_op jit(solution)/shard_map/ppermute | solution.py:25
  53.0 14.7 %collective-permute-start.22 = (bf16[1024,128]{1,0:T(8,128)(2,1)S(1)}, bf16[1024,128]{1,0:T(8,128)(2,1)S(1)}, u32[]{:S(2)}, u32[]{:S(2)}) collective-permute-start(bf16[1024,128]{1,0:T(8,128)(2,1)S(1)} %copy-done), channel_id=1, source_target_pairs={{0,8},{1,9},{2,10},{3,11},{4,12},{5,13},{6,14},{7,15},{8,0},{9,1},... | collective-permute-start | bytes 786440 | tf_op jit(solution)/shard_map/ppermute | solution.py:25
  56.7 11.6 %collective-permute-start.13 = (bf16[1024,128]{1,0:T(8,128)(2,1)S(1)}, bf16[1024,128]{1,0:T(8,128)(2,1)S(1)}, u32[]{:S(2)}, u32[]{:S(2)}) collective-permute-start(bf16[1024,128]{1,0:T(8,128)(2,1)S(1)} %copy-done), channel_id=1, source_target_pairs={{0,2},{1,3},{2,0},{3,1},{4,6},{5,7},{6,4},{7,5},{8,10},{9,11},{10,... | collective-permute-start | bytes 786440 | tf_op jit(solution)/shard_map/ppermute | solution.py:25
  58.2 15.6 %collective-permute-start.6 = (bf16[8,32,512]{2,1,0:T(8,128)(2,1)S(1)}, bf16[8,32,512]{2,1,0:T(8,128)(2,1)S(1)}, u32[]{:S(2)}, u32[]{:S(2)}) collective-permute-start(bf16[8,32,512]{2,1,0:T(8,128)(2,1)S(1)} %get-tuple-element.13.refs_0_), channel_id=1, source_target_pairs={{0,4},{1,5},{2,6},{3,7},{4,8},{5,9},{6,10},{7,11},{8,12},{9,13},{1... | collective-permute-start | bytes 786440 | tf_op jit(solution)/shard_map/ppermute | solution.py:25
  64.3 32.5 %collective-permute-start.19 = (bf16[8,2,128,128]{3,2,1,0:T(8,128)(2,1)S(1)}, bf16[8,2,128,128]{3,2,1,0:T(8,128)(2,1)S(1)}, u32[]{:S(2)}, u32[]{:S(2)}) collective-permute-start(bf16[8,2,128,128]{3,2,1,0:T(8,128)(2,1)S(1)} %shard_map.77), channel_id=1, source_target_pairs={{0,4},{1,5},{2,6},{3,7},{4,8},{5,9},{6,10},{7,11},{8,12},{9,13},{1... | collective-permute-start | bytes 1572872 | tf_op jit(solution)/shard_map/ppermute | solution.py:25
  66.7 14.8 %collective-permute-start.7 = (bf16[8,32,512]{2,1,0:T(8,128)(2,1)S(1)}, bf16[8,32,512]{2,1,0:T(8,128)(2,1)S(1)}, u32[]{:S(2)}, u32[]{:S(2)}) collective-permute-start(bf16[8,32,512]{2,1,0:T(8,128)(2,1)S(1)} %get-tuple-element.13.refs_0_), channel_id=1, source_target_pairs={{0,12},{1,13},{2,14},{3,15},{4,0},{5,1},{6,2},{7,3},{8,4},{9,5},{1... | collective-permute-start | bytes 786440 | tf_op jit(solution)/shard_map/ppermute | solution.py:25
  67.7 18.8 %collective-permute-start.8 = (bf16[8,32,512]{2,1,0:T(8,128)(2,1)S(1)}, bf16[8,32,512]{2,1,0:T(8,128)(2,1)S(1)}, u32[]{:S(2)}, u32[]{:S(2)}) collective-permute-start(bf16[8,32,512]{2,1,0:T(8,128)(2,1)S(1)} %get-tuple-element.13.refs_0_), channel_id=1, source_target_pairs={{0,8},{1,9},{2,10},{3,11},{4,12},{5,13},{6,14},{7,15},{8,0},{9,1},... | collective-permute-start | bytes 786440 | tf_op jit(solution)/shard_map/ppermute | solution.py:25
  68.3 20.7 %collective-permute-start.11 = (bf16[1024,128]{1,0:T(8,128)(2,1)S(1)}, bf16[1024,128]{1,0:T(8,128)(2,1)S(1)}, u32[]{:S(2)}, u32[]{:S(2)}) collective-permute-start(bf16[1024,128]{1,0:T(8,128)(2,1)S(1)} %copy-done), channel_id=1, source_target_pairs={{0,1},{1,2},{2,3},{3,0},{4,5},{5,6},{6,7},{7,4},{8,9},{9,10},{10,1... | collective-permute-start | bytes 786440 | tf_op jit(solution)/shard_map/ppermute | solution.py:25
  73.8 22.4 %collective-permute-start.9 = (bf16[1024,128]{1,0:T(8,128)(2,1)S(1)}, bf16[1024,128]{1,0:T(8,128)(2,1)S(1)}, u32[]{:S(2)}, u32[]{:S(2)}) collective-permute-start(bf16[1024,128]{1,0:T(8,128)(2,1)S(1)} %copy-done), channel_id=1, source_target_pairs={{0,3},{1,0},{2,1},{3,2},{4,7},{5,4},{6,5},{7,6},{8,11},{9,8},{10,9... | collective-permute-start | bytes 786440 | tf_op jit(solution)/shard_map/ppermute | solution.py:25
  81.5 20.9 %collective-permute-start.21 = (bf16[8,2,128,128]{3,2,1,0:T(8,128)(2,1)S(1)}, bf16[8,2,128,128]{3,2,1,0:T(8,128)(2,1)S(1)}, u32[]{:S(2)}, u32[]{:S(2)}) collective-permute-start(bf16[8,2,128,128]{3,2,1,0:T(8,128)(2,1)S(1)} %shard_map.78), channel_id=1, source_target_pairs={{0,12},{1,13},{2,14},{3,15},{4,0},{5,1},{6,2},{7,3},{8,4},{9,5},{1... | collective-permute-start | bytes 1572872 | tf_op jit(solution)/shard_map/ppermute | solution.py:25
  86.5 15.9 %collective-permute-start.23 = (bf16[8,2,128,128]{3,2,1,0:T(8,128)(2,1)S(1)}, bf16[8,2,128,128]{3,2,1,0:T(8,128)(2,1)S(1)}, u32[]{:S(2)}, u32[]{:S(2)}) collective-permute-start(bf16[8,2,128,128]{3,2,1,0:T(8,128)(2,1)S(1)} %shard_map.79), channel_id=1, source_target_pairs={{0,8},{1,9},{2,10},{3,11},{4,12},{5,13},{6,14},{7,15},{8,0},{9,1},... | collective-permute-start | bytes 1572872 | tf_op jit(solution)/shard_map/ppermute | solution.py:25
  89.0 19.3 %collective-permute-start.14 = (bf16[8,2,128,128]{3,2,1,0:T(8,128)(2,1)S(1)}, bf16[8,2,128,128]{3,2,1,0:T(8,128)(2,1)S(1)}, u32[]{:S(2)}, u32[]{:S(2)}) collective-permute-start(bf16[8,2,128,128]{3,2,1,0:T(8,128)(2,1)S(1)} %shard_map.75), channel_id=1, source_target_pairs={{0,2},{1,3},{2,0},{3,1},{4,6},{5,7},{6,4},{7,5},{8,10},{9,11},{10,... | collective-permute-start | bytes 1572872 | tf_op jit(solution)/shard_map/ppermute | solution.py:25
  96.1 17.0 %collective-permute-start.12 = (bf16[8,2,128,128]{3,2,1,0:T(8,128)(2,1)S(1)}, bf16[8,2,128,128]{3,2,1,0:T(8,128)(2,1)S(1)}, u32[]{:S(2)}, u32[]{:S(2)}) collective-permute-start(bf16[8,2,128,128]{3,2,1,0:T(8,128)(2,1)S(1)} %shard_map.74), channel_id=1, source_target_pairs={{0,3},{1,0},{2,1},{3,2},{4,7},{5,4},{6,5},{7,6},{8,11},{9,8},{10,9... | collective-permute-start | bytes 1572872 | tf_op jit(solution)/shard_map/ppermute | solution.py:25
  96.8 16.3 %collective-permute-start.10 = (bf16[8,2,128,128]{3,2,1,0:T(8,128)(2,1)S(1)}, bf16[8,2,128,128]{3,2,1,0:T(8,128)(2,1)S(1)}, u32[]{:S(2)}, u32[]{:S(2)}) collective-permute-start(bf16[8,2,128,128]{3,2,1,0:T(8,128)(2,1)S(1)} %shard_map.73), channel_id=1, source_target_pairs={{0,1},{1,2},{2,3},{3,0},{4,5},{5,6},{6,7},{7,4},{8,9},{9,10},{10,1... | collective-permute-start | bytes 1572872 | tf_op jit(solution)/shard_map/ppermute | solution.py:25
  (5 other events, 69.4 us)

commit v2 on v0

v2 whole, which is shorter than its diff:
```python
import functools

import jax
import jax.numpy as jnp
from jax import lax
from jax.experimental import pallas as pl
from jax.experimental.pallas import tpu as pltpu
from jax.sharding import PartitionSpec as P


SIDE = 4
HOPS = (0, 1, -1, 2)
VMEM = pltpu.VMEM
MIB = 1 << 20
BF16 = jnp.bfloat16
OTHER = {"x": "y", "y": "x"}


def move(array, along, hop):
    pairs = []
    for y in range(SIDE):
        for x in range(SIDE):
            to = (y, (x + hop) % SIDE) if along == "x" else ((y + hop) % SIDE, x)
            pairs.append((y * SIDE + x, to[0] * SIDE + to[1]))
    return lax.ppermute(array, "tp", pairs)


def sender(along, hop):
    t = lax.axis_index("tp")
    mine = t % SIDE if along == "x" else t // SIDE
    return (mine - hop + SIDE) % SIDE


def whole(n, space=VMEM):
    return [pl.BlockSpec(memory_space=space)] * n


def shape(*dims):
    return jax.ShapeDtypeStruct(dims, BF16)


def call(kernel, outs, args, out_space=VMEM, in_specs=None, limit=24 * MIB, scratch=(), alias=None, flops=0, nbytes=MIB):
    return pl.pallas_call(
        kernel,
        out_shape=outs,
        in_specs=in_specs or whole(len(args)),
        out_specs=jax.tree.map(lambda _: pl.BlockSpec(memory_space=out_space), outs),
        scratch_shapes=list(scratch),
        input_output_aliases=alias or {},
        compiler_params=pltpu.CompilerParams(vmem_limit_bytes=limit),
        cost_estimate=pl.CostEstimate(flops=flops, bytes_accessed=nbytes, transcendentals=0),
    )(*args)


def regroup(parts):
    return [jnp.concatenate([p[:, 32 * k : 32 * k + 32] for p in parts], axis=-1) for k in range(4)]


def ready_kernel(lat_in, rot_in, gain_in, key_in, value_in, rows, weights, lat, rot, gain, sems):
    copies = [
        pltpu.make_async_copy(src, dst, sems.at[i])
        for i, (src, dst) in enumerate(
            (
                (lat_in, lat),
                (gain_in, gain),
                (rot_in, rot),
                (key_in, weights.at[0:512, :]),
                (value_in, weights.at[512:1024, :]),
            )
        )
    ]
    for copy in copies:
        copy.start()
    copies[0].wait()
    copies[1].wait()
    gains = gain[...]
    for b in range(lat.shape[0]):
        v = lat[b].astype(jnp.float32)
        v = v * lax.rsqrt(jnp.mean(v * v, axis=-1, keepdims=True) + 1e-06) * gains
        v = v.astype(BF16)
        for j in range(4):
            rows[b, 32 * j : 32 * j + 32, :] = v[:, 128 * j : 128 * j + 128]
    copies[2].wait()
    for b in range(0, lat.shape[0], 8):
        four = []
        for q in range(4):
            pair = [rot[b + q].astype(jnp.float32), rot[b + q + 4].astype(jnp.float32)]
            four.append(jnp.concatenate(pair, axis=-1))
        turned = jnp.concatenate(four, axis=0).astype(BF16).T
        for k in range(2):
            parts = [turned[64 * k + 16 * d : 64 * k + 16 * d + 16] for d in range(4)]
            for q, part in enumerate(regroup(parts)):
                rows[b + q + 4 * k, 128:144, :] = part
    copies[3].wait()
    copies[4].wait()


def ready(latents, rotary, gain, key_up, value_up):
    b = latents.shape[0]
    return call(
        ready_kernel,
        (shape(b, 144, 128), shape(1024, 128)),
        (latents, rotary, gain.reshape(1, -1), key_up.reshape(512, 128), value_up.reshape(512, 128)),
        in_specs=whole(5, pltpu.HBM),
        limit=67043328,
        scratch=[
            VMEM(latents.shape, BF16),
            VMEM(rotary.shape, BF16),
            VMEM((1, 512), jnp.float32),
            pltpu.SemaphoreType.DMA((5,)),
        ],
    )


def expand_kernel(along, *refs):
    rows, head, out, block, rotary = refs[:4], *refs[4:]
    s = block.shape[0]
    for i, hop in enumerate(HOPS):
        place = sender(along, hop)
        at = pl.multiple_of(place * 32, 32)
        for b in range(s):
            for j in range(4):
                block[b, pl.ds(at, 32), 128 * j : 128 * j + 128] = rows[i][b, 32 * j : 32 * j + 32]
            rotary[place, b] = rows[i][b, 128:144]
    w = jnp.concatenate([head[0:512, :], head[512:1024, :]], axis=-1)
    for b in range(0, s, 2):
        wide = jnp.dot(
            block[b : b + 2].reshape(256, 512), w, preferred_element_type=jnp.float32
        ).astype(BF16)
        for k in range(2):
            part = wide[128 * k : 128 * k + 128]
            out[b + k, 0:128] = part[:, 0:128].T
            for d, turned in enumerate(regroup([rotary[p, b + k] for p in range(SIDE)])):
                out[b + k, 128 + 16 * d : 144 + 16 * d] = turned
            out[b + k, 192:320] = part[:, 128:256]


def expand(rows, head, along):
    s = rows[0].shape[0]
    return call(
        functools.partial(expand_kernel, along),
        shape(s, 320, 128),
        (*rows, head),
        limit=8 * MIB,
        scratch=[VMEM((s, 128, 512), BF16), VMEM((SIDE, s, 16, 128), BF16)],
        flops=s * 128 * 512 * 256 * 2,
    )


def join_kernel(*refs):
    x_got, y_got, keys, values, sorted_, lined, sems = refs[:4], refs[4:8], *refs[8:]
    s = sorted_.shape[1]
    copies = []

    def copy(src, dst):
        copies.append(pltpu.make_async_copy(src, dst, sems.at[len(copies)]))
        copies[-1].start()

    for i, hop in enumerate(HOPS):
        y = sender("y", hop)
        copy(x_got[i].at[:, 192:320], values.at[0:s, y])
        for b in range(s):
            lanes = pl.ds(pl.multiple_of(b * 512 + y * 128, 128), 128)
            copy(x_got[i].at[b, 0:192], keys.at[:, lanes])
    for i, hop in enumerate(HOPS):
        x = sender("x", hop)
        rows = pl.ds(pl.multiple_of(x * 32, 32), 32)
        for y in range(SIDE):
            copy(y_got[i].at[:, 192 + 32 * y : 224 + 32 * y], values.at[s : 2 * s, y, rows])
        for b in range(s):
            sorted_[x, b] = y_got[i][b, 0:192]
    for b in range(s):
        for y, part in enumerate(regroup([sorted_[x, b] for x in range(SIDE)])):
            lined[b, :, 128 * y : 128 * y + 128] = part
        copy(lined.at[b], keys.at[:, (s + b) * 512 : (s + b + 1) * 512])
    for each in copies:
        each.wait()


def join(x_got, y_got):
    s = x_got[0].shape[0]
    return call(
        join_kernel,
        (shape(192, 2 * s * 512), shape(2 * s, SIDE, 128, 128)),
        (*x_got, *y_got),
        out_space=pltpu.HBM,
        limit=10 * MIB,
        scratch=[
            VMEM((SIDE, s, 192, 128), BF16),
            VMEM((s, 192, 512), BF16),
            pltpu.SemaphoreType.DMA((SIDE * (s + 1) + SIDE * SIDE + s,)),
        ],
        nbytes=8 * MIB,
    )


def named_move(array, along, i, back=False):
    return move(array, along, -HOPS[i] if back else HOPS[i])


def shards(latents, rotary_rows, latent_gain, key_up, value_up):
    rows, head = ready(latents, rotary_rows, latent_gain, key_up, value_up)
    mine = lax.all_to_all(rows, "seq", split_axis=0, concat_axis=0, tiled=True)
    heads = {a: [head] + [named_move(head, a, i, back=True) for i in (1, 2, 3)] for a in "xy"}
    mine, heads["x"][1] = lax.optimization_barrier((mine, heads["x"][1]))
    half = mine.shape[0] // 2
    near = {"x": [mine[:half]], "y": [mine[half:]]}
    for i in (1, 2, 3):
        for a in "xy":
            near[a].append(named_move(near[a][0], a, i))
    got = {"x": [None] * 4, "y": [None] * 4}
    for i in (3, 1, 2, 0):
        for a in "xy":
            piece = expand(near[a], heads[OTHER[a]][i], a)
            got[a][i] = named_move(piece, OTHER[a], i) if i else piece
    keys, values = join(got["x"], got["y"])
    return keys[None, None], values.reshape(1, -1, 1, 128)


def solution(mesh):
    return jax.shard_map(
        shards,
        mesh=mesh,
        in_specs=(
            P(None, ("seq", "tp"), None),
            P(None, ("seq", "tp"), None),
            P(),
            P(None, "tp", None),
            P(None, "tp", None),
        ),
        out_specs=(P("seq", "tp", None, None), P("seq", None, "tp", None)),
        check_vma=False,
    )
```

time: 153 us -> 129 us (0.84)
  starting transfers between devices: 0.04 us -> 34.8 us
  blocking collectives: 30 us -> 0 us
  between operations: 14.1 us -> 0.91 us
  Pallas kernels: 0 us -> 10.9 us
  matrix products: 10 us -> 0 us
  local copies, waits for them, and re-layouts: 9.92 us -> 0.05 us
  other arithmetic: 6.3 us -> 0 us
    all_gather x1 -> x0, waiting for transfers between devices: 82 us -> none  [in_one_piece_2(): filled, at, done = (lax.all_gather(both, axis, axis=dim, tiled=True), 0, [])]
    ppermute x0 -> x18, waiting for transfers between devices: none -> 71 us  [move(): return lax.ppermute(array, 'tp', pairs)]
    all_to_all x1 -> x0, blocking collectives: 30 us -> none  [in_one_piece(): lax.all_to_all(both, axis, split_axis=split_dim, concat_axis=concat_dim,...]
    ppermute x0 -> x18, starting transfers between devices: none -> 24.6 us  [move(): return lax.ppermute(array, 'tp', pairs)]
    pallas_call x0 -> x10, Pallas kernels: none -> 10.9 us  [call(): pl.pallas_call(kernel, out_shape=outs, in_specs=in_specs or whole(len(arg...]
    all_to_all x0 -> x1, waiting for transfers between devices: none -> 10.3 us  [shards(): mine = lax.all_to_all(rows, 'seq', split_axis=0, concat_axis=0, tiled=True)]
    all_to_all x0 -> x1, starting transfers between devices: none -> 10.1 us  [shards(): mine = lax.all_to_all(rows, 'seq', split_axis=0, concat_axis=0, tiled=True)]
    dot_general x2 -> x0, matrix products: 10 us -> none  [the longest x1 6.37 us: expand_rows(): jnp.einsum('btr,rhk->bthk', rows, key_up, preferred_element_type=jnp.floa...]
  transfers between devices with their start and end apart: 1 -> 19, of which waited for: 1 -> 13; matrix products, arithmetic and copies ran while one was open for 0% -> 0% of each run, Pallas kernels for 0% -> 4%
where the time goes in v2:
time: 129 us; the launch traced here: 128 us
  waiting for transfers between devices  81.3 us (63%)
  starting transfers between devices  34.8 us (27%)
  Pallas kernels  10.9 us (8%)
    ppermute x18, waiting for transfers between devices, move(): return lax.ppermute(array, 'tp', pairs)  71 us
    ppermute x18, starting transfers between devices, move(): return lax.ppermute(array, 'tp', pairs)  24.6 us
    pallas_call x10, Pallas kernels, call(): pl.pallas_call(kernel, out_shape=outs, in_specs=in_specs or whole(len(arg...  10.9 us
    all_to_all x1, waiting for transfers between devices, shards(): mine = lax.all_to_all(rows, 'seq', split_axis=0, concat_axis=0, tiled=True)  10.3 us
    all_to_all x1, starting transfers between devices, shards(): mine = lax.all_to_all(rows, 'seq', split_axis=0, concat_axis=0, tiled=True)  10.1 us
  transfers between devices with their start and end apart: 19, of which 13 were waited for; matrix products, arithmetic and copies ran while one was open for 0% of the time, Pallas kernels for 4%

profile of v2, /device:TPU:1, one launch (start us, length us, event | category | flops | bytes accessed | tf_op | source)
XLA Modules:
  0.0 127.8 jit_solution(16244559149852650607)
XLA Ops:
  0.6 2.4 %shard_map.68 = (bf16[16,144,128]{2,1,0:T(8,128)(2,1)}, bf16[1024,128]{1,0:T(8,128)(2,1)}) custom-call(bf16[16,32,512]{2,1,0:T(8,128)(2,1)} %lat_in.1, bf16[16,32,64]{2,1,0:T(8,128)(2,1)} %rot_in.1, f32[1,512]{1,0:T(1,128)} %bitcast.7, bf16[512,128]{1,0:T(8,128)(2,1)} %bitcast.5, bf16[512,128]{1,0:T(8,128)(2,1)} %bitcast.6), custom_call_target="tpu_custom_call" | custom-call | bytes 1048576 | tf_op jit(solution)/shard_map/pallas_call | solution.py:43
  3.1 10.1 %all-to-all-start = ((bf16[16,144,128]{2,1,0:T(8,128)(2,1)}), bf16[16,144,128]{2,1,0:T(8,128)(2,1)S(1)}, u32[]{:S(2)}, u32[]{:S(2)}) async-start(bf16[16,144,128]{2,1,0:T(8,128)(2,1)} %get-tuple-element.8), calls=%async_computation | async-start | bytes 1179648 | tf_op jit(solution)/shard_map/all_to_all | solution.py:203
  13.2 2.5 %collective-permute-start = (bf16[1024,128]{1,0:T(8,128)(2,1)}, bf16[1024,128]{1,0:T(8,128)(2,1)S(1)}, u32[]{:S(2)}, u32[]{:S(2)}) collective-permute-start(bf16[1024,128]{1,0:T(8,128)(2,1)} %get-tuple-element.9.refs_4_), channel_id=1, source_target_pairs={{0,3},{1,0},{2,1},{3,2},{4,7},{5,4},{6,5},{7,6},{8,11},{9,8},{10,9... | collective-permute-start | bytes 786440 | tf_op jit(solution)/shard_map/ppermute | solution.py:25
  15.7 5.8 %collective-permute-done.refs_4_ = bf16[1024,128]{1,0:T(8,128)(2,1)S(1)} collective-permute-done((bf16[1024,128]{1,0:T(8,128)(2,1)}, bf16[1024,128]{1,0:T(8,128)(2,1)S(1)}, u32[]{:S(2)}, u32[]{:S(2)}) %collective-permute-start) | collective-permute-done | bytes 262176 | tf_op jit(solution)/shard_map/ppermute | solution.py:25
  21.5 10.3 %all-to-all-done = bf16[16,144,128]{2,1,0:T(8,128)(2,1)S(1)} async-done(((bf16[16,144,128]{2,1,0:T(8,128)(2,1)}), bf16[16,144,128]{2,1,0:T(8,128)(2,1)S(1)}, u32[]{:S(2)}, u32[]{:S(2)}) %all-to-all-start) | async-done | bytes 589856 | tf_op jit(solution)/shard_map/all_to_all | solution.py:203
  31.8 3.0 %collective-permute-start.12 = (bf16[8,144,128]{2,1,0:T(8,128)(2,1)S(1)}, bf16[8,144,128]{2,1,0:T(8,128)(2,1)S(1)}, u32[]{:S(2)}, u32[]{:S(2)}) collective-permute-start(bf16[8,144,128]{2,1,0:T(8,128)(2,1)S(1)} %get-tuple-element.14.refs_0_), channel_id=1, source_target_pairs={{0,8},{1,9},{2,10},{3,11},{4,12},{5,13},{6,14},{7,15},{8,0},{9,1},... | collective-permute-start | bytes 884744 | tf_op jit(solution)/shard_map/ppermute | solution.py:25
  36.3 5.9 %collective-permute-done.12.refs_3_ = bf16[8,144,128]{2,1,0:T(8,128)(2,1)S(1)} collective-permute-done((bf16[8,144,128]{2,1,0:T(8,128)(2,1)S(1)}, bf16[8,144,128]{2,1,0:T(8,128)(2,1)S(1)}, u32[]{:S(2)}, u32[]{:S(2)}) %collective-permute-start.12) | collective-permute-done | bytes 294944 | tf_op jit(solution)/shard_map/ppermute | solution.py:25
  42.1 5.8 %collective-permute-done.11.refs_2_ = bf16[8,144,128]{2,1,0:T(8,128)(2,1)S(1)} collective-permute-done((bf16[8,144,128]{2,1,0:T(8,128)(2,1)S(1)}, bf16[8,144,128]{2,1,0:T(8,128)(2,1)S(1)}, u32[]{:S(2)}, u32[]{:S(2)}) %collective-permute-start.11) | collective-permute-done | bytes 294944 | tf_op jit(solution)/shard_map/ppermute | solution.py:25
  48.6 1.3 %collective-permute-start.13 = (bf16[8,320,128]{2,1,0:T(8,128)(2,1)S(1)}, bf16[8,320,128]{2,1,0:T(8,128)(2,1)S(1)}, u32[]{:S(2)}, u32[]{:S(2)}) collective-permute-start(bf16[8,320,128]{2,1,0:T(8,128)(2,1)S(1)} %shard_map.74), channel_id=1, source_target_pairs={{0,1},{1,2},{2,3},{3,0},{4,5},{5,6},{6,7},{7,4},{8,9},{9,10},{10,1... | collective-permute-start | bytes 1966088 | tf_op jit(solution)/shard_map/ppermute | solution.py:25
  49.9 2.5 %collective-permute-start.16 = (bf16[1024,128]{1,0:T(8,128)(2,1)S(1)}, bf16[1024,128]{1,0:T(8,128)(2,1)S(1)}, u32[]{:S(2)}, u32[]{:S(2)}) collective-permute-start(bf16[1024,128]{1,0:T(8,128)(2,1)S(1)} %copy-done), channel_id=1, source_target_pairs={{0,2},{1,3},{2,0},{3,1},{4,6},{5,7},{6,4},{7,5},{8,10},{9,11},{10,... | collective-permute-start | bytes 786440 | tf_op jit(solution)/shard_map/ppermute | solution.py:25
  52.4 2.3 %collective-permute-start.3 = (bf16[8,144,128]{2,1,0:T(8,128)(2,1)S(1)}, bf16[8,144,128]{2,1,0:T(8,128)(2,1)S(1)}, u32[]{:S(2)}, u32[]{:S(2)}) collective-permute-start(bf16[8,144,128]{2,1,0:T(8,128)(2,1)S(1)} %get-tuple-element.15.refs_0_), channel_id=1, source_target_pairs={{0,2},{1,3},{2,0},{3,1},{4,6},{5,7},{6,4},{7,5},{8,10},{9,11},{10,... | collective-permute-start | bytes 884744 | tf_op jit(solution)/shard_map/ppermute | solution.py:25
  54.7 2.6 %collective-permute-start.4 = (bf16[1024,128]{1,0:T(8,128)(2,1)S(1)}, bf16[1024,128]{1,0:T(8,128)(2,1)S(1)}, u32[]{:S(2)}, u32[]{:S(2)}) collective-permute-start(bf16[1024,128]{1,0:T(8,128)(2,1)S(1)} %copy-done), channel_id=1, source_target_pairs={{0,12},{1,13},{2,14},{3,15},{4,0},{5,1},{6,2},{7,3},{8,4},{9,5},{1... | collective-permute-start | bytes 786440 | tf_op jit(solution)/shard_map/ppermute | solution.py:25
  57.3 15.3 %collective-permute-done.16.refs_4_ = bf16[1024,128]{1,0:T(8,128)(2,1)S(1)} collective-permute-done((bf16[1024,128]{1,0:T(8,128)(2,1)S(1)}, bf16[1024,128]{1,0:T(8,128)(2,1)S(1)}, u32[]{:S(2)}, u32[]{:S(2)}) %collective-permute-start.16) | collective-permute-done | bytes 262176 | tf_op jit(solution)/shard_map/ppermute | solution.py:25
  72.6 4.6 %collective-permute-done.14.refs_4_ = bf16[1024,128]{1,0:T(8,128)(2,1)S(1)} collective-permute-done((bf16[1024,128]{1,0:T(8,128)(2,1)S(1)}, bf16[1024,128]{1,0:T(8,128)(2,1)S(1)}, u32[]{:S(2)}, u32[]{:S(2)}) %collective-permute-start.14) | collective-permute-done | bytes 262176 | tf_op jit(solution)/shard_map/ppermute | solution.py:25
  78.3 6.3 %collective-permute-done.3.refs_3_ = bf16[8,144,128]{2,1,0:T(8,128)(2,1)S(1)} collective-permute-done((bf16[8,144,128]{2,1,0:T(8,128)(2,1)S(1)}, bf16[8,144,128]{2,1,0:T(8,128)(2,1)S(1)}, u32[]{:S(2)}, u32[]{:S(2)}) %collective-permute-start.3) | collective-permute-done | bytes 294944 | tf_op jit(solution)/shard_map/ppermute | solution.py:25
  84.6 2.7 %collective-permute-start.8 = (bf16[1024,128]{1,0:T(8,128)(2,1)S(1)}, bf16[1024,128]{1,0:T(8,128)(2,1)S(1)}, u32[]{:S(2)}, u32[]{:S(2)}) collective-permute-start(bf16[1024,128]{1,0:T(8,128)(2,1)S(1)} %copy-done), channel_id=1, source_target_pairs={{0,8},{1,9},{2,10},{3,11},{4,12},{5,13},{6,14},{7,15},{8,0},{9,1},... | collective-permute-start | bytes 786440 | tf_op jit(solution)/shard_map/ppermute | solution.py:25
  88.9 2.6 %collective-permute-done.1.refs_1_ = bf16[8,144,128]{2,1,0:T(8,128)(2,1)S(1)} collective-permute-done((bf16[8,144,128]{2,1,0:T(8,128)(2,1)S(1)}, bf16[8,144,128]{2,1,0:T(8,128)(2,1)S(1)}, u32[]{:S(2)}, u32[]{:S(2)}) %collective-permute-start.1) | collective-permute-done | bytes 294944 | tf_op jit(solution)/shard_map/ppermute | solution.py:25
  92.7 1.2 collective-permute-start.5
  94.6 1.6 %collective-permute-start.7 = (bf16[8,320,128]{2,1,0:T(8,128)(2,1)S(1)}, bf16[8,320,128]{2,1,0:T(8,128)(2,1)S(1)}, u32[]{:S(2)}, u32[]{:S(2)}) collective-permute-start(bf16[8,320,128]{2,1,0:T(8,128)(2,1)S(1)} %shard_map.71), channel_id=1, source_target_pairs={{0,12},{1,13},{2,14},{3,15},{4,0},{5,1},{6,2},{7,3},{8,4},{9,5},{1... | collective-permute-start | bytes 1966088 | tf_op jit(solution)/shard_map/ppermute | solution.py:25
  96.9 1.7 %collective-permute-start.9 = (bf16[8,320,128]{2,1,0:T(8,128)(2,1)S(1)}, bf16[8,320,128]{2,1,0:T(8,128)(2,1)S(1)}, u32[]{:S(2)}, u32[]{:S(2)}) collective-permute-start(bf16[8,320,128]{2,1,0:T(8,128)(2,1)S(1)} %shard_map.72), channel_id=1, source_target_pairs={{0,8},{1,9},{2,10},{3,11},{4,12},{5,13},{6,14},{7,15},{8,0},{9,1},... | collective-permute-start | bytes 1966088 | tf_op jit(solution)/shard_map/ppermute | solution.py:25
  99.9 2.8 %collective-permute-done.15.refs_6_ = bf16[8,320,128]{2,1,0:T(8,128)(2,1)S(1)} collective-permute-done((bf16[8,320,128]{2,1,0:T(8,128)(2,1)S(1)}, bf16[8,320,128]{2,1,0:T(8,128)(2,1)S(1)}, u32[]{:S(2)}, u32[]{:S(2)}) %collective-permute-start.15) | collective-permute-done | bytes 655392 | tf_op jit(solution)/shard_map/ppermute | solution.py:25
  102.8 6.0 %collective-permute-done.17.refs_7_ = bf16[8,320,128]{2,1,0:T(8,128)(2,1)S(1)} collective-permute-done((bf16[8,320,128]{2,1,0:T(8,128)(2,1)S(1)}, bf16[8,320,128]{2,1,0:T(8,128)(2,1)S(1)}, u32[]{:S(2)}, u32[]{:S(2)}) %collective-permute-start.17) | collective-permute-done | bytes 655392 | tf_op jit(solution)/shard_map/ppermute | solution.py:25
  109.9 14.7 %collective-permute-done.9.refs_3_ = bf16[8,320,128]{2,1,0:T(8,128)(2,1)S(1)} collective-permute-done((bf16[8,320,128]{2,1,0:T(8,128)(2,1)S(1)}, bf16[8,320,128]{2,1,0:T(8,128)(2,1)S(1)}, u32[]{:S(2)}, u32[]{:S(2)}) %collective-permute-start.9) | collective-permute-done | bytes 655392 | tf_op jit(solution)/shard_map/ppermute | solution.py:25
  124.6 3.0 %shard_map.77 = (bf16[192,8192]{1,0:T(8,128)(2,1)}, bf16[16,4,128,128]{3,2,1,0:T(8,128)(2,1)}) custom-call(bf16[8,320,128]{2,1,0:T(8,128)(2,1)S(1)} %shard_map.69.refs_0_, bf16[8,320,128]{2,1,0:T(8,128)(2,1)S(1)} %collective-permute-done.5.refs_1_, bf16[8,320,128]{2,1,0:T(8,128)(2,1)S(1)} %collective-permute-done.7.refs_2_, ...), custom_call_target="tpu_custom_call" | custom-call | bytes 8388608 | tf_op jit(solution)/shard_map/pallas_call | solution.py:43
  (27 shorter events, 9.9 us)
Async XLA Ops:
  3.1 46.9 %copy-start = (bf16[1024,128]{1,0:T(8,128)(2,1)S(1)}, bf16[1024,128]{1,0:T(8,128)(2,1)}, u32[]{:S(2)}) copy-start(bf16[1024,128]{1,0:T(8,128)(2,1)} %get-tuple-element.9.refs_4_) | copy-start | bytes 786436
  3.1 28.7 %all-to-all-start = ((bf16[16,144,128]{2,1,0:T(8,128)(2,1)}), bf16[16,144,128]{2,1,0:T(8,128)(2,1)S(1)}, u32[]{:S(2)}, u32[]{:S(2)}) async-start(bf16[16,144,128]{2,1,0:T(8,128)(2,1)} %get-tuple-element.8), calls=%async_computation | async-start | bytes 1179648 | tf_op jit(solution)/shard_map/all_to_all | solution.py:203
  13.2 8.3 %collective-permute-start = (bf16[1024,128]{1,0:T(8,128)(2,1)}, bf16[1024,128]{1,0:T(8,128)(2,1)S(1)}, u32[]{:S(2)}, u32[]{:S(2)}) collective-permute-start(bf16[1024,128]{1,0:T(8,128)(2,1)} %get-tuple-element.9.refs_4_), channel_id=1, source_target_pairs={{0,3},{1,0},{2,1},{3,2},{4,7},{5,4},{6,5},{7,6},{8,11},{9,8},{10,9... | collective-permute-start | bytes 786440 | tf_op jit(solution)/shard_map/ppermute | solution.py:25
  31.8 10.3 %collective-permute-start.12 = (bf16[8,144,128]{2,1,0:T(8,128)(2,1)S(1)}, bf16[8,144,128]{2,1,0:T(8,128)(2,1)S(1)}, u32[]{:S(2)}, u32[]{:S(2)}) collective-permute-start(bf16[8,144,128]{2,1,0:T(8,128)(2,1)S(1)} %get-tuple-element.14.refs_0_), channel_id=1, source_target_pairs={{0,8},{1,9},{2,10},{3,11},{4,12},{5,13},{6,14},{7,15},{8,0},{9,1},... | collective-permute-start | bytes 884744 | tf_op jit(solution)/shard_map/ppermute | solution.py:25
  34.8 13.2 %collective-permute-start.11 = (bf16[8,144,128]{2,1,0:T(8,128)(2,1)S(1)}, bf16[8,144,128]{2,1,0:T(8,128)(2,1)S(1)}, u32[]{:S(2)}, u32[]{:S(2)}) collective-permute-start(bf16[8,144,128]{2,1,0:T(8,128)(2,1)S(1)} %get-tuple-element.14.refs_0_), channel_id=1, source_target_pairs={{0,12},{1,13},{2,14},{3,15},{4,0},{5,1},{6,2},{7,3},{8,4},{9,5},{1... | collective-permute-start | bytes 884744 | tf_op jit(solution)/shard_map/ppermute | solution.py:25
  35.6 12.4 %collective-permute-start.10 = (bf16[8,144,128]{2,1,0:T(8,128)(2,1)S(1)}, bf16[8,144,128]{2,1,0:T(8,128)(2,1)S(1)}, u32[]{:S(2)}, u32[]{:S(2)}) collective-permute-start(bf16[8,144,128]{2,1,0:T(8,128)(2,1)S(1)} %get-tuple-element.14.refs_0_), channel_id=1, source_target_pairs={{0,4},{1,5},{2,6},{3,7},{4,8},{5,9},{6,10},{7,11},{8,12},{9,13},{1... | collective-permute-start | bytes 884744 | tf_op jit(solution)/shard_map/ppermute | solution.py:25
  48.6 48.3 %collective-permute-start.13 = (bf16[8,320,128]{2,1,0:T(8,128)(2,1)S(1)}, bf16[8,320,128]{2,1,0:T(8,128)(2,1)S(1)}, u32[]{:S(2)}, u32[]{:S(2)}) collective-permute-start(bf16[8,320,128]{2,1,0:T(8,128)(2,1)S(1)} %shard_map.74), channel_id=1, source_target_pairs={{0,1},{1,2},{2,3},{3,0},{4,5},{5,6},{6,7},{7,4},{8,9},{9,10},{10,1... | collective-permute-start | bytes 1966088 | tf_op jit(solution)/shard_map/ppermute | solution.py:25
  49.9 22.7 %collective-permute-start.16 = (bf16[1024,128]{1,0:T(8,128)(2,1)S(1)}, bf16[1024,128]{1,0:T(8,128)(2,1)S(1)}, u32[]{:S(2)}, u32[]{:S(2)}) collective-permute-start(bf16[1024,128]{1,0:T(8,128)(2,1)S(1)} %copy-done), channel_id=1, source_target_pairs={{0,2},{1,3},{2,0},{3,1},{4,6},{5,7},{6,4},{7,5},{8,10},{9,11},{10,... | collective-permute-start | bytes 786440 | tf_op jit(solution)/shard_map/ppermute | solution.py:25
  52.4 24.8 %collective-permute-start.14 = (bf16[1024,128]{1,0:T(8,128)(2,1)S(1)}, bf16[1024,128]{1,0:T(8,128)(2,1)S(1)}, u32[]{:S(2)}, u32[]{:S(2)}) collective-permute-start(bf16[1024,128]{1,0:T(8,128)(2,1)S(1)} %copy-done), channel_id=1, source_target_pairs={{0,1},{1,2},{2,3},{3,0},{4,5},{5,6},{6,7},{7,4},{8,9},{9,10},{10,1... | collective-permute-start | bytes 786440 | tf_op jit(solution)/shard_map/ppermute | solution.py:25
  52.4 32.2 %collective-permute-start.3 = (bf16[8,144,128]{2,1,0:T(8,128)(2,1)S(1)}, bf16[8,144,128]{2,1,0:T(8,128)(2,1)S(1)}, u32[]{:S(2)}, u32[]{:S(2)}) collective-permute-start(bf16[8,144,128]{2,1,0:T(8,128)(2,1)S(1)} %get-tuple-element.15.refs_0_), channel_id=1, source_target_pairs={{0,2},{1,3},{2,0},{3,1},{4,6},{5,7},{6,4},{7,5},{8,10},{9,11},{10,... | collective-permute-start | bytes 884744 | tf_op jit(solution)/shard_map/ppermute | solution.py:25
  54.7 22.5 %collective-permute-start.4 = (bf16[1024,128]{1,0:T(8,128)(2,1)S(1)}, bf16[1024,128]{1,0:T(8,128)(2,1)S(1)}, u32[]{:S(2)}, u32[]{:S(2)}) collective-permute-start(bf16[1024,128]{1,0:T(8,128)(2,1)S(1)} %copy-done), channel_id=1, source_target_pairs={{0,12},{1,13},{2,14},{3,15},{4,0},{5,1},{6,2},{7,3},{8,4},{9,5},{1... | collective-permute-start | bytes 786440 | tf_op jit(solution)/shard_map/ppermute | solution.py:25
  72.6 16.0 %collective-permute-start.2 = (bf16[8,144,128]{2,1,0:T(8,128)(2,1)S(1)}, bf16[8,144,128]{2,1,0:T(8,128)(2,1)S(1)}, u32[]{:S(2)}, u32[]{:S(2)}) collective-permute-start(bf16[8,144,128]{2,1,0:T(8,128)(2,1)S(1)} %get-tuple-element.15.refs_0_), channel_id=1, source_target_pairs={{0,3},{1,0},{2,1},{3,2},{4,7},{5,4},{6,5},{7,6},{8,11},{9,8},{10,9... | collective-permute-start | bytes 884744 | tf_op jit(solution)/shard_map/ppermute | solution.py:25
  77.2 14.3 %collective-permute-start.1 = (bf16[8,144,128]{2,1,0:T(8,128)(2,1)S(1)}, bf16[8,144,128]{2,1,0:T(8,128)(2,1)S(1)}, u32[]{:S(2)}, u32[]{:S(2)}) collective-permute-start(bf16[8,144,128]{2,1,0:T(8,128)(2,1)S(1)} %get-tuple-element.15.refs_0_), channel_id=1, source_target_pairs={{0,1},{1,2},{2,3},{3,0},{4,5},{5,6},{6,7},{7,4},{8,9},{9,10},{10,1... | collective-permute-start | bytes 884744 | tf_op jit(solution)/shard_map/ppermute | solution.py:25
  77.2 15.5 %collective-permute-start.6 = (bf16[1024,128]{1,0:T(8,128)(2,1)S(1)}, bf16[1024,128]{1,0:T(8,128)(2,1)S(1)}, u32[]{:S(2)}, u32[]{:S(2)}) collective-permute-start(bf16[1024,128]{1,0:T(8,128)(2,1)S(1)} %copy-done), channel_id=1, source_target_pairs={{0,4},{1,5},{2,6},{3,7},{4,8},{5,9},{6,10},{7,11},{8,12},{9,13},{1... | collective-permute-start | bytes 786440 | tf_op jit(solution)/shard_map/ppermute | solution.py:25
  84.6 10.0 %collective-permute-start.8 = (bf16[1024,128]{1,0:T(8,128)(2,1)S(1)}, bf16[1024,128]{1,0:T(8,128)(2,1)S(1)}, u32[]{:S(2)}, u32[]{:S(2)}) collective-permute-start(bf16[1024,128]{1,0:T(8,128)(2,1)S(1)} %copy-done), channel_id=1, source_target_pairs={{0,8},{1,9},{2,10},{3,11},{4,12},{5,13},{6,14},{7,15},{8,0},{9,1},... | collective-permute-start | bytes 786440 | tf_op jit(solution)/shard_map/ppermute | solution.py:25
  88.6 14.2 %collective-permute-start.15 = (bf16[8,320,128]{2,1,0:T(8,128)(2,1)S(1)}, bf16[8,320,128]{2,1,0:T(8,128)(2,1)S(1)}, u32[]{:S(2)}, u32[]{:S(2)}) collective-permute-start(bf16[8,320,128]{2,1,0:T(8,128)(2,1)S(1)} %shard_map.75), channel_id=1, source_target_pairs={{0,3},{1,0},{2,1},{3,2},{4,7},{5,4},{6,5},{7,6},{8,11},{9,8},{10,9... | collective-permute-start | bytes 1966088 | tf_op jit(solution)/shard_map/ppermute | solution.py:25
  91.5 17.3 %collective-permute-start.17 = (bf16[8,320,128]{2,1,0:T(8,128)(2,1)S(1)}, bf16[8,320,128]{2,1,0:T(8,128)(2,1)S(1)}, u32[]{:S(2)}, u32[]{:S(2)}) collective-permute-start(bf16[8,320,128]{2,1,0:T(8,128)(2,1)S(1)} %shard_map.76), channel_id=1, source_target_pairs={{0,2},{1,3},{2,0},{3,1},{4,6},{5,7},{6,4},{7,5},{8,10},{9,11},{10,... | collective-permute-start | bytes 1966088 | tf_op jit(solution)/shard_map/ppermute | solution.py:25
  92.7 16.8 %collective-permute-start.5 = (bf16[8,320,128]{2,1,0:T(8,128)(2,1)S(1)}, bf16[8,320,128]{2,1,0:T(8,128)(2,1)S(1)}, u32[]{:S(2)}, u32[]{:S(2)}) collective-permute-start(bf16[8,320,128]{2,1,0:T(8,128)(2,1)S(1)} %shard_map.70), channel_id=1, source_target_pairs={{0,4},{1,5},{2,6},{3,7},{4,8},{5,9},{6,10},{7,11},{8,12},{9,13},{1... | collective-permute-start | bytes 1966088 | tf_op jit(solution)/shard_map/ppermute | solution.py:25
  94.6 15.3 %collective-permute-start.7 = (bf16[8,320,128]{2,1,0:T(8,128)(2,1)S(1)}, bf16[8,320,128]{2,1,0:T(8,128)(2,1)S(1)}, u32[]{:S(2)}, u32[]{:S(2)}) collective-permute-start(bf16[8,320,128]{2,1,0:T(8,128)(2,1)S(1)} %shard_map.71), channel_id=1, source_target_pairs={{0,12},{1,13},{2,14},{3,15},{4,0},{5,1},{6,2},{7,3},{8,4},{9,5},{1... | collective-permute-start | bytes 1966088 | tf_op jit(solution)/shard_map/ppermute | solution.py:25
  96.9 27.7 %collective-permute-start.9 = (bf16[8,320,128]{2,1,0:T(8,128)(2,1)S(1)}, bf16[8,320,128]{2,1,0:T(8,128)(2,1)S(1)}, u32[]{:S(2)}, u32[]{:S(2)}) collective-permute-start(bf16[8,320,128]{2,1,0:T(8,128)(2,1)S(1)} %shard_map.72), channel_id=1, source_target_pairs={{0,8},{1,9},{2,10},{3,11},{4,12},{5,13},{6,14},{7,15},{8,0},{9,1},... | collective-permute-start | bytes 1966088 | tf_op jit(solution)/shard_map/ppermute | solution.py:25

commit v3 on v2

--- a/solution.py
+++ b/solution.py
@@ -112,83 +112,90 @@
     )
 
 
-def expand_kernel(along, *refs):
-    rows, head, out, block, rotary = refs[:4], *refs[4:]
-    s = block.shape[0]
-    for i, hop in enumerate(HOPS):
-        place = sender(along, hop)
-        at = pl.multiple_of(place * 32, 32)
-        for b in range(s):
-            for j in range(4):
-                block[b, pl.ds(at, 32), 128 * j : 128 * j + 128] = rows[i][b, 32 * j : 32 * j + 32]
-            rotary[place, b] = rows[i][b, 128:144]
+def expand_kernel(n, *refs):
+    rows, head, out = refs[:n], refs[n], refs[n + 1]
     w = jnp.concatenate([head[0:512, :], head[512:1024, :]], axis=-1)
-    for b in range(0, s, 2):
-        wide = jnp.dot(
-            block[b : b + 2].reshape(256, 512), w, preferred_element_type=jnp.float32
-        ).astype(BF16)
-        for k in range(2):
-            part = wide[128 * k : 128 * k + 128]
-            out[b + k, 0:128] = part[:, 0:128].T
-            for d, turned in enumerate(regroup([rotary[p, b + k] for p in range(SIDE)])):
-                out[b + k, 128 + 16 * d : 144 + 16 * d] = turned
-            out[b + k, 192:320] = part[:, 128:256]
-
-
-def expand(rows, head, along):
-    s = rows[0].shape[0]
+    for i in range(n):
+        a = rows[i]
+        for g in range(a.shape[0] // 4):
+            four = a[4 * g : 4 * g + 4]
+            lhs = jnp.concatenate(
+                [four[:, 32 * j : 32 * j + 32].reshape(128, 128) for j in range(4)], axis=-1
+            )
+            wide = jnp.dot(lhs, w, preferred_element_type=jnp.float32).astype(BF16)
+            out[i, g, 0:128] = wide[:, 0:128].T
+            for d, turned in enumerate(regroup([four[k, 128:144] for k in range(4)])):
+                out[i, g, 128 + 16 * d : 144 + 16 * d] = turned
+            out[i, g, 192:320] = wide[:, 128:256]
+
+
+def expand(rows, head):
+    n, s = len(rows), rows[0].shape[0]
     return call(
-        functools.partial(expand_kernel, along),
-        shape(s, 320, 128),
+        functools.partial(expand_kernel, n),
+        shape(n, s // 4, 320, 128),
         (*rows, head),
-        limit=8 * MIB,
-        scratch=[VMEM((s, 128, 512), BF16), VMEM((SIDE, s, 16, 128), BF16)],
-        flops=s * 128 * 512 * 256 * 2,
-    )
-
-
-def join_kernel(*refs):
-    x_got, y_got, keys, values, sorted_, lined, sems = refs[:4], refs[4:8], *refs[8:]
-    s = sorted_.shape[1]
+        limit=4 * MIB,
+        flops=n * s * 32 * 512 * 256 * 2,
+    )
+
+
+def join_kernel(counts, *refs):
+    pieces, (keys, values, sorted_, lined, sems) = refs[: sum(counts)], refs[sum(counts) :]
+    groups = sorted_.shape[2]
     copies = []
 
     def copy(src, dst):
         copies.append(pltpu.make_async_copy(src, dst, sems.at[len(copies)]))
         copies[-1].start()
 
-    for i, hop in enumerate(HOPS):
-        y = sender("y", hop)
-        copy(x_got[i].at[:, 192:320], values.at[0:s, y])
-        for b in range(s):
-            lanes = pl.ds(pl.multiple_of(b * 512 + y * 128, 128), 128)
-            copy(x_got[i].at[b, 0:192], keys.at[:, lanes])
-    for i, hop in enumerate(HOPS):
-        x = sender("x", hop)
-        rows = pl.ds(pl.multiple_of(x * 32, 32), 32)
-        for y in range(SIDE):
-            copy(y_got[i].at[:, 192 + 32 * y : 224 + 32 * y], values.at[s : 2 * s, y, rows])
-        for b in range(s):
-            sorted_[x, b] = y_got[i][b, 0:192]
-    for b in range(s):
-        for y, part in enumerate(regroup([sorted_[x, b] for x in range(SIDE)])):
-            lined[b, :, 128 * y : 128 * y + 128] = part
-        copy(lined.at[b], keys.at[:, (s + b) * 512 : (s + b + 1) * 512])
+    at = 0
+    for h, (outer, inner) in enumerate(("yx", "xy")):
+        sources = []
+        for o in range(len(HOPS)):
+            mine = pieces[at : at + counts[h * 4 + o]]
+            at += len(mine)
+            sources.append([p.at[k] for p in mine for k in range(p.shape[0])])
+        for o in range(4):
+            for n in range(4):
+                place = {outer: sender(outer, HOPS[o]), inner: sender(inner, HOPS[n])}
+                rows = pl.ds(pl.multiple_of(place["x"] * 32, 32), 32)
+                for g in range(groups):
+                    for k in range(4):
+                        copy(
+                            sources[o][n].at[g, 192 + 32 * k : 224 + 32 * k],
+                            values.at[(h * groups + g) * 4 + k, place["y"], rows],
+                        )
+        for o in range(4):
+            for n in range(4):
+                place = {outer: sender(outer, HOPS[o]), inner: sender(inner, HOPS[n])}
+                slot = place["y"] * SIDE + place["x"]
+                for g in range(groups):
+                    sorted_[h, slot, g] = sources[o][n][g, 0:192]
+        for g in range(groups):
+            for y in range(SIDE):
+                parts = [sorted_[h, y * SIDE + x, g] for x in range(SIDE)]
+                for k, part in enumerate(regroup(parts)):
+                    lined[h * groups + g, :, 512 * k + 128 * y : 512 * k + 128 * y + 128] = part
+            first = (h * groups + g) * 2048
+            copy(lined.at[h * groups + g], keys.at[:, first : first + 2048])
     for each in copies:
         each.wait()
 
 
 def join(x_got, y_got):
-    s = x_got[0].shape[0]
+    groups = x_got[0][0].shape[1]
+    got = x_got + y_got
     return call(
-        join_kernel,
-        (shape(192, 2 * s * 512), shape(2 * s, SIDE, 128, 128)),
-        (*x_got, *y_got),
+        functools.partial(join_kernel, tuple(map(len, got))),
+        (shape(192, 2 * groups * 2048), shape(2 * groups * 4, SIDE, 128, 128)),
+        sum(got, []),
         out_space=pltpu.HBM,
-        limit=10 * MIB,
+        limit=16 * MIB,
         scratch=[
-            VMEM((SIDE, s, 192, 128), BF16),
-            VMEM((s, 192, 512), BF16),
-            pltpu.SemaphoreType.DMA((SIDE * (s + 1) + SIDE * SIDE + s,)),
+            VMEM((2, SIDE * SIDE, groups, 192, 128), BF16),
+            VMEM((2 * groups, 192, 2048), BF16),
+            pltpu.SemaphoreType.DMA((2 * groups * (SIDE * SIDE * 4 + 1),)),
         ],
         nbytes=8 * MIB,
     )
@@ -209,10 +216,17 @@
         for a in "xy":
             near[a].append(named_move(near[a][0], a, i))
     got = {"x": [None] * 4, "y": [None] * 4}
+    ahead = {}
+    for a in "yx":
+        ahead[a] = expand(near[a][:1], heads[OTHER[a]][3])
+    for a in "yx":
+        ahead[a] = named_move(ahead[a], OTHER[a], 3)
     for i in (3, 1, 2, 0):
         for a in "xy":
-            piece = expand(near[a], heads[OTHER[a]][i], a)
-            got[a][i] = named_move(piece, OTHER[a], i) if i else piece
+            piece = expand(near[a][1:] if i == 3 else near[a], heads[OTHER[a]][i])
+            got[a][i] = [named_move(piece, OTHER[a], i) if i else piece]
+    for a in "xy":
+        got[a][3].insert(0, ahead[a])
     keys, values = join(got["x"], got["y"])
     return keys[None, None], values.reshape(1, -1, 1, 128)
 

time: 129 us -> 110 us (0.85)
  the two profiles are of different devices: /device:TPU:1 before, /device:TPU:14 now
where the time goes in v3:
time: 110 us; the launch traced here: 109 us
  waiting for transfers between devices  54.8 us (50%)
  starting transfers between devices  40.5 us (37%)
  Pallas kernels  13.2 us (12%)
    ppermute x20, waiting for transfers between devices, move(): return lax.ppermute(array, 'tp', pairs)  47.7 us
    ppermute x20, starting transfers between devices, move(): return lax.ppermute(array, 'tp', pairs)  31.8 us
    pallas_call x12, Pallas kernels, call(): pl.pallas_call(kernel, out_shape=outs, in_specs=in_specs or whole(len(arg...  13.2 us
    all_to_all x1, starting transfers between devices, shards(): mine = lax.all_to_all(rows, 'seq', split_axis=0, concat_axis=0, tiled=True)  8.71 us
    all_to_all x1, waiting for transfers between devices, shards(): mine = lax.all_to_all(rows, 'seq', split_axis=0, concat_axis=0, tiled=True)  7.07 us
  transfers between devices with their start and end apart: 21, of which 9 were waited for; matrix products, arithmetic and copies ran while one was open for 0% of the time, Pallas kernels for 4%

profile of v3, /device:TPU:14, one launch (start us, length us, event | category | flops | bytes accessed | tf_op | source)
XLA Modules:
  0.0 109.5 jit_solution(13238485003737139859)
XLA Ops:
  0.6 2.4 %shard_map.68 = (bf16[16,144,128]{2,1,0:T(8,128)(2,1)}, bf16[1024,128]{1,0:T(8,128)(2,1)}) custom-call(bf16[16,32,512]{2,1,0:T(8,128)(2,1)} %lat_in.1, bf16[16,32,64]{2,1,0:T(8,128)(2,1)} %rot_in.1, f32[1,512]{1,0:T(1,128)} %bitcast.7, bf16[512,128]{1,0:T(8,128)(2,1)} %bitcast.5, bf16[512,128]{1,0:T(8,128)(2,1)} %bitcast.6), custom_call_target="tpu_custom_call" | custom-call | bytes 1048576 | tf_op jit(solution)/shard_map/pallas_call | solution.py:43
  3.1 8.7 %all-to-all-start = ((bf16[16,144,128]{2,1,0:T(8,128)(2,1)}), bf16[16,144,128]{2,1,0:T(8,128)(2,1)S(1)}, u32[]{:S(2)}, u32[]{:S(2)}) async-start(bf16[16,144,128]{2,1,0:T(8,128)(2,1)} %get-tuple-element.8), calls=%async_computation | async-start | bytes 1179648 | tf_op jit(solution)/shard_map/all_to_all | solution.py:210
  11.8 0.9 collective-permute-start
  12.7 9.1 %collective-permute-done.refs_4_ = bf16[1024,128]{1,0:T(8,128)(2,1)S(1)} collective-permute-done((bf16[1024,128]{1,0:T(8,128)(2,1)}, bf16[1024,128]{1,0:T(8,128)(2,1)S(1)}, u32[]{:S(2)}, u32[]{:S(2)}) %collective-permute-start) | collective-permute-done | bytes 262176 | tf_op jit(solution)/shard_map/ppermute | solution.py:25
  21.9 7.1 %all-to-all-done = bf16[16,144,128]{2,1,0:T(8,128)(2,1)S(1)} async-done(((bf16[16,144,128]{2,1,0:T(8,128)(2,1)}), bf16[16,144,128]{2,1,0:T(8,128)(2,1)S(1)}, u32[]{:S(2)}, u32[]{:S(2)}) %all-to-all-start) | async-done | bytes 589856 | tf_op jit(solution)/shard_map/all_to_all | solution.py:210
  29.0 1.5 %collective-permute-start.3 = (bf16[8,144,128]{2,1,0:T(8,128)(2,1)S(1)}, bf16[8,144,128]{2,1,0:T(8,128)(2,1)S(1)}, u32[]{:S(2)}, u32[]{:S(2)}) collective-permute-start(bf16[8,144,128]{2,1,0:T(8,128)(2,1)S(1)} %get-tuple-element.15.refs_0_), channel_id=1, source_target_pairs={{0,2},{1,3},{2,0},{3,1},{4,6},{5,7},{6,4},{7,5},{8,10},{9,11},{10,... | collective-permute-start | bytes 884744 | tf_op jit(solution)/shard_map/ppermute | solution.py:25
  30.5 2.3 %collective-permute-start.8 = (bf16[1024,128]{1,0:T(8,128)(2,1)}, bf16[1024,128]{1,0:T(8,128)(2,1)S(1)}, u32[]{:S(2)}, u32[]{:S(2)}) collective-permute-start(bf16[1024,128]{1,0:T(8,128)(2,1)} %get-tuple-element.9.refs_4_), channel_id=1, source_target_pairs={{0,8},{1,9},{2,10},{3,11},{4,12},{5,13},{6,14},{7,15},{8,0},{9,1},... | collective-permute-start | bytes 786440 | tf_op jit(solution)/shard_map/ppermute | solution.py:25
  32.8 3.2 %collective-permute-start.1 = (bf16[8,144,128]{2,1,0:T(8,128)(2,1)S(1)}, bf16[8,144,128]{2,1,0:T(8,128)(2,1)S(1)}, u32[]{:S(2)}, u32[]{:S(2)}) collective-permute-start(bf16[8,144,128]{2,1,0:T(8,128)(2,1)S(1)} %get-tuple-element.15.refs_0_), channel_id=1, source_target_pairs={{0,1},{1,2},{2,3},{3,0},{4,5},{5,6},{6,7},{7,4},{8,9},{9,10},{10,1... | collective-permute-start | bytes 884744 | tf_op jit(solution)/shard_map/ppermute | solution.py:25
  36.0 0.9 collective-permute-start.17
  36.9 3.9 %collective-permute-done.8.refs_1_.refs_3_ = bf16[1024,128]{1,0:T(8,128)(2,1)S(1)} collective-permute-done((bf16[1024,128]{1,0:T(8,128)(2,1)}, bf16[1024,128]{1,0:T(8,128)(2,1)S(1)}, u32[]{:S(2)}, u32[]{:S(2)}) %collective-permute-start.8) | collective-permute-done | bytes 262176 | tf_op jit(solution)/shard_map/ppermute | solution.py:25
  40.8 2.3 %collective-permute-start.13 = (bf16[8,144,128]{2,1,0:T(8,128)(2,1)S(1)}, bf16[8,144,128]{2,1,0:T(8,128)(2,1)S(1)}, u32[]{:S(2)}, u32[]{:S(2)}) collective-permute-start(bf16[8,144,128]{2,1,0:T(8,128)(2,1)S(1)} %get-tuple-element.14.refs_0_), channel_id=1, source_target_pairs={{0,8},{1,9},{2,10},{3,11},{4,12},{5,13},{6,14},{7,15},{8,0},{9,1},... | collective-permute-start | bytes 884744 | tf_op jit(solution)/shard_map/ppermute | solution.py:25
  43.1 4.4 %collective-permute-done.2.refs_2_.refs_1_ = bf16[8,144,128]{2,1,0:T(8,128)(2,1)S(1)} collective-permute-done((bf16[8,144,128]{2,1,0:T(8,128)(2,1)S(1)}, bf16[8,144,128]{2,1,0:T(8,128)(2,1)S(1)}, u32[]{:S(2)}, u32[]{:S(2)}) %collective-permute-start.2) | collective-permute-done | bytes 294944 | tf_op jit(solution)/shard_map/ppermute | solution.py:25
  48.0 1.5 %collective-permute-start.11 = (bf16[8,144,128]{2,1,0:T(8,128)(2,1)S(1)}, bf16[8,144,128]{2,1,0:T(8,128)(2,1)S(1)}, u32[]{:S(2)}, u32[]{:S(2)}) collective-permute-start(bf16[8,144,128]{2,1,0:T(8,128)(2,1)S(1)} %get-tuple-element.14.refs_0_), channel_id=1, source_target_pairs={{0,4},{1,5},{2,6},{3,7},{4,8},{5,9},{6,10},{7,11},{8,12},{9,13},{1... | collective-permute-start | bytes 884744 | tf_op jit(solution)/shard_map/ppermute | solution.py:25
  50.0 1.6 %collective-permute-done.17.refs_1_.refs_3_ = bf16[1024,128]{1,0:T(8,128)(2,1)S(1)} collective-permute-done((bf16[1024,128]{1,0:T(8,128)(2,1)}, bf16[1024,128]{1,0:T(8,128)(2,1)S(1)}, u32[]{:S(2)}, u32[]{:S(2)}) %collective-permute-start.17) | collective-permute-done | bytes 262176 | tf_op jit(solution)/shard_map/ppermute | solution.py:25
  51.6 2.3 %collective-permute-start.10 = (bf16[3,2,320,128]{3,2,1,0:T(8,128)(2,1)S(1)}, bf16[3,2,320,128]{3,2,1,0:T(8,128)(2,1)S(1)}, u32[]{:S(2)}, u32[]{:S(2)}) collective-permute-start(bf16[3,2,320,128]{3,2,1,0:T(8,128)(2,1)S(1)} %shard_map.73), channel_id=1, source_target_pairs={{0,8},{1,9},{2,10},{3,11},{4,12},{5,13},{6,14},{7,15},{8,0},{9,1},... | collective-permute-start | bytes 1474568 | tf_op jit(solution)/shard_map/ppermute | solution.py:25
  53.9 4.1 %collective-permute-done.6.refs_4_ = bf16[1024,128]{1,0:T(8,128)(2,1)S(1)} collective-permute-done((bf16[1024,128]{1,0:T(8,128)(2,1)}, bf16[1024,128]{1,0:T(8,128)(2,1)S(1)}, u32[]{:S(2)}, u32[]{:S(2)}) %collective-permute-start.6) | collective-permute-done | bytes 262176 | tf_op jit(solution)/shard_map/ppermute | solution.py:25
  58.0 2.1 %collective-permute-start.15 = (bf16[1024,128]{1,0:T(8,128)(2,1)S(1)}, bf16[1024,128]{1,0:T(8,128)(2,1)S(1)}, u32[]{:S(2)}, u32[]{:S(2)}) collective-permute-start(bf16[1024,128]{1,0:T(8,128)(2,1)S(1)} %copy-done), channel_id=1, source_target_pairs={{0,1},{1,2},{2,3},{3,0},{4,5},{5,6},{6,7},{7,4},{8,9},{9,10},{10,1... | collective-permute-start | bytes 786440 | tf_op jit(solution)/shard_map/ppermute | solution.py:25
  60.7 10.2 %collective-permute-start.9 = (bf16[1,2,320,128]{3,2,1,0:T(8,128)(2,1)S(1)}, bf16[1,2,320,128]{3,2,1,0:T(8,128)(2,1)S(1)}, u32[]{:S(2)}, u32[]{:S(2)}) collective-permute-start(bf16[1,2,320,128]{3,2,1,0:T(8,128)(2,1)S(1)} %shard_map.72), channel_id=1, source_target_pairs={{0,8},{1,9},{2,10},{3,11},{4,12},{5,13},{6,14},{7,15},{8,0},{9,1},... | collective-permute-start | bytes 491528 | tf_op jit(solution)/shard_map/ppermute | solution.py:25
  72.6 2.0 %collective-permute-done.4.refs_4_ = bf16[1024,128]{1,0:T(8,128)(2,1)S(1)} collective-permute-done((bf16[1024,128]{1,0:T(8,128)(2,1)S(1)}, bf16[1024,128]{1,0:T(8,128)(2,1)S(1)}, u32[]{:S(2)}, u32[]{:S(2)}) %collective-permute-start.4) | collective-permute-done | bytes 262176 | tf_op jit(solution)/shard_map/ppermute | solution.py:25
  75.2 2.7 %collective-permute-done.9.refs_3_ = bf16[1,2,320,128]{3,2,1,0:T(8,128)(2,1)S(1)} collective-permute-done((bf16[1,2,320,128]{3,2,1,0:T(8,128)(2,1)S(1)}, bf16[1,2,320,128]{3,2,1,0:T(8,128)(2,1)S(1)}, u32[]{:S(2)}, u32[]{:S(2)}) %collective-permute-start.9) | collective-permute-done | bytes 163872 | tf_op jit(solution)/shard_map/ppermute | solution.py:25
  77.9 1.6 %collective-permute-start.5 = (bf16[4,2,320,128]{3,2,1,0:T(8,128)(2,1)S(1)}, bf16[4,2,320,128]{3,2,1,0:T(8,128)(2,1)S(1)}, u32[]{:S(2)}, u32[]{:S(2)}) collective-permute-start(bf16[4,2,320,128]{3,2,1,0:T(8,128)(2,1)S(1)} %shard_map.70), channel_id=1, source_target_pairs={{0,4},{1,5},{2,6},{3,7},{4,8},{5,9},{6,10},{7,11},{8,12},{9,13},{1... | collective-permute-start | bytes 1966088 | tf_op jit(solution)/shard_map/ppermute | solution.py:25
  80.4 1.9 %collective-permute-start.19 = (bf16[3,2,320,128]{3,2,1,0:T(8,128)(2,1)S(1)}, bf16[3,2,320,128]{3,2,1,0:T(8,128)(2,1)S(1)}, u32[]{:S(2)}, u32[]{:S(2)}) collective-permute-start(bf16[3,2,320,128]{3,2,1,0:T(8,128)(2,1)S(1)} %shard_map.78), channel_id=1, source_target_pairs={{0,2},{1,3},{2,0},{3,1},{4,6},{5,7},{6,4},{7,5},{8,10},{9,11},{10,... | collective-permute-start | bytes 1474568 | tf_op jit(solution)/shard_map/ppermute | solution.py:25
  83.4 19.9 %collective-permute-done.19.refs_9_ = bf16[3,2,320,128]{3,2,1,0:T(8,128)(2,1)S(1)} collective-permute-done((bf16[3,2,320,128]{3,2,1,0:T(8,128)(2,1)S(1)}, bf16[3,2,320,128]{3,2,1,0:T(8,128)(2,1)S(1)}, u32[]{:S(2)}, u32[]{:S(2)}) %collective-permute-start.19) | collective-permute-done | bytes 491552 | tf_op jit(solution)/shard_map/ppermute | solution.py:25
  103.3 6.0 %shard_map.79 = (bf16[192,8192]{1,0:T(8,128)(2,1)}, bf16[16,4,128,128]{3,2,1,0:T(8,128)(2,1)}) custom-call(bf16[4,2,320,128]{3,2,1,0:T(8,128)(2,1)S(1)} %shard_map.69.refs_0_, bf16[4,2,320,128]{3,2,1,0:T(8,128)(2,1)S(1)} %collective-permute-done.5.refs_1_, bf16[4,2,320,128]{3,2,1,0:T(8,128)(2,1)S(1)} %collective-permute-done.7.refs_2_, ...), custom_call_target="tpu_custom_call" | custom-call | bytes 8388608 | tf_op jit(solution)/shard_map/pallas_call | solution.py:43
  (33 shorter events, 5.9 us)
Async XLA Ops:
  3.1 54.9 %copy-start = (bf16[1024,128]{1,0:T(8,128)(2,1)S(1)}, bf16[1024,128]{1,0:T(8,128)(2,1)}, u32[]{:S(2)}) copy-start(bf16[1024,128]{1,0:T(8,128)(2,1)} %get-tuple-element.9.refs_4_) | copy-start | bytes 786436
  3.1 25.8 %all-to-all-start = ((bf16[16,144,128]{2,1,0:T(8,128)(2,1)}), bf16[16,144,128]{2,1,0:T(8,128)(2,1)S(1)}, u32[]{:S(2)}, u32[]{:S(2)}) async-start(bf16[16,144,128]{2,1,0:T(8,128)(2,1)} %get-tuple-element.8), calls=%async_computation | async-start | bytes 1179648 | tf_op jit(solution)/shard_map/all_to_all | solution.py:210
  11.8 10.0 %collective-permute-start = (bf16[1024,128]{1,0:T(8,128)(2,1)}, bf16[1024,128]{1,0:T(8,128)(2,1)S(1)}, u32[]{:S(2)}, u32[]{:S(2)}) collective-permute-start(bf16[1024,128]{1,0:T(8,128)(2,1)} %get-tuple-element.9.refs_4_), channel_id=1, source_target_pairs={{0,3},{1,0},{2,1},{3,2},{4,7},{5,4},{6,5},{7,6},{8,11},{9,8},{10,9... | collective-permute-start | bytes 786440 | tf_op jit(solution)/shard_map/ppermute | solution.py:25
  29.0 14.1 %collective-permute-start.3 = (bf16[8,144,128]{2,1,0:T(8,128)(2,1)S(1)}, bf16[8,144,128]{2,1,0:T(8,128)(2,1)S(1)}, u32[]{:S(2)}, u32[]{:S(2)}) collective-permute-start(bf16[8,144,128]{2,1,0:T(8,128)(2,1)S(1)} %get-tuple-element.15.refs_0_), channel_id=1, source_target_pairs={{0,2},{1,3},{2,0},{3,1},{4,6},{5,7},{6,4},{7,5},{8,10},{9,11},{10,... | collective-permute-start | bytes 884744 | tf_op jit(solution)/shard_map/ppermute | solution.py:25
  30.5 10.3 %collective-permute-start.8 = (bf16[1024,128]{1,0:T(8,128)(2,1)}, bf16[1024,128]{1,0:T(8,128)(2,1)S(1)}, u32[]{:S(2)}, u32[]{:S(2)}) collective-permute-start(bf16[1024,128]{1,0:T(8,128)(2,1)} %get-tuple-element.9.refs_4_), channel_id=1, source_target_pairs={{0,8},{1,9},{2,10},{3,11},{4,12},{5,13},{6,14},{7,15},{8,0},{9,1},... | collective-permute-start | bytes 786440 | tf_op jit(solution)/shard_map/ppermute | solution.py:25
  32.8 14.8 %collective-permute-start.2 = (bf16[8,144,128]{2,1,0:T(8,128)(2,1)S(1)}, bf16[8,144,128]{2,1,0:T(8,128)(2,1)S(1)}, u32[]{:S(2)}, u32[]{:S(2)}) collective-permute-start(bf16[8,144,128]{2,1,0:T(8,128)(2,1)S(1)} %get-tuple-element.15.refs_0_), channel_id=1, source_target_pairs={{0,3},{1,0},{2,1},{3,2},{4,7},{5,4},{6,5},{7,6},{8,11},{9,8},{10,9... | collective-permute-start | bytes 884744 | tf_op jit(solution)/shard_map/ppermute | solution.py:25
  32.8 15.3 %collective-permute-start.1 = (bf16[8,144,128]{2,1,0:T(8,128)(2,1)S(1)}, bf16[8,144,128]{2,1,0:T(8,128)(2,1)S(1)}, u32[]{:S(2)}, u32[]{:S(2)}) collective-permute-start(bf16[8,144,128]{2,1,0:T(8,128)(2,1)S(1)} %get-tuple-element.15.refs_0_), channel_id=1, source_target_pairs={{0,1},{1,2},{2,3},{3,0},{4,5},{5,6},{6,7},{7,4},{8,9},{9,10},{10,1... | collective-permute-start | bytes 884744 | tf_op jit(solution)/shard_map/ppermute | solution.py:25
  36.0 15.6 %collective-permute-start.17 = (bf16[1024,128]{1,0:T(8,128)(2,1)}, bf16[1024,128]{1,0:T(8,128)(2,1)S(1)}, u32[]{:S(2)}, u32[]{:S(2)}) collective-permute-start(bf16[1024,128]{1,0:T(8,128)(2,1)} %get-tuple-element.9.refs_4_), channel_id=1, source_target_pairs={{0,2},{1,3},{2,0},{3,1},{4,6},{5,7},{6,4},{7,5},{8,10},{9,11},{10,... | collective-permute-start | bytes 786440 | tf_op jit(solution)/shard_map/ppermute | solution.py:25
  40.8 19.3 %collective-permute-start.13 = (bf16[8,144,128]{2,1,0:T(8,128)(2,1)S(1)}, bf16[8,144,128]{2,1,0:T(8,128)(2,1)S(1)}, u32[]{:S(2)}, u32[]{:S(2)}) collective-permute-start(bf16[8,144,128]{2,1,0:T(8,128)(2,1)S(1)} %get-tuple-element.14.refs_0_), channel_id=1, source_target_pairs={{0,8},{1,9},{2,10},{3,11},{4,12},{5,13},{6,14},{7,15},{8,0},{9,1},... | collective-permute-start | bytes 884744 | tf_op jit(solution)/shard_map/ppermute | solution.py:25
  43.1 14.9 %collective-permute-start.6 = (bf16[1024,128]{1,0:T(8,128)(2,1)}, bf16[1024,128]{1,0:T(8,128)(2,1)S(1)}, u32[]{:S(2)}, u32[]{:S(2)}) collective-permute-start(bf16[1024,128]{1,0:T(8,128)(2,1)} %get-tuple-element.9.refs_4_), channel_id=1, source_target_pairs={{0,4},{1,5},{2,6},{3,7},{4,8},{5,9},{6,10},{7,11},{8,12},{9,13},{1... | collective-permute-start | bytes 786440 | tf_op jit(solution)/shard_map/ppermute | solution.py:25
  47.5 13.2 %collective-permute-start.12 = (bf16[8,144,128]{2,1,0:T(8,128)(2,1)S(1)}, bf16[8,144,128]{2,1,0:T(8,128)(2,1)S(1)}, u32[]{:S(2)}, u32[]{:S(2)}) collective-permute-start(bf16[8,144,128]{2,1,0:T(8,128)(2,1)S(1)} %get-tuple-element.14.refs_0_), channel_id=1, source_target_pairs={{0,12},{1,13},{2,14},{3,15},{4,0},{5,1},{6,2},{7,3},{8,4},{9,5},{1... | collective-permute-start | bytes 884744 | tf_op jit(solution)/shard_map/ppermute | solution.py:25
  48.0 22.8 %collective-permute-start.11 = (bf16[8,144,128]{2,1,0:T(8,128)(2,1)S(1)}, bf16[8,144,128]{2,1,0:T(8,128)(2,1)S(1)}, u32[]{:S(2)}, u32[]{:S(2)}) collective-permute-start(bf16[8,144,128]{2,1,0:T(8,128)(2,1)S(1)} %get-tuple-element.14.refs_0_), channel_id=1, source_target_pairs={{0,4},{1,5},{2,6},{3,7},{4,8},{5,9},{6,10},{7,11},{8,12},{9,13},{1... | collective-permute-start | bytes 884744 | tf_op jit(solution)/shard_map/ppermute | solution.py:25
  51.6 28.8 %collective-permute-start.10 = (bf16[3,2,320,128]{3,2,1,0:T(8,128)(2,1)S(1)}, bf16[3,2,320,128]{3,2,1,0:T(8,128)(2,1)S(1)}, u32[]{:S(2)}, u32[]{:S(2)}) collective-permute-start(bf16[3,2,320,128]{3,2,1,0:T(8,128)(2,1)S(1)} %shard_map.73), channel_id=1, source_target_pairs={{0,8},{1,9},{2,10},{3,11},{4,12},{5,13},{6,14},{7,15},{8,0},{9,1},... | collective-permute-start | bytes 1474568 | tf_op jit(solution)/shard_map/ppermute | solution.py:25
  58.0 14.0 %collective-permute-start.15 = (bf16[1024,128]{1,0:T(8,128)(2,1)S(1)}, bf16[1024,128]{1,0:T(8,128)(2,1)S(1)}, u32[]{:S(2)}, u32[]{:S(2)}) collective-permute-start(bf16[1024,128]{1,0:T(8,128)(2,1)S(1)} %copy-done), channel_id=1, source_target_pairs={{0,1},{1,2},{2,3},{3,0},{4,5},{5,6},{6,7},{7,4},{8,9},{9,10},{10,1... | collective-permute-start | bytes 786440 | tf_op jit(solution)/shard_map/ppermute | solution.py:25
  60.1 14.5 %collective-permute-start.4 = (bf16[1024,128]{1,0:T(8,128)(2,1)S(1)}, bf16[1024,128]{1,0:T(8,128)(2,1)S(1)}, u32[]{:S(2)}, u32[]{:S(2)}) collective-permute-start(bf16[1024,128]{1,0:T(8,128)(2,1)S(1)} %copy-done), channel_id=1, source_target_pairs={{0,12},{1,13},{2,14},{3,15},{4,0},{5,1},{6,2},{7,3},{8,4},{9,5},{1... | collective-permute-start | bytes 786440 | tf_op jit(solution)/shard_map/ppermute | solution.py:25
  60.7 17.2 %collective-permute-start.9 = (bf16[1,2,320,128]{3,2,1,0:T(8,128)(2,1)S(1)}, bf16[1,2,320,128]{3,2,1,0:T(8,128)(2,1)S(1)}, u32[]{:S(2)}, u32[]{:S(2)}) collective-permute-start(bf16[1,2,320,128]{3,2,1,0:T(8,128)(2,1)S(1)} %shard_map.72), channel_id=1, source_target_pairs={{0,8},{1,9},{2,10},{3,11},{4,12},{5,13},{6,14},{7,15},{8,0},{9,1},... | collective-permute-start | bytes 491528 | tf_op jit(solution)/shard_map/ppermute | solution.py:25
  70.9 8.6 %collective-permute-start.18 = (bf16[1,2,320,128]{3,2,1,0:T(8,128)(2,1)S(1)}, bf16[1,2,320,128]{3,2,1,0:T(8,128)(2,1)S(1)}, u32[]{:S(2)}, u32[]{:S(2)}) collective-permute-start(bf16[1,2,320,128]{3,2,1,0:T(8,128)(2,1)S(1)} %shard_map.77), channel_id=1, source_target_pairs={{0,2},{1,3},{2,0},{3,1},{4,6},{5,7},{6,4},{7,5},{8,10},{9,11},{10,... | collective-permute-start | bytes 491528 | tf_op jit(solution)/shard_map/ppermute | solution.py:25
  71.9 31.3 %collective-permute-start.14 = (bf16[4,2,320,128]{3,2,1,0:T(8,128)(2,1)S(1)}, bf16[4,2,320,128]{3,2,1,0:T(8,128)(2,1)S(1)}, u32[]{:S(2)}, u32[]{:S(2)}) collective-permute-start(bf16[4,2,320,128]{3,2,1,0:T(8,128)(2,1)S(1)} %shard_map.75), channel_id=1, source_target_pairs={{0,1},{1,2},{2,3},{3,0},{4,5},{5,6},{6,7},{7,4},{8,9},{9,10},{10,1... | collective-permute-start | bytes 1966088 | tf_op jit(solution)/shard_map/ppermute | solution.py:25
  74.6 28.7 %collective-permute-start.16 = (bf16[4,2,320,128]{3,2,1,0:T(8,128)(2,1)S(1)}, bf16[4,2,320,128]{3,2,1,0:T(8,128)(2,1)S(1)}, u32[]{:S(2)}, u32[]{:S(2)}) collective-permute-start(bf16[4,2,320,128]{3,2,1,0:T(8,128)(2,1)S(1)} %shard_map.76), channel_id=1, source_target_pairs={{0,3},{1,0},{2,1},{3,2},{4,7},{5,4},{6,5},{7,6},{8,11},{9,8},{10,9... | collective-permute-start | bytes 1966088 | tf_op jit(solution)/shard_map/ppermute | solution.py:25
  77.9 25.3 %collective-permute-start.5 = (bf16[4,2,320,128]{3,2,1,0:T(8,128)(2,1)S(1)}, bf16[4,2,320,128]{3,2,1,0:T(8,128)(2,1)S(1)}, u32[]{:S(2)}, u32[]{:S(2)}) collective-permute-start(bf16[4,2,320,128]{3,2,1,0:T(8,128)(2,1)S(1)} %shard_map.70), channel_id=1, source_target_pairs={{0,4},{1,5},{2,6},{3,7},{4,8},{5,9},{6,10},{7,11},{8,12},{9,13},{1... | collective-permute-start | bytes 1966088 | tf_op jit(solution)/shard_map/ppermute | solution.py:25
  79.5 23.8 %collective-permute-start.7 = (bf16[4,2,320,128]{3,2,1,0:T(8,128)(2,1)S(1)}, bf16[4,2,320,128]{3,2,1,0:T(8,128)(2,1)S(1)}, u32[]{:S(2)}, u32[]{:S(2)}) collective-permute-start(bf16[4,2,320,128]{3,2,1,0:T(8,128)(2,1)S(1)} %shard_map.71), channel_id=1, source_target_pairs={{0,12},{1,13},{2,14},{3,15},{4,0},{5,1},{6,2},{7,3},{8,4},{9,5},{1... | collective-permute-start | bytes 1966088 | tf_op jit(solution)/shard_map/ppermute | solution.py:25
  80.4 22.9 %collective-permute-start.19 = (bf16[3,2,320,128]{3,2,1,0:T(8,128)(2,1)S(1)}, bf16[3,2,320,128]{3,2,1,0:T(8,128)(2,1)S(1)}, u32[]{:S(2)}, u32[]{:S(2)}) collective-permute-start(bf16[3,2,320,128]{3,2,1,0:T(8,128)(2,1)S(1)} %shard_map.78), channel_id=1, source_target_pairs={{0,2},{1,3},{2,0},{3,1},{4,6},{5,7},{6,4},{7,5},{8,10},{9,11},{10,... | collective-permute-start | bytes 1474568 | tf_op jit(solution)/shard_map/ppermute | solution.py:25

commit v4 on v3

--- a/solution.py
+++ b/solution.py
@@ -123,17 +123,17 @@
                 [four[:, 32 * j : 32 * j + 32].reshape(128, 128) for j in range(4)], axis=-1
             )
             wide = jnp.dot(lhs, w, preferred_element_type=jnp.float32).astype(BF16)
-            out[i, g, 0:128] = wide[:, 0:128].T
-            for d, turned in enumerate(regroup([four[k, 128:144] for k in range(4)])):
-                out[i, g, 128 + 16 * d : 144 + 16 * d] = turned
-            out[i, g, 192:320] = wide[:, 128:256]
+            out[i, g, 0:4] = wide[:, 0:128].T.reshape(4, 32, 128)
+            turned = jnp.concatenate(regroup([four[k, 128:144] for k in range(4)]), axis=0)
+            out[i, g, 4:6] = turned.reshape(2, 32, 128)
+            out[i, g, 6:10] = wide[:, 128:256].reshape(4, 32, 128)
 
 
 def expand(rows, head):
     n, s = len(rows), rows[0].shape[0]
     return call(
         functools.partial(expand_kernel, n),
-        shape(n, s // 4, 320, 128),
+        shape(n, s // 4, 10, 32, 128),
         (*rows, head),
         limit=4 * MIB,
         flops=n * s * 32 * 512 * 256 * 2,
@@ -161,17 +161,14 @@
                 place = {outer: sender(outer, HOPS[o]), inner: sender(inner, HOPS[n])}
                 rows = pl.ds(pl.multiple_of(place["x"] * 32, 32), 32)
                 for g in range(groups):
-                    for k in range(4):
-                        copy(
-                            sources[o][n].at[g, 192 + 32 * k : 224 + 32 * k],
-                            values.at[(h * groups + g) * 4 + k, place["y"], rows],
-                        )
+                    to = (h * groups + g) * 4
+                    copy(sources[o][n].at[g, 6:10], values.at[to : to + 4, place["y"], rows])
         for o in range(4):
             for n in range(4):
                 place = {outer: sender(outer, HOPS[o]), inner: sender(inner, HOPS[n])}
                 slot = place["y"] * SIDE + place["x"]
                 for g in range(groups):
-                    sorted_[h, slot, g] = sources[o][n][g, 0:192]
+                    sorted_[h, slot, g] = sources[o][n][g, 0:6].reshape(192, 128)
         for g in range(groups):
             for y in range(SIDE):
                 parts = [sorted_[h, y * SIDE + x, g] for x in range(SIDE)]
@@ -195,7 +192,7 @@
         scratch=[
             VMEM((2, SIDE * SIDE, groups, 192, 128), BF16),
             VMEM((2 * groups, 192, 2048), BF16),
-            pltpu.SemaphoreType.DMA((2 * groups * (SIDE * SIDE * 4 + 1),)),
+            pltpu.SemaphoreType.DMA((2 * groups * (SIDE * SIDE + 1),)),
         ],
         nbytes=8 * MIB,
     )
@@ -216,17 +213,15 @@
         for a in "xy":
             near[a].append(named_move(near[a][0], a, i))
     got = {"x": [None] * 4, "y": [None] * 4}
-    ahead = {}
-    for a in "yx":
-        ahead[a] = expand(near[a][:1], heads[OTHER[a]][3])
-    for a in "yx":
-        ahead[a] = named_move(ahead[a], OTHER[a], 3)
+    ahead = {"x": [None] * 4, "y": [None] * 4}
+    for i in (3, 1, 2):
+        for a in "yx":
+            ahead[a][i] = expand(near[a][:1], heads[OTHER[a]][i])
+            ahead[a][i] = named_move(ahead[a][i], OTHER[a], i)
     for i in (3, 1, 2, 0):
-        for a in "xy":
-            piece = expand(near[a][1:] if i == 3 else near[a], heads[OTHER[a]][i])
-            got[a][i] = [named_move(piece, OTHER[a], i) if i else piece]
-    for a in "xy":
-        got[a][3].insert(0, ahead[a])
+        for a in "yx":
+            piece = expand(near[a][1:] if i else near[a], heads[OTHER[a]][i])
+            got[a][i] = [ahead[a][i], named_move(piece, OTHER[a], i)] if i else [piece]
     keys, values = join(got["x"], got["y"])
     return keys[None, None], values.reshape(1, -1, 1, 128)
 

time: 110 us -> 122 us (1.11)
  the two profiles are of different devices: /device:TPU:14 before, /device:TPU:1 now
where the time goes in v4:
time: 122 us; the launch traced here: 121 us
  waiting for transfers between devices  65.8 us (54%)
  starting transfers between devices  42 us (34%)
  Pallas kernels  12.3 us (10%)
    ppermute x24, waiting for transfers between devices, move(): return lax.ppermute(array, 'tp', pairs)  55.6 us
    ppermute x24, starting transfers between devices, move(): return lax.ppermute(array, 'tp', pairs)  32 us
    pallas_call x16, Pallas kernels, call(): pl.pallas_call(kernel, out_shape=outs, in_specs=in_specs or whole(len(arg...  12.3 us
    all_to_all x1, waiting for transfers between devices, shards(): mine = lax.all_to_all(rows, 'seq', split_axis=0, concat_axis=0, tiled=True)  10.3 us
    all_to_all x1, starting transfers between devices, shards(): mine = lax.all_to_all(rows, 'seq', split_axis=0, concat_axis=0, tiled=True)  9.98 us
  transfers between devices with their start and end apart: 25, of which 14 were waited for; matrix products, arithmetic and copies ran while one was open for 0% of the time, Pallas kernels for 5%

profile of v4, /device:TPU:1, one launch (start us, length us, event | category | flops | bytes accessed | tf_op | source)
XLA Modules:
  0.0 121.0 jit_solution(1966827450755718628)
XLA Ops:
  0.6 2.4 %shard_map.68 = (bf16[16,144,128]{2,1,0:T(8,128)(2,1)}, bf16[1024,128]{1,0:T(8,128)(2,1)}) custom-call(bf16[16,32,512]{2,1,0:T(8,128)(2,1)} %lat_in.1, bf16[16,32,64]{2,1,0:T(8,128)(2,1)} %rot_in.1, f32[1,512]{1,0:T(1,128)} %bitcast.7, bf16[512,128]{1,0:T(8,128)(2,1)} %bitcast.5, bf16[512,128]{1,0:T(8,128)(2,1)} %bitcast.6), custom_call_target="tpu_custom_call" | custom-call | bytes 1048576 | tf_op jit(solution)/shard_map/pallas_call | solution.py:43
  3.1 10.0 %all-to-all-start = ((bf16[16,144,128]{2,1,0:T(8,128)(2,1)}), bf16[16,144,128]{2,1,0:T(8,128)(2,1)S(1)}, u32[]{:S(2)}, u32[]{:S(2)}) async-start(bf16[16,144,128]{2,1,0:T(8,128)(2,1)} %get-tuple-element.8), calls=%async_computation | async-start | bytes 1179648 | tf_op jit(solution)/shard_map/all_to_all | solution.py:207
  13.1 2.5 %collective-permute-start = (bf16[1024,128]{1,0:T(8,128)(2,1)}, bf16[1024,128]{1,0:T(8,128)(2,1)S(1)}, u32[]{:S(2)}, u32[]{:S(2)}) collective-permute-start(bf16[1024,128]{1,0:T(8,128)(2,1)} %get-tuple-element.9.refs_4_), channel_id=1, source_target_pairs={{0,3},{1,0},{2,1},{3,2},{4,7},{5,4},{6,5},{7,6},{8,11},{9,8},{10,9... | collective-permute-start | bytes 786440 | tf_op jit(solution)/shard_map/ppermute | solution.py:25
  15.5 5.8 %collective-permute-done.refs_1_.refs_3_ = bf16[1024,128]{1,0:T(8,128)(2,1)S(1)} collective-permute-done((bf16[1024,128]{1,0:T(8,128)(2,1)}, bf16[1024,128]{1,0:T(8,128)(2,1)S(1)}, u32[]{:S(2)}, u32[]{:S(2)}) %collective-permute-start) | collective-permute-done | bytes 262176 | tf_op jit(solution)/shard_map/ppermute | solution.py:25
  21.3 10.3 %all-to-all-done = bf16[16,144,128]{2,1,0:T(8,128)(2,1)S(1)} async-done(((bf16[16,144,128]{2,1,0:T(8,128)(2,1)}), bf16[16,144,128]{2,1,0:T(8,128)(2,1)S(1)}, u32[]{:S(2)}, u32[]{:S(2)}) %all-to-all-start) | async-done | bytes 589856 | tf_op jit(solution)/shard_map/all_to_all | solution.py:207
  31.6 2.8 %collective-permute-start.3 = (bf16[8,144,128]{2,1,0:T(8,128)(2,1)S(1)}, bf16[8,144,128]{2,1,0:T(8,128)(2,1)S(1)}, u32[]{:S(2)}, u32[]{:S(2)}) collective-permute-start(bf16[8,144,128]{2,1,0:T(8,128)(2,1)S(1)} %get-tuple-element.15.refs_0_), channel_id=1, source_target_pairs={{0,2},{1,3},{2,0},{3,1},{4,6},{5,7},{6,4},{7,5},{8,10},{9,11},{10,... | collective-permute-start | bytes 884744 | tf_op jit(solution)/shard_map/ppermute | solution.py:25
  35.3 2.7 %collective-permute-start.4 = (bf16[1024,128]{1,0:T(8,128)(2,1)}, bf16[1024,128]{1,0:T(8,128)(2,1)S(1)}, u32[]{:S(2)}, u32[]{:S(2)}) collective-permute-start(bf16[1024,128]{1,0:T(8,128)(2,1)} %get-tuple-element.9.refs_4_), channel_id=1, source_target_pairs={{0,12},{1,13},{2,14},{3,15},{4,0},{5,1},{6,2},{7,3},{8,4},{9,5},{1... | collective-permute-start | bytes 786440 | tf_op jit(solution)/shard_map/ppermute | solution.py:25
  39.3 4.9 %collective-permute-done.4.refs_1_.refs_3_ = bf16[1024,128]{1,0:T(8,128)(2,1)S(1)} collective-permute-done((bf16[1024,128]{1,0:T(8,128)(2,1)}, bf16[1024,128]{1,0:T(8,128)(2,1)S(1)}, u32[]{:S(2)}, u32[]{:S(2)}) %collective-permute-start.4) | collective-permute-done | bytes 262176 | tf_op jit(solution)/shard_map/ppermute | solution.py:25
  44.8 2.3 %collective-permute-start.10 = (bf16[1024,128]{1,0:T(8,128)(2,1)}, bf16[1024,128]{1,0:T(8,128)(2,1)S(1)}, u32[]{:S(2)}, u32[]{:S(2)}) collective-permute-start(bf16[1024,128]{1,0:T(8,128)(2,1)} %get-tuple-element.9.refs_4_), channel_id=1, source_target_pairs={{0,8},{1,9},{2,10},{3,11},{4,12},{5,13},{6,14},{7,15},{8,0},{9,1},... | collective-permute-start | bytes 786440 | tf_op jit(solution)/shard_map/ppermute | solution.py:25
  47.1 1.6 %collective-permute-done.2.refs_2_.refs_1_ = bf16[8,144,128]{2,1,0:T(8,128)(2,1)S(1)} collective-permute-done((bf16[8,144,128]{2,1,0:T(8,128)(2,1)S(1)}, bf16[8,144,128]{2,1,0:T(8,128)(2,1)S(1)}, u32[]{:S(2)}, u32[]{:S(2)}) %collective-permute-start.2) | collective-permute-done | bytes 294944 | tf_op jit(solution)/shard_map/ppermute | solution.py:25
  50.3 3.6 %collective-permute-done.1.refs_1_.refs_0_ = bf16[8,144,128]{2,1,0:T(8,128)(2,1)S(1)} collective-permute-done((bf16[8,144,128]{2,1,0:T(8,128)(2,1)S(1)}, bf16[8,144,128]{2,1,0:T(8,128)(2,1)S(1)}, u32[]{:S(2)}, u32[]{:S(2)}) %collective-permute-start.1) | collective-permute-done | bytes 294944 | tf_op jit(solution)/shard_map/ppermute | solution.py:25
  55.2 4.4 %collective-permute-done.18.refs_1_.refs_3_ = bf16[1024,128]{1,0:T(8,128)(2,1)S(1)} collective-permute-done((bf16[1024,128]{1,0:T(8,128)(2,1)}, bf16[1024,128]{1,0:T(8,128)(2,1)S(1)}, u32[]{:S(2)}, u32[]{:S(2)}) %collective-permute-start.18) | collective-permute-done | bytes 262176 | tf_op jit(solution)/shard_map/ppermute | solution.py:25
  59.7 2.2 %collective-permute-start.15 = (bf16[8,144,128]{2,1,0:T(8,128)(2,1)S(1)}, bf16[8,144,128]{2,1,0:T(8,128)(2,1)S(1)}, u32[]{:S(2)}, u32[]{:S(2)}) collective-permute-start(bf16[8,144,128]{2,1,0:T(8,128)(2,1)S(1)} %get-tuple-element.14.refs_0_), channel_id=1, source_target_pairs={{0,8},{1,9},{2,10},{3,11},{4,12},{5,13},{6,14},{7,15},{8,0},{9,1},... | collective-permute-start | bytes 884744 | tf_op jit(solution)/shard_map/ppermute | solution.py:25
  64.0 1.9 %collective-permute-start.8 = (bf16[1,2,10,32,128]{4,3,2,1,0:T(8,128)(2,1)S(1)}, bf16[1,2,10,32,128]{4,3,2,1,0:T(8,128)(2,1)S(1)}, u32[]{:S(2)}, u32[]{:S(2)}) collective-permute-start(bf16[1,2,10,32,128]{4,3,2,1,0:T(8,128)(2,1)S(1)} %shard_map.72), channel_id=1, source_target_pairs={{0,12},{1,13},{2,14},{3,15},{4,0},{5,1},{6,2},{7,3},{8,4},{9,5},{1... | collective-permute-start | bytes 491528 | tf_op jit(solution)/shard_map/ppermute | solution.py:25
  67.2 11.6 %collective-permute-done.8.refs_3_ = bf16[1,2,10,32,128]{4,3,2,1,0:T(8,128)(2,1)S(1)} collective-permute-done((bf16[1,2,10,32,128]{4,3,2,1,0:T(8,128)(2,1)S(1)}, bf16[1,2,10,32,128]{4,3,2,1,0:T(8,128)(2,1)S(1)}, u32[]{:S(2)}, u32[]{:S(2)}) %collective-permute-start.8) | collective-permute-done | bytes 163872 | tf_op jit(solution)/shard_map/ppermute | solution.py:25
  78.7 1.7 %collective-permute-start.11 = (bf16[1,2,10,32,128]{4,3,2,1,0:T(8,128)(2,1)S(1)}, bf16[1,2,10,32,128]{4,3,2,1,0:T(8,128)(2,1)S(1)}, u32[]{:S(2)}, u32[]{:S(2)}) collective-permute-start(bf16[1,2,10,32,128]{4,3,2,1,0:T(8,128)(2,1)S(1)} %shard_map.74), channel_id=1, source_target_pairs={{0,8},{1,9},{2,10},{3,11},{4,12},{5,13},{6,14},{7,15},{8,0},{9,1},... | collective-permute-start | bytes 491528 | tf_op jit(solution)/shard_map/ppermute | solution.py:25
  80.4 2.2 %collective-permute-start.16 = (bf16[1,2,10,32,128]{4,3,2,1,0:T(8,128)(2,1)S(1)}, bf16[1,2,10,32,128]{4,3,2,1,0:T(8,128)(2,1)S(1)}, u32[]{:S(2)}, u32[]{:S(2)}) collective-permute-start(bf16[1,2,10,32,128]{4,3,2,1,0:T(8,128)(2,1)S(1)} %shard_map.77), channel_id=1, source_target_pairs={{0,1},{1,2},{2,3},{3,0},{4,5},{5,6},{6,7},{7,4},{8,9},{9,10},{10,1... | collective-permute-start | bytes 491528 | tf_op jit(solution)/shard_map/ppermute | solution.py:25
  83.1 4.8 %collective-permute-done.13.refs_1_.refs_0_ = bf16[8,144,128]{2,1,0:T(8,128)(2,1)S(1)} collective-permute-done((bf16[8,144,128]{2,1,0:T(8,128)(2,1)S(1)}, bf16[8,144,128]{2,1,0:T(8,128)(2,1)S(1)}, u32[]{:S(2)}, u32[]{:S(2)}) %collective-permute-start.13) | collective-permute-done | bytes 294944 | tf_op jit(solution)/shard_map/ppermute | solution.py:25
  90.5 2.5 %collective-permute-start.12 = (bf16[3,2,10,32,128]{4,3,2,1,0:T(8,128)(2,1)S(1)}, bf16[3,2,10,32,128]{4,3,2,1,0:T(8,128)(2,1)S(1)}, u32[]{:S(2)}, u32[]{:S(2)}) collective-permute-start(bf16[3,2,10,32,128]{4,3,2,1,0:T(8,128)(2,1)S(1)} %shard_map.75), channel_id=1, source_target_pairs={{0,8},{1,9},{2,10},{3,11},{4,12},{5,13},{6,14},{7,15},{8,0},{9,1},... | collective-permute-start | bytes 1474568 | tf_op jit(solution)/shard_map/ppermute | solution.py:25
  93.0 2.2 %collective-permute-start.17 = (bf16[3,2,10,32,128]{4,3,2,1,0:T(8,128)(2,1)S(1)}, bf16[3,2,10,32,128]{4,3,2,1,0:T(8,128)(2,1)S(1)}, u32[]{:S(2)}, u32[]{:S(2)}) collective-permute-start(bf16[3,2,10,32,128]{4,3,2,1,0:T(8,128)(2,1)S(1)} %shard_map.78), channel_id=1, source_target_pairs={{0,1},{1,2},{2,3},{3,0},{4,5},{5,6},{6,7},{7,4},{8,9},{9,10},{10,1... | collective-permute-start | bytes 1474568 | tf_op jit(solution)/shard_map/ppermute | solution.py:25
  98.1 4.2 %collective-permute-done.9.refs_4_ = bf16[3,2,10,32,128]{4,3,2,1,0:T(8,128)(2,1)S(1)} collective-permute-done((bf16[3,2,10,32,128]{4,3,2,1,0:T(8,128)(2,1)S(1)}, bf16[3,2,10,32,128]{4,3,2,1,0:T(8,128)(2,1)S(1)}, u32[]{:S(2)}, u32[]{:S(2)}) %collective-permute-start.9) | collective-permute-done | bytes 491552 | tf_op jit(solution)/shard_map/ppermute | solution.py:25
  102.3 1.6 %collective-permute-done.12.refs_6_ = bf16[3,2,10,32,128]{4,3,2,1,0:T(8,128)(2,1)S(1)} collective-permute-done((bf16[3,2,10,32,128]{4,3,2,1,0:T(8,128)(2,1)S(1)}, bf16[3,2,10,32,128]{4,3,2,1,0:T(8,128)(2,1)S(1)}, u32[]{:S(2)}, u32[]{:S(2)}) %collective-permute-start.12) | collective-permute-done | bytes 491552 | tf_op jit(solution)/shard_map/ppermute | solution.py:25
  106.1 10.6 %collective-permute-done.23.refs_13_ = bf16[3,2,10,32,128]{4,3,2,1,0:T(8,128)(2,1)S(1)} collective-permute-done((bf16[3,2,10,32,128]{4,3,2,1,0:T(8,128)(2,1)S(1)}, bf16[3,2,10,32,128]{4,3,2,1,0:T(8,128)(2,1)S(1)}, u32[]{:S(2)}, u32[]{:S(2)}) %collective-permute-start.23) | collective-permute-done | bytes 491552 | tf_op jit(solution)/shard_map/ppermute | solution.py:25
  116.6 4.2 %shard_map.83 = (bf16[192,8192]{1,0:T(8,128)(2,1)}, bf16[16,4,128,128]{3,2,1,0:T(8,128)(2,1)}) custom-call(bf16[4,2,10,32,128]{4,3,2,1,0:T(8,128)(2,1)S(1)} %shard_map.69.refs_0_, bf16[1,2,10,32,128]{4,3,2,1,0:T(8,128)(2,1)S(1)} %collective-permute-done.5.refs_1_, bf16[3,2,10,32,128]{4,3,2,1,0:T(8,128)(2,1)S(1)} %collective-permute-done.6.refs_2_, ...), custom_call_target="tpu_custom_call" | custom-call | bytes 8388608 | tf_op jit(solution)/shard_map/pallas_call | solution.py:43
  (45 shorter events, 17.3 us)
Async XLA Ops:
  3.1 28.5 %all-to-all-start = ((bf16[16,144,128]{2,1,0:T(8,128)(2,1)}), bf16[16,144,128]{2,1,0:T(8,128)(2,1)S(1)}, u32[]{:S(2)}, u32[]{:S(2)}) async-start(bf16[16,144,128]{2,1,0:T(8,128)(2,1)} %get-tuple-element.8), calls=%async_computation | async-start | bytes 1179648 | tf_op jit(solution)/shard_map/all_to_all | solution.py:207
  13.1 8.3 %collective-permute-start = (bf16[1024,128]{1,0:T(8,128)(2,1)}, bf16[1024,128]{1,0:T(8,128)(2,1)S(1)}, u32[]{:S(2)}, u32[]{:S(2)}) collective-permute-start(bf16[1024,128]{1,0:T(8,128)(2,1)} %get-tuple-element.9.refs_4_), channel_id=1, source_target_pairs={{0,3},{1,0},{2,1},{3,2},{4,7},{5,4},{6,5},{7,6},{8,11},{9,8},{10,9... | collective-permute-start | bytes 786440 | tf_op jit(solution)/shard_map/ppermute | solution.py:25
  31.6 13.2 %collective-permute-start.3 = (bf16[8,144,128]{2,1,0:T(8,128)(2,1)S(1)}, bf16[8,144,128]{2,1,0:T(8,128)(2,1)S(1)}, u32[]{:S(2)}, u32[]{:S(2)}) collective-permute-start(bf16[8,144,128]{2,1,0:T(8,128)(2,1)S(1)} %get-tuple-element.15.refs_0_), channel_id=1, source_target_pairs={{0,2},{1,3},{2,0},{3,1},{4,6},{5,7},{6,4},{7,5},{8,10},{9,11},{10,... | collective-permute-start | bytes 884744 | tf_op jit(solution)/shard_map/ppermute | solution.py:25
  34.5 14.2 %collective-permute-start.2 = (bf16[8,144,128]{2,1,0:T(8,128)(2,1)S(1)}, bf16[8,144,128]{2,1,0:T(8,128)(2,1)S(1)}, u32[]{:S(2)}, u32[]{:S(2)}) collective-permute-start(bf16[8,144,128]{2,1,0:T(8,128)(2,1)S(1)} %get-tuple-element.15.refs_0_), channel_id=1, source_target_pairs={{0,3},{1,0},{2,1},{3,2},{4,7},{5,4},{6,5},{7,6},{8,11},{9,8},{10,9... | collective-permute-start | bytes 884744 | tf_op jit(solution)/shard_map/ppermute | solution.py:25
  35.3 8.9 %collective-permute-start.4 = (bf16[1024,128]{1,0:T(8,128)(2,1)}, bf16[1024,128]{1,0:T(8,128)(2,1)S(1)}, u32[]{:S(2)}, u32[]{:S(2)}) collective-permute-start(bf16[1024,128]{1,0:T(8,128)(2,1)} %get-tuple-element.9.refs_4_), channel_id=1, source_target_pairs={{0,12},{1,13},{2,14},{3,15},{4,0},{5,1},{6,2},{7,3},{8,4},{9,5},{1... | collective-permute-start | bytes 786440 | tf_op jit(solution)/shard_map/ppermute | solution.py:25
  38.1 15.8 %collective-permute-start.1 = (bf16[8,144,128]{2,1,0:T(8,128)(2,1)S(1)}, bf16[8,144,128]{2,1,0:T(8,128)(2,1)S(1)}, u32[]{:S(2)}, u32[]{:S(2)}) collective-permute-start(bf16[8,144,128]{2,1,0:T(8,128)(2,1)S(1)} %get-tuple-element.15.refs_0_), channel_id=1, source_target_pairs={{0,1},{1,2},{2,3},{3,0},{4,5},{5,6},{6,7},{7,4},{8,9},{9,10},{10,1... | collective-permute-start | bytes 884744 | tf_op jit(solution)/shard_map/ppermute | solution.py:25
  38.7 15.7 %collective-permute-start.21 = (bf16[1024,128]{1,0:T(8,128)(2,1)}, bf16[1024,128]{1,0:T(8,128)(2,1)S(1)}, u32[]{:S(2)}, u32[]{:S(2)}) collective-permute-start(bf16[1024,128]{1,0:T(8,128)(2,1)} %get-tuple-element.9.refs_4_), channel_id=1, source_target_pairs={{0,2},{1,3},{2,0},{3,1},{4,6},{5,7},{6,4},{7,5},{8,10},{9,11},{10,... | collective-permute-start | bytes 786440 | tf_op jit(solution)/shard_map/ppermute | solution.py:25
  44.2 15.5 %collective-permute-start.18 = (bf16[1024,128]{1,0:T(8,128)(2,1)}, bf16[1024,128]{1,0:T(8,128)(2,1)S(1)}, u32[]{:S(2)}, u32[]{:S(2)}) collective-permute-start(bf16[1024,128]{1,0:T(8,128)(2,1)} %get-tuple-element.9.refs_4_), channel_id=1, source_target_pairs={{0,1},{1,2},{2,3},{3,0},{4,5},{5,6},{6,7},{7,4},{8,9},{9,10},{10,1... | collective-permute-start | bytes 786440 | tf_op jit(solution)/shard_map/ppermute | solution.py:25
  44.8 17.0 %collective-permute-start.10 = (bf16[1024,128]{1,0:T(8,128)(2,1)}, bf16[1024,128]{1,0:T(8,128)(2,1)S(1)}, u32[]{:S(2)}, u32[]{:S(2)}) collective-permute-start(bf16[1024,128]{1,0:T(8,128)(2,1)} %get-tuple-element.9.refs_4_), channel_id=1, source_target_pairs={{0,8},{1,9},{2,10},{3,11},{4,12},{5,13},{6,14},{7,15},{8,0},{9,1},... | collective-permute-start | bytes 786440 | tf_op jit(solution)/shard_map/ppermute | solution.py:25
  48.7 13.9 %collective-permute-start.7 = (bf16[1024,128]{1,0:T(8,128)(2,1)}, bf16[1024,128]{1,0:T(8,128)(2,1)S(1)}, u32[]{:S(2)}, u32[]{:S(2)}) collective-permute-start(bf16[1024,128]{1,0:T(8,128)(2,1)} %get-tuple-element.9.refs_4_), channel_id=1, source_target_pairs={{0,4},{1,5},{2,6},{3,7},{4,8},{5,9},{6,10},{7,11},{8,12},{9,13},{1... | collective-permute-start | bytes 786440 | tf_op jit(solution)/shard_map/ppermute | solution.py:25
  53.9 10.2 %collective-permute-start.5 = (bf16[1,2,10,32,128]{4,3,2,1,0:T(8,128)(2,1)S(1)}, bf16[1,2,10,32,128]{4,3,2,1,0:T(8,128)(2,1)S(1)}, u32[]{:S(2)}, u32[]{:S(2)}) collective-permute-start(bf16[1,2,10,32,128]{4,3,2,1,0:T(8,128)(2,1)S(1)} %shard_map.70), channel_id=1, source_target_pairs={{0,4},{1,5},{2,6},{3,7},{4,8},{5,9},{6,10},{7,11},{8,12},{9,13},{1... | collective-permute-start | bytes 491528 | tf_op jit(solution)/shard_map/ppermute | solution.py:25
  54.3 42.0 %collective-permute-start.6 = (bf16[3,2,10,32,128]{4,3,2,1,0:T(8,128)(2,1)S(1)}, bf16[3,2,10,32,128]{4,3,2,1,0:T(8,128)(2,1)S(1)}, u32[]{:S(2)}, u32[]{:S(2)}) collective-permute-start(bf16[3,2,10,32,128]{4,3,2,1,0:T(8,128)(2,1)S(1)} %shard_map.71), channel_id=1, source_target_pairs={{0,4},{1,5},{2,6},{3,7},{4,8},{5,9},{6,10},{7,11},{8,12},{9,13},{1... | collective-permute-start | bytes 1474568 | tf_op jit(solution)/shard_map/ppermute | solution.py:25
  59.7 20.7 %collective-permute-start.15 = (bf16[8,144,128]{2,1,0:T(8,128)(2,1)S(1)}, bf16[8,144,128]{2,1,0:T(8,128)(2,1)S(1)}, u32[]{:S(2)}, u32[]{:S(2)}) collective-permute-start(bf16[8,144,128]{2,1,0:T(8,128)(2,1)S(1)} %get-tuple-element.14.refs_0_), channel_id=1, source_target_pairs={{0,8},{1,9},{2,10},{3,11},{4,12},{5,13},{6,14},{7,15},{8,0},{9,1},... | collective-permute-start | bytes 884744 | tf_op jit(solution)/shard_map/ppermute | solution.py:25
  61.9 20.7 %collective-permute-start.14 = (bf16[8,144,128]{2,1,0:T(8,128)(2,1)S(1)}, bf16[8,144,128]{2,1,0:T(8,128)(2,1)S(1)}, u32[]{:S(2)}, u32[]{:S(2)}) collective-permute-start(bf16[8,144,128]{2,1,0:T(8,128)(2,1)S(1)} %get-tuple-element.14.refs_0_), channel_id=1, source_target_pairs={{0,12},{1,13},{2,14},{3,15},{4,0},{5,1},{6,2},{7,3},{8,4},{9,5},{1... | collective-permute-start | bytes 884744 | tf_op jit(solution)/shard_map/ppermute | solution.py:25
  62.7 25.2 %collective-permute-start.13 = (bf16[8,144,128]{2,1,0:T(8,128)(2,1)S(1)}, bf16[8,144,128]{2,1,0:T(8,128)(2,1)S(1)}, u32[]{:S(2)}, u32[]{:S(2)}) collective-permute-start(bf16[8,144,128]{2,1,0:T(8,128)(2,1)S(1)} %get-tuple-element.14.refs_0_), channel_id=1, source_target_pairs={{0,4},{1,5},{2,6},{3,7},{4,8},{5,9},{6,10},{7,11},{8,12},{9,13},{1... | collective-permute-start | bytes 884744 | tf_op jit(solution)/shard_map/ppermute | solution.py:25
  64.0 14.7 %collective-permute-start.8 = (bf16[1,2,10,32,128]{4,3,2,1,0:T(8,128)(2,1)S(1)}, bf16[1,2,10,32,128]{4,3,2,1,0:T(8,128)(2,1)S(1)}, u32[]{:S(2)}, u32[]{:S(2)}) collective-permute-start(bf16[1,2,10,32,128]{4,3,2,1,0:T(8,128)(2,1)S(1)} %shard_map.72), channel_id=1, source_target_pairs={{0,12},{1,13},{2,14},{3,15},{4,0},{5,1},{6,2},{7,3},{8,4},{9,5},{1... | collective-permute-start | bytes 491528 | tf_op jit(solution)/shard_map/ppermute | solution.py:25
  78.7 11.5 %collective-permute-start.11 = (bf16[1,2,10,32,128]{4,3,2,1,0:T(8,128)(2,1)S(1)}, bf16[1,2,10,32,128]{4,3,2,1,0:T(8,128)(2,1)S(1)}, u32[]{:S(2)}, u32[]{:S(2)}) collective-permute-start(bf16[1,2,10,32,128]{4,3,2,1,0:T(8,128)(2,1)S(1)} %shard_map.74), channel_id=1, source_target_pairs={{0,8},{1,9},{2,10},{3,11},{4,12},{5,13},{6,14},{7,15},{8,0},{9,1},... | collective-permute-start | bytes 491528 | tf_op jit(solution)/shard_map/ppermute | solution.py:25
  80.4 10.1 %collective-permute-start.16 = (bf16[1,2,10,32,128]{4,3,2,1,0:T(8,128)(2,1)S(1)}, bf16[1,2,10,32,128]{4,3,2,1,0:T(8,128)(2,1)S(1)}, u32[]{:S(2)}, u32[]{:S(2)}) collective-permute-start(bf16[1,2,10,32,128]{4,3,2,1,0:T(8,128)(2,1)S(1)} %shard_map.77), channel_id=1, source_target_pairs={{0,1},{1,2},{2,3},{3,0},{4,5},{5,6},{6,7},{7,4},{8,9},{9,10},{10,1... | collective-permute-start | bytes 491528 | tf_op jit(solution)/shard_map/ppermute | solution.py:25
  82.6 10.4 %collective-permute-start.19 = (bf16[1,2,10,32,128]{4,3,2,1,0:T(8,128)(2,1)S(1)}, bf16[1,2,10,32,128]{4,3,2,1,0:T(8,128)(2,1)S(1)}, u32[]{:S(2)}, u32[]{:S(2)}) collective-permute-start(bf16[1,2,10,32,128]{4,3,2,1,0:T(8,128)(2,1)S(1)} %shard_map.79), channel_id=1, source_target_pairs={{0,3},{1,0},{2,1},{3,2},{4,7},{5,4},{6,5},{7,6},{8,11},{9,8},{10,9... | collective-permute-start | bytes 491528 | tf_op jit(solution)/shard_map/ppermute | solution.py:25
  90.3 12.1 %collective-permute-start.9 = (bf16[3,2,10,32,128]{4,3,2,1,0:T(8,128)(2,1)S(1)}, bf16[3,2,10,32,128]{4,3,2,1,0:T(8,128)(2,1)S(1)}, u32[]{:S(2)}, u32[]{:S(2)}) collective-permute-start(bf16[3,2,10,32,128]{4,3,2,1,0:T(8,128)(2,1)S(1)} %shard_map.73), channel_id=1, source_target_pairs={{0,12},{1,13},{2,14},{3,15},{4,0},{5,1},{6,2},{7,3},{8,4},{9,5},{1... | collective-permute-start | bytes 1474568 | tf_op jit(solution)/shard_map/ppermute | solution.py:25
  90.5 13.4 %collective-permute-start.12 = (bf16[3,2,10,32,128]{4,3,2,1,0:T(8,128)(2,1)S(1)}, bf16[3,2,10,32,128]{4,3,2,1,0:T(8,128)(2,1)S(1)}, u32[]{:S(2)}, u32[]{:S(2)}) collective-permute-start(bf16[3,2,10,32,128]{4,3,2,1,0:T(8,128)(2,1)S(1)} %shard_map.75), channel_id=1, source_target_pairs={{0,8},{1,9},{2,10},{3,11},{4,12},{5,13},{6,14},{7,15},{8,0},{9,1},... | collective-permute-start | bytes 1474568 | tf_op jit(solution)/shard_map/ppermute | solution.py:25
  93.0 12.4 %collective-permute-start.17 = (bf16[3,2,10,32,128]{4,3,2,1,0:T(8,128)(2,1)S(1)}, bf16[3,2,10,32,128]{4,3,2,1,0:T(8,128)(2,1)S(1)}, u32[]{:S(2)}, u32[]{:S(2)}) collective-permute-start(bf16[3,2,10,32,128]{4,3,2,1,0:T(8,128)(2,1)S(1)} %shard_map.78), channel_id=1, source_target_pairs={{0,1},{1,2},{2,3},{3,0},{4,5},{5,6},{6,7},{7,4},{8,9},{9,10},{10,1... | collective-permute-start | bytes 1474568 | tf_op jit(solution)/shard_map/ppermute | solution.py:25
  95.2 10.9 %collective-permute-start.20 = (bf16[3,2,10,32,128]{4,3,2,1,0:T(8,128)(2,1)S(1)}, bf16[3,2,10,32,128]{4,3,2,1,0:T(8,128)(2,1)S(1)}, u32[]{:S(2)}, u32[]{:S(2)}) collective-permute-start(bf16[3,2,10,32,128]{4,3,2,1,0:T(8,128)(2,1)S(1)} %shard_map.80), channel_id=1, source_target_pairs={{0,3},{1,0},{2,1},{3,2},{4,7},{5,4},{6,5},{7,6},{8,11},{9,8},{10,9... | collective-permute-start | bytes 1474568 | tf_op jit(solution)/shard_map/ppermute | solution.py:25
  96.4 20.3 %collective-permute-start.23 = (bf16[3,2,10,32,128]{4,3,2,1,0:T(8,128)(2,1)S(1)}, bf16[3,2,10,32,128]{4,3,2,1,0:T(8,128)(2,1)S(1)}, u32[]{:S(2)}, u32[]{:S(2)}) collective-permute-start(bf16[3,2,10,32,128]{4,3,2,1,0:T(8,128)(2,1)S(1)} %shard_map.82), channel_id=1, source_target_pairs={{0,2},{1,3},{2,0},{3,1},{4,6},{5,7},{6,4},{7,5},{8,10},{9,11},{10,... | collective-permute-start | bytes 1474568 | tf_op jit(solution)/shard_map/ppermute | solution.py:25
  (2 other events, 15.9 us)

commit v5 on v4

--- a/solution.py
+++ b/solution.py
@@ -140,9 +140,9 @@
     )
 
 
-def join_kernel(counts, *refs):
-    pieces, (keys, values, sorted_, lined, sems) = refs[: sum(counts)], refs[sum(counts) :]
-    groups = sorted_.shape[2]
+def join_kernel(first, outer, inner, counts, *refs):
+    pieces, (keys, values, sorted_, lined, sems) = refs[: sum(counts)], refs[-5:]
+    groups = sorted_.shape[1]
     copies = []
 
     def copy(src, dst):
@@ -150,51 +150,47 @@
         copies[-1].start()
 
     at = 0
-    for h, (outer, inner) in enumerate(("yx", "xy")):
-        sources = []
-        for o in range(len(HOPS)):
-            mine = pieces[at : at + counts[h * 4 + o]]
-            at += len(mine)
-            sources.append([p.at[k] for p in mine for k in range(p.shape[0])])
-        for o in range(4):
-            for n in range(4):
-                place = {outer: sender(outer, HOPS[o]), inner: sender(inner, HOPS[n])}
-                rows = pl.ds(pl.multiple_of(place["x"] * 32, 32), 32)
-                for g in range(groups):
-                    to = (h * groups + g) * 4
-                    copy(sources[o][n].at[g, 6:10], values.at[to : to + 4, place["y"], rows])
-        for o in range(4):
-            for n in range(4):
-                place = {outer: sender(outer, HOPS[o]), inner: sender(inner, HOPS[n])}
-                slot = place["y"] * SIDE + place["x"]
-                for g in range(groups):
-                    sorted_[h, slot, g] = sources[o][n][g, 0:6].reshape(192, 128)
-        for g in range(groups):
-            for y in range(SIDE):
-                parts = [sorted_[h, y * SIDE + x, g] for x in range(SIDE)]
-                for k, part in enumerate(regroup(parts)):
-                    lined[h * groups + g, :, 512 * k + 128 * y : 512 * k + 128 * y + 128] = part
-            first = (h * groups + g) * 2048
-            copy(lined.at[h * groups + g], keys.at[:, first : first + 2048])
+    for o in range(len(HOPS)):
+        mine = pieces[at : at + counts[o]]
+        at += len(mine)
+        units = [p.at[k] for p in mine for k in range(p.shape[0])]
+        for n, unit in enumerate(units):
+            place = {outer: sender(outer, HOPS[o]), inner: sender(inner, HOPS[n])}
+            rows = pl.ds(pl.multiple_of(place["x"] * 32, 32), 32)
+            slot = place["y"] * SIDE + place["x"]
+            for g in range(groups):
+                to = first + 4 * g
+                copy(unit.at[g, 6:10], values.at[to : to + 4, place["y"], rows])
+                sorted_[slot, g] = unit[g, 0:6].reshape(192, 128)
+    for g in range(groups):
+        for y in range(SIDE):
+            parts = [sorted_[y * SIDE + x, g] for x in range(SIDE)]
+            for k, part in enumerate(regroup(parts)):
+                lined[g, :, 512 * k + 128 * y : 512 * k + 128 * y + 128] = part
+        at = (first + 4 * g) * 512
+        copy(lined.at[g], keys.at[:, at : at + 2048])
     for each in copies:
         each.wait()
 
 
-def join(x_got, y_got):
-    groups = x_got[0][0].shape[1]
-    got = x_got + y_got
+def join(got, first, outer, inner, before=()):
+    pieces = sum(got, [])
+    groups = got[0][0].shape[1]
+    n = len(pieces)
     return call(
-        functools.partial(join_kernel, tuple(map(len, got))),
+        functools.partial(join_kernel, first, outer, inner, tuple(map(len, got))),
         (shape(192, 2 * groups * 2048), shape(2 * groups * 4, SIDE, 128, 128)),
-        sum(got, []),
+        (*pieces, *before),
+        in_specs=whole(n) + whole(len(before), pltpu.HBM),
         out_space=pltpu.HBM,
-        limit=16 * MIB,
+        limit=8 * MIB,
         scratch=[
-            VMEM((2, SIDE * SIDE, groups, 192, 128), BF16),
-            VMEM((2 * groups, 192, 2048), BF16),
-            pltpu.SemaphoreType.DMA((2 * groups * (SIDE * SIDE + 1),)),
+            VMEM((SIDE * SIDE, groups, 192, 128), BF16),
+            VMEM((groups, 192, 2048), BF16),
+            pltpu.SemaphoreType.DMA((groups * (SIDE * SIDE + 1),)),
         ],
-        nbytes=8 * MIB,
+        alias={n + k: k for k in range(len(before))},
+        nbytes=4 * MIB,
     )
 
 
@@ -222,7 +218,8 @@
         for a in "yx":
             piece = expand(near[a][1:] if i else near[a], heads[OTHER[a]][i])
             got[a][i] = [ahead[a][i], named_move(piece, OTHER[a], i)] if i else [piece]
-    keys, values = join(got["x"], got["y"])
+    outs = join(got["y"], half, "x", "y")
+    keys, values = join(got["x"], 0, "y", "x", outs)
     return keys[None, None], values.reshape(1, -1, 1, 128)
 
 

time: 122 us -> 152 us (1.25)
  the two profiles are of different devices: /device:TPU:1 before, /device:TPU:14 now
where the time goes in v5:
time: 152 us; the launch traced here: 151 us
  waiting for transfers between devices  97.2 us (64%)
  starting transfers between devices  39.8 us (26%)
  Pallas kernels  13.4 us (9%)
    ppermute x24, waiting for transfers between devices, move(): return lax.ppermute(array, 'tp', pairs)  90.1 us
    ppermute x24, starting transfers between devices, move(): return lax.ppermute(array, 'tp', pairs)  31.2 us
    pallas_call x17, Pallas kernels, call(): pl.pallas_call(kernel, out_shape=outs, in_specs=in_specs or whole(len(arg...  13.4 us
    all_to_all x1, starting transfers between devices, shards(): mine = lax.all_to_all(rows, 'seq', split_axis=0, concat_axis=0, tiled=True)  8.58 us
    all_to_all x1, waiting for transfers between devices, shards(): mine = lax.all_to_all(rows, 'seq', split_axis=0, concat_axis=0, tiled=True)  7.07 us
  transfers between devices with their start and end apart: 25, of which 11 were waited for; matrix products, arithmetic and copies ran while one was open for 0% of the time, Pallas kernels for 5%

profile of v5, /device:TPU:14, one launch (start us, length us, event | category | flops | bytes accessed | tf_op | source)
XLA Modules:
  0.0 151.3 jit_solution(10614623599210975826)
XLA Ops:
  0.6 2.4 %shard_map.68 = (bf16[16,144,128]{2,1,0:T(8,128)(2,1)}, bf16[1024,128]{1,0:T(8,128)(2,1)}) custom-call(bf16[16,32,512]{2,1,0:T(8,128)(2,1)} %lat_in.1, bf16[16,32,64]{2,1,0:T(8,128)(2,1)} %rot_in.1, f32[1,512]{1,0:T(1,128)} %bitcast.9, bf16[512,128]{1,0:T(8,128)(2,1)} %bitcast.7, bf16[512,128]{1,0:T(8,128)(2,1)} %bitcast.8), custom_call_target="tpu_custom_call" | custom-call | bytes 1048576 | tf_op jit(solution)/shard_map/pallas_call | solution.py:43
  3.1 8.6 %all-to-all-start = ((bf16[16,144,128]{2,1,0:T(8,128)(2,1)}), bf16[16,144,128]{2,1,0:T(8,128)(2,1)S(1)}, u32[]{:S(2)}, u32[]{:S(2)}) async-start(bf16[16,144,128]{2,1,0:T(8,128)(2,1)} %get-tuple-element.10), calls=%async_computation | async-start | bytes 1179648 | tf_op jit(solution)/shard_map/all_to_all | solution.py:203
  12.6 9.1 %collective-permute-done.refs_1_.refs_3_ = bf16[1024,128]{1,0:T(8,128)(2,1)S(1)} collective-permute-done((bf16[1024,128]{1,0:T(8,128)(2,1)}, bf16[1024,128]{1,0:T(8,128)(2,1)S(1)}, u32[]{:S(2)}, u32[]{:S(2)}) %collective-permute-start) | collective-permute-done | bytes 262176 | tf_op jit(solution)/shard_map/ppermute | solution.py:25
  21.7 7.1 %all-to-all-done = bf16[16,144,128]{2,1,0:T(8,128)(2,1)S(1)} async-done(((bf16[16,144,128]{2,1,0:T(8,128)(2,1)}), bf16[16,144,128]{2,1,0:T(8,128)(2,1)S(1)}, u32[]{:S(2)}, u32[]{:S(2)}) %all-to-all-start) | async-done | bytes 589856 | tf_op jit(solution)/shard_map/all_to_all | solution.py:203
  28.8 2.4 %collective-permute-start.15 = (bf16[8,144,128]{2,1,0:T(8,128)(2,1)S(1)}, bf16[8,144,128]{2,1,0:T(8,128)(2,1)S(1)}, u32[]{:S(2)}, u32[]{:S(2)}) collective-permute-start(bf16[8,144,128]{2,1,0:T(8,128)(2,1)S(1)} %get-tuple-element.18.refs_0_), channel_id=1, source_target_pairs={{0,8},{1,9},{2,10},{3,11},{4,12},{5,13},{6,14},{7,15},{8,0},{9,1},... | collective-permute-start | bytes 884744 | tf_op jit(solution)/shard_map/ppermute | solution.py:25
  36.0 16.2 %collective-permute-done.4.refs_1_.refs_3_ = bf16[1024,128]{1,0:T(8,128)(2,1)S(1)} collective-permute-done((bf16[1024,128]{1,0:T(8,128)(2,1)}, bf16[1024,128]{1,0:T(8,128)(2,1)S(1)}, u32[]{:S(2)}, u32[]{:S(2)}) %collective-permute-start.4) | collective-permute-done | bytes 262176 | tf_op jit(solution)/shard_map/ppermute | solution.py:25
  52.7 2.3 %collective-permute-start.10 = (bf16[1024,128]{1,0:T(8,128)(2,1)}, bf16[1024,128]{1,0:T(8,128)(2,1)S(1)}, u32[]{:S(2)}, u32[]{:S(2)}) collective-permute-start(bf16[1024,128]{1,0:T(8,128)(2,1)} %get-tuple-element.11.refs_4_), channel_id=1, source_target_pairs={{0,8},{1,9},{2,10},{3,11},{4,12},{5,13},{6,14},{7,15},{8,0},{9,1},... | collective-permute-start | bytes 786440 | tf_op jit(solution)/shard_map/ppermute | solution.py:25
  55.3 1.9 %collective-permute-start.5 = (bf16[1,2,10,32,128]{4,3,2,1,0:T(8,128)(2,1)S(1)}, bf16[1,2,10,32,128]{4,3,2,1,0:T(8,128)(2,1)S(1)}, u32[]{:S(2)}, u32[]{:S(2)}) collective-permute-start(bf16[1,2,10,32,128]{4,3,2,1,0:T(8,128)(2,1)S(1)} %shard_map.70), channel_id=1, source_target_pairs={{0,4},{1,5},{2,6},{3,7},{4,8},{5,9},{6,10},{7,11},{8,12},{9,13},{1... | collective-permute-start | bytes 491528 | tf_op jit(solution)/shard_map/ppermute | solution.py:25
  57.6 1.6 %collective-permute-start.17 = (bf16[3,2,10,32,128]{4,3,2,1,0:T(8,128)(2,1)S(1)}, bf16[3,2,10,32,128]{4,3,2,1,0:T(8,128)(2,1)S(1)}, u32[]{:S(2)}, u32[]{:S(2)}) collective-permute-start(bf16[3,2,10,32,128]{4,3,2,1,0:T(8,128)(2,1)S(1)} %shard_map.78), channel_id=1, source_target_pairs={{0,1},{1,2},{2,3},{3,0},{4,5},{5,6},{6,7},{7,4},{8,9},{9,10},{10,1... | collective-permute-start | bytes 1474568 | tf_op jit(solution)/shard_map/ppermute | solution.py:25
  59.2 2.4 %collective-permute-done.18.refs_1_.refs_3_ = bf16[1024,128]{1,0:T(8,128)(2,1)S(1)} collective-permute-done((bf16[1024,128]{1,0:T(8,128)(2,1)}, bf16[1024,128]{1,0:T(8,128)(2,1)S(1)}, u32[]{:S(2)}, u32[]{:S(2)}) %collective-permute-start.18) | collective-permute-done | bytes 262176 | tf_op jit(solution)/shard_map/ppermute | solution.py:25
  64.0 3.6 %collective-permute-done.7.refs_1_.refs_3_ = bf16[1024,128]{1,0:T(8,128)(2,1)S(1)} collective-permute-done((bf16[1024,128]{1,0:T(8,128)(2,1)}, bf16[1024,128]{1,0:T(8,128)(2,1)S(1)}, u32[]{:S(2)}, u32[]{:S(2)}) %collective-permute-start.7) | collective-permute-done | bytes 262176 | tf_op jit(solution)/shard_map/ppermute | solution.py:25
  67.6 1.5 collective-permute-start.1
  70.5 1.5 collective-permute-start.16
  73.5 13.9 %collective-permute-done.16.refs_1_ = bf16[1,2,10,32,128]{4,3,2,1,0:T(8,128)(2,1)S(1)} collective-permute-done((bf16[1,2,10,32,128]{4,3,2,1,0:T(8,128)(2,1)S(1)}, bf16[1,2,10,32,128]{4,3,2,1,0:T(8,128)(2,1)S(1)}, u32[]{:S(2)}, u32[]{:S(2)}) %collective-permute-start.16) | collective-permute-done | bytes 163872 | tf_op jit(solution)/shard_map/ppermute | solution.py:25
  88.8 3.3 %collective-permute-start.23 = (bf16[3,2,10,32,128]{4,3,2,1,0:T(8,128)(2,1)S(1)}, bf16[3,2,10,32,128]{4,3,2,1,0:T(8,128)(2,1)S(1)}, u32[]{:S(2)}, u32[]{:S(2)}) collective-permute-start(bf16[3,2,10,32,128]{4,3,2,1,0:T(8,128)(2,1)S(1)} %shard_map.82), channel_id=1, source_target_pairs={{0,2},{1,3},{2,0},{3,1},{4,6},{5,7},{6,4},{7,5},{8,10},{9,11},{10,... | collective-permute-start | bytes 1474568 | tf_op jit(solution)/shard_map/ppermute | solution.py:25
  93.7 2.0 %collective-permute-done.19.refs_3_ = bf16[1,2,10,32,128]{4,3,2,1,0:T(8,128)(2,1)S(1)} collective-permute-done((bf16[1,2,10,32,128]{4,3,2,1,0:T(8,128)(2,1)S(1)}, bf16[1,2,10,32,128]{4,3,2,1,0:T(8,128)(2,1)S(1)}, u32[]{:S(2)}, u32[]{:S(2)}) %collective-permute-start.19) | collective-permute-done | bytes 163872 | tf_op jit(solution)/shard_map/ppermute | solution.py:25
  96.1 22.2 %collective-permute-done.22.refs_5_ = bf16[1,2,10,32,128]{4,3,2,1,0:T(8,128)(2,1)S(1)} collective-permute-done((bf16[1,2,10,32,128]{4,3,2,1,0:T(8,128)(2,1)S(1)}, bf16[1,2,10,32,128]{4,3,2,1,0:T(8,128)(2,1)S(1)}, u32[]{:S(2)}, u32[]{:S(2)}) %collective-permute-start.22) | collective-permute-done | bytes 163872 | tf_op jit(solution)/shard_map/ppermute | solution.py:25
  118.3 1.4 collective-permute-start.9
  121.7 1.4 collective-permute-start.8
  123.1 2.1 %collective-permute-start.11 = (bf16[1,2,10,32,128]{4,3,2,1,0:T(8,128)(2,1)S(1)}, bf16[1,2,10,32,128]{4,3,2,1,0:T(8,128)(2,1)S(1)}, u32[]{:S(2)}, u32[]{:S(2)}) collective-permute-start(bf16[1,2,10,32,128]{4,3,2,1,0:T(8,128)(2,1)S(1)} %shard_map.74), channel_id=1, source_target_pairs={{0,8},{1,9},{2,10},{3,11},{4,12},{5,13},{6,14},{7,15},{8,0},{9,1},... | collective-permute-start | bytes 491528 | tf_op jit(solution)/shard_map/ppermute | solution.py:25
  126.3 2.7 %shard_map.83 = (bf16[192,8192]{1,0:T(8,128)(2,1)}, bf16[16,4,128,128]{3,2,1,0:T(8,128)(2,1)}) custom-call(bf16[4,2,10,32,128]{4,3,2,1,0:T(8,128)(2,1)S(1)} %shard_map.76.refs_0_, bf16[1,2,10,32,128]{4,3,2,1,0:T(8,128)(2,1)S(1)} %collective-permute-done.16.refs_1_, bf16[3,2,10,32,128]{4,3,2,1,0:T(8,128)(2,1)S(1)} %collective-permute-done.17.refs_2_, ...), custom_call_target="tpu_custom_call" | custom-call | bytes 4194304 | tf_op jit(solution)/shard_map/pallas_call | solution.py:43
  129.0 15.8 %collective-permute-done.8.refs_3_ = bf16[1,2,10,32,128]{4,3,2,1,0:T(8,128)(2,1)S(1)} collective-permute-done((bf16[1,2,10,32,128]{4,3,2,1,0:T(8,128)(2,1)S(1)}, bf16[1,2,10,32,128]{4,3,2,1,0:T(8,128)(2,1)S(1)}, u32[]{:S(2)}, u32[]{:S(2)}) %collective-permute-start.8) | collective-permute-done | bytes 163872 | tf_op jit(solution)/shard_map/ppermute | solution.py:25
  144.8 3.7 %collective-permute-done.11.refs_5_ = bf16[1,2,10,32,128]{4,3,2,1,0:T(8,128)(2,1)S(1)} collective-permute-done((bf16[1,2,10,32,128]{4,3,2,1,0:T(8,128)(2,1)S(1)}, bf16[1,2,10,32,128]{4,3,2,1,0:T(8,128)(2,1)S(1)}, u32[]{:S(2)}, u32[]{:S(2)}) %collective-permute-start.11) | collective-permute-done | bytes 163872 | tf_op jit(solution)/shard_map/ppermute | solution.py:25
  148.5 2.7 %shard_map.84 = (bf16[192,8192]{1,0:T(8,128)(2,1)}, bf16[16,4,128,128]{3,2,1,0:T(8,128)(2,1)}) custom-call(bf16[4,2,10,32,128]{4,3,2,1,0:T(8,128)(2,1)S(1)} %shard_map.69.refs_0_, bf16[1,2,10,32,128]{4,3,2,1,0:T(8,128)(2,1)S(1)} %collective-permute-done.5.refs_1_, ...), custom_call_target="tpu_custom_call", output_to_operand_aliasing={{0}: (7, {}), {1}: (8, {})} | custom-call | bytes 4194304 | tf_op jit(solution)/shard_map/pallas_call | solution.py:43
  (46 shorter events, 18.6 us)
Async XLA Ops:
  3.1 25.7 %all-to-all-start = ((bf16[16,144,128]{2,1,0:T(8,128)(2,1)}), bf16[16,144,128]{2,1,0:T(8,128)(2,1)S(1)}, u32[]{:S(2)}, u32[]{:S(2)}) async-start(bf16[16,144,128]{2,1,0:T(8,128)(2,1)} %get-tuple-element.10), calls=%async_computation | async-start | bytes 1179648 | tf_op jit(solution)/shard_map/all_to_all | solution.py:203
  11.7 10.0 %collective-permute-start = (bf16[1024,128]{1,0:T(8,128)(2,1)}, bf16[1024,128]{1,0:T(8,128)(2,1)S(1)}, u32[]{:S(2)}, u32[]{:S(2)}) collective-permute-start(bf16[1024,128]{1,0:T(8,128)(2,1)} %get-tuple-element.11.refs_4_), channel_id=1, source_target_pairs={{0,3},{1,0},{2,1},{3,2},{4,7},{5,4},{6,5},{7,6},{8,11},{9,8},{10,9... | collective-permute-start | bytes 786440 | tf_op jit(solution)/shard_map/ppermute | solution.py:25
  28.8 23.8 %collective-permute-start.15 = (bf16[8,144,128]{2,1,0:T(8,128)(2,1)S(1)}, bf16[8,144,128]{2,1,0:T(8,128)(2,1)S(1)}, u32[]{:S(2)}, u32[]{:S(2)}) collective-permute-start(bf16[8,144,128]{2,1,0:T(8,128)(2,1)S(1)} %get-tuple-element.18.refs_0_), channel_id=1, source_target_pairs={{0,8},{1,9},{2,10},{3,11},{4,12},{5,13},{6,14},{7,15},{8,0},{9,1},... | collective-permute-start | bytes 884744 | tf_op jit(solution)/shard_map/ppermute | solution.py:25
  31.2 23.8 %collective-permute-start.14 = (bf16[8,144,128]{2,1,0:T(8,128)(2,1)S(1)}, bf16[8,144,128]{2,1,0:T(8,128)(2,1)S(1)}, u32[]{:S(2)}, u32[]{:S(2)}) collective-permute-start(bf16[8,144,128]{2,1,0:T(8,128)(2,1)S(1)} %get-tuple-element.18.refs_0_), channel_id=1, source_target_pairs={{0,12},{1,13},{2,14},{3,15},{4,0},{5,1},{6,2},{7,3},{8,4},{9,5},{1... | collective-permute-start | bytes 884744 | tf_op jit(solution)/shard_map/ppermute | solution.py:25
  32.6 19.6 %collective-permute-start.4 = (bf16[1024,128]{1,0:T(8,128)(2,1)}, bf16[1024,128]{1,0:T(8,128)(2,1)S(1)}, u32[]{:S(2)}, u32[]{:S(2)}) collective-permute-start(bf16[1024,128]{1,0:T(8,128)(2,1)} %get-tuple-element.11.refs_4_), channel_id=1, source_target_pairs={{0,12},{1,13},{2,14},{3,15},{4,0},{5,1},{6,2},{7,3},{8,4},{9,5},{1... | collective-permute-start | bytes 786440 | tf_op jit(solution)/shard_map/ppermute | solution.py:25
  33.6 21.7 %collective-permute-start.13 = (bf16[8,144,128]{2,1,0:T(8,128)(2,1)S(1)}, bf16[8,144,128]{2,1,0:T(8,128)(2,1)S(1)}, u32[]{:S(2)}, u32[]{:S(2)}) collective-permute-start(bf16[8,144,128]{2,1,0:T(8,128)(2,1)S(1)} %get-tuple-element.18.refs_0_), channel_id=1, source_target_pairs={{0,4},{1,5},{2,6},{3,7},{4,8},{5,9},{6,10},{7,11},{8,12},{9,13},{1... | collective-permute-start | bytes 884744 | tf_op jit(solution)/shard_map/ppermute | solution.py:25
  34.6 23.0 %collective-permute-start.21 = (bf16[1024,128]{1,0:T(8,128)(2,1)}, bf16[1024,128]{1,0:T(8,128)(2,1)S(1)}, u32[]{:S(2)}, u32[]{:S(2)}) collective-permute-start(bf16[1024,128]{1,0:T(8,128)(2,1)} %get-tuple-element.11.refs_4_), channel_id=1, source_target_pairs={{0,2},{1,3},{2,0},{3,1},{4,6},{5,7},{6,4},{7,5},{8,10},{9,11},{10,... | collective-permute-start | bytes 786440 | tf_op jit(solution)/shard_map/ppermute | solution.py:25
  52.2 9.4 %collective-permute-start.18 = (bf16[1024,128]{1,0:T(8,128)(2,1)}, bf16[1024,128]{1,0:T(8,128)(2,1)S(1)}, u32[]{:S(2)}, u32[]{:S(2)}) collective-permute-start(bf16[1024,128]{1,0:T(8,128)(2,1)} %get-tuple-element.11.refs_4_), channel_id=1, source_target_pairs={{0,1},{1,2},{2,3},{3,0},{4,5},{5,6},{6,7},{7,4},{8,9},{9,10},{10,1... | collective-permute-start | bytes 786440 | tf_op jit(solution)/shard_map/ppermute | solution.py:25
  52.7 9.9 %collective-permute-start.10 = (bf16[1024,128]{1,0:T(8,128)(2,1)}, bf16[1024,128]{1,0:T(8,128)(2,1)S(1)}, u32[]{:S(2)}, u32[]{:S(2)}) collective-permute-start(bf16[1024,128]{1,0:T(8,128)(2,1)} %get-tuple-element.11.refs_4_), channel_id=1, source_target_pairs={{0,8},{1,9},{2,10},{3,11},{4,12},{5,13},{6,14},{7,15},{8,0},{9,1},... | collective-permute-start | bytes 786440 | tf_op jit(solution)/shard_map/ppermute | solution.py:25
  55.0 12.6 %collective-permute-start.7 = (bf16[1024,128]{1,0:T(8,128)(2,1)}, bf16[1024,128]{1,0:T(8,128)(2,1)S(1)}, u32[]{:S(2)}, u32[]{:S(2)}) collective-permute-start(bf16[1024,128]{1,0:T(8,128)(2,1)} %get-tuple-element.11.refs_4_), channel_id=1, source_target_pairs={{0,4},{1,5},{2,6},{3,7},{4,8},{5,9},{6,10},{7,11},{8,12},{9,13},{1... | collective-permute-start | bytes 786440 | tf_op jit(solution)/shard_map/ppermute | solution.py:25
  55.3 15.2 %collective-permute-start.5 = (bf16[1,2,10,32,128]{4,3,2,1,0:T(8,128)(2,1)S(1)}, bf16[1,2,10,32,128]{4,3,2,1,0:T(8,128)(2,1)S(1)}, u32[]{:S(2)}, u32[]{:S(2)}) collective-permute-start(bf16[1,2,10,32,128]{4,3,2,1,0:T(8,128)(2,1)S(1)} %shard_map.70), channel_id=1, source_target_pairs={{0,4},{1,5},{2,6},{3,7},{4,8},{5,9},{6,10},{7,11},{8,12},{9,13},{1... | collective-permute-start | bytes 491528 | tf_op jit(solution)/shard_map/ppermute | solution.py:25
  57.6 62.1 %collective-permute-start.17 = (bf16[3,2,10,32,128]{4,3,2,1,0:T(8,128)(2,1)S(1)}, bf16[3,2,10,32,128]{4,3,2,1,0:T(8,128)(2,1)S(1)}, u32[]{:S(2)}, u32[]{:S(2)}) collective-permute-start(bf16[3,2,10,32,128]{4,3,2,1,0:T(8,128)(2,1)S(1)} %shard_map.78), channel_id=1, source_target_pairs={{0,1},{1,2},{2,3},{3,0},{4,5},{5,6},{6,7},{7,4},{8,9},{9,10},{10,1... | collective-permute-start | bytes 1474568 | tf_op jit(solution)/shard_map/ppermute | solution.py:25
  61.6 26.7 %collective-permute-start.3 = (bf16[8,144,128]{2,1,0:T(8,128)(2,1)S(1)}, bf16[8,144,128]{2,1,0:T(8,128)(2,1)S(1)}, u32[]{:S(2)}, u32[]{:S(2)}) collective-permute-start(bf16[8,144,128]{2,1,0:T(8,128)(2,1)S(1)} %get-tuple-element.19.refs_0_), channel_id=1, source_target_pairs={{0,2},{1,3},{2,0},{3,1},{4,6},{5,7},{6,4},{7,5},{8,10},{9,11},{10,... | collective-permute-start | bytes 884744 | tf_op jit(solution)/shard_map/ppermute | solution.py:25
  62.6 26.3 %collective-permute-start.2 = (bf16[8,144,128]{2,1,0:T(8,128)(2,1)S(1)}, bf16[8,144,128]{2,1,0:T(8,128)(2,1)S(1)}, u32[]{:S(2)}, u32[]{:S(2)}) collective-permute-start(bf16[8,144,128]{2,1,0:T(8,128)(2,1)S(1)} %get-tuple-element.19.refs_0_), channel_id=1, source_target_pairs={{0,3},{1,0},{2,1},{3,2},{4,7},{5,4},{6,5},{7,6},{8,11},{9,8},{10,9... | collective-permute-start | bytes 884744 | tf_op jit(solution)/shard_map/ppermute | solution.py:25
  67.6 24.6 %collective-permute-start.1 = (bf16[8,144,128]{2,1,0:T(8,128)(2,1)S(1)}, bf16[8,144,128]{2,1,0:T(8,128)(2,1)S(1)}, u32[]{:S(2)}, u32[]{:S(2)}) collective-permute-start(bf16[8,144,128]{2,1,0:T(8,128)(2,1)S(1)} %get-tuple-element.19.refs_0_), channel_id=1, source_target_pairs={{0,1},{1,2},{2,3},{3,0},{4,5},{5,6},{6,7},{7,4},{8,9},{9,10},{10,1... | collective-permute-start | bytes 884744 | tf_op jit(solution)/shard_map/ppermute | solution.py:25
  70.5 16.9 %collective-permute-start.16 = (bf16[1,2,10,32,128]{4,3,2,1,0:T(8,128)(2,1)S(1)}, bf16[1,2,10,32,128]{4,3,2,1,0:T(8,128)(2,1)S(1)}, u32[]{:S(2)}, u32[]{:S(2)}) collective-permute-start(bf16[1,2,10,32,128]{4,3,2,1,0:T(8,128)(2,1)S(1)} %shard_map.77), channel_id=1, source_target_pairs={{0,1},{1,2},{2,3},{3,0},{4,5},{5,6},{6,7},{7,4},{8,9},{9,10},{10,1... | collective-permute-start | bytes 491528 | tf_op jit(solution)/shard_map/ppermute | solution.py:25
  88.2 33.4 %collective-permute-start.20 = (bf16[3,2,10,32,128]{4,3,2,1,0:T(8,128)(2,1)S(1)}, bf16[3,2,10,32,128]{4,3,2,1,0:T(8,128)(2,1)S(1)}, u32[]{:S(2)}, u32[]{:S(2)}) collective-permute-start(bf16[3,2,10,32,128]{4,3,2,1,0:T(8,128)(2,1)S(1)} %shard_map.80), channel_id=1, source_target_pairs={{0,3},{1,0},{2,1},{3,2},{4,7},{5,4},{6,5},{7,6},{8,11},{9,8},{10,9... | collective-permute-start | bytes 1474568 | tf_op jit(solution)/shard_map/ppermute | solution.py:25
  88.8 34.3 %collective-permute-start.23 = (bf16[3,2,10,32,128]{4,3,2,1,0:T(8,128)(2,1)S(1)}, bf16[3,2,10,32,128]{4,3,2,1,0:T(8,128)(2,1)S(1)}, u32[]{:S(2)}, u32[]{:S(2)}) collective-permute-start(bf16[3,2,10,32,128]{4,3,2,1,0:T(8,128)(2,1)S(1)} %shard_map.82), channel_id=1, source_target_pairs={{0,2},{1,3},{2,0},{3,1},{4,6},{5,7},{6,4},{7,5},{8,10},{9,11},{10,... | collective-permute-start | bytes 1474568 | tf_op jit(solution)/shard_map/ppermute | solution.py:25
  92.2 26.2 %collective-permute-start.22 = (bf16[1,2,10,32,128]{4,3,2,1,0:T(8,128)(2,1)S(1)}, bf16[1,2,10,32,128]{4,3,2,1,0:T(8,128)(2,1)S(1)}, u32[]{:S(2)}, u32[]{:S(2)}) collective-permute-start(bf16[1,2,10,32,128]{4,3,2,1,0:T(8,128)(2,1)S(1)} %shard_map.81), channel_id=1, source_target_pairs={{0,2},{1,3},{2,0},{3,1},{4,6},{5,7},{6,4},{7,5},{8,10},{9,11},{10,... | collective-permute-start | bytes 491528 | tf_op jit(solution)/shard_map/ppermute | solution.py:25
  95.7 52.7 %collective-permute-start.6 = (bf16[3,2,10,32,128]{4,3,2,1,0:T(8,128)(2,1)S(1)}, bf16[3,2,10,32,128]{4,3,2,1,0:T(8,128)(2,1)S(1)}, u32[]{:S(2)}, u32[]{:S(2)}) collective-permute-start(bf16[3,2,10,32,128]{4,3,2,1,0:T(8,128)(2,1)S(1)} %shard_map.71), channel_id=1, source_target_pairs={{0,4},{1,5},{2,6},{3,7},{4,8},{5,9},{6,10},{7,11},{8,12},{9,13},{1... | collective-permute-start | bytes 1474568 | tf_op jit(solution)/shard_map/ppermute | solution.py:25
  118.3 30.2 %collective-permute-start.9 = (bf16[3,2,10,32,128]{4,3,2,1,0:T(8,128)(2,1)S(1)}, bf16[3,2,10,32,128]{4,3,2,1,0:T(8,128)(2,1)S(1)}, u32[]{:S(2)}, u32[]{:S(2)}) collective-permute-start(bf16[3,2,10,32,128]{4,3,2,1,0:T(8,128)(2,1)S(1)} %shard_map.73), channel_id=1, source_target_pairs={{0,12},{1,13},{2,14},{3,15},{4,0},{5,1},{6,2},{7,3},{8,4},{9,5},{1... | collective-permute-start | bytes 1474568 | tf_op jit(solution)/shard_map/ppermute | solution.py:25
  119.8 28.7 %collective-permute-start.12 = (bf16[3,2,10,32,128]{4,3,2,1,0:T(8,128)(2,1)S(1)}, bf16[3,2,10,32,128]{4,3,2,1,0:T(8,128)(2,1)S(1)}, u32[]{:S(2)}, u32[]{:S(2)}) collective-permute-start(bf16[3,2,10,32,128]{4,3,2,1,0:T(8,128)(2,1)S(1)} %shard_map.75), channel_id=1, source_target_pairs={{0,8},{1,9},{2,10},{3,11},{4,12},{5,13},{6,14},{7,15},{8,0},{9,1},... | collective-permute-start | bytes 1474568 | tf_op jit(solution)/shard_map/ppermute | solution.py:25
  121.7 23.1 %collective-permute-start.8 = (bf16[1,2,10,32,128]{4,3,2,1,0:T(8,128)(2,1)S(1)}, bf16[1,2,10,32,128]{4,3,2,1,0:T(8,128)(2,1)S(1)}, u32[]{:S(2)}, u32[]{:S(2)}) collective-permute-start(bf16[1,2,10,32,128]{4,3,2,1,0:T(8,128)(2,1)S(1)} %shard_map.72), channel_id=1, source_target_pairs={{0,12},{1,13},{2,14},{3,15},{4,0},{5,1},{6,2},{7,3},{8,4},{9,5},{1... | collective-permute-start | bytes 491528 | tf_op jit(solution)/shard_map/ppermute | solution.py:25
  123.1 25.3 %collective-permute-start.11 = (bf16[1,2,10,32,128]{4,3,2,1,0:T(8,128)(2,1)S(1)}, bf16[1,2,10,32,128]{4,3,2,1,0:T(8,128)(2,1)S(1)}, u32[]{:S(2)}, u32[]{:S(2)}) collective-permute-start(bf16[1,2,10,32,128]{4,3,2,1,0:T(8,128)(2,1)S(1)} %shard_map.74), channel_id=1, source_target_pairs={{0,8},{1,9},{2,10},{3,11},{4,12},{5,13},{6,14},{7,15},{8,0},{9,1},... | collective-permute-start | bytes 491528 | tf_op jit(solution)/shard_map/ppermute | solution.py:25
  (2 other events, 60.0 us)

commit v6 on v5

--- a/solution.py
+++ b/solution.py
@@ -140,57 +140,117 @@
     )
 
 
-def join_kernel(first, outer, inner, counts, *refs):
-    pieces, (keys, values, sorted_, lined, sems) = refs[: sum(counts)], refs[-5:]
-    groups = sorted_.shape[1]
-    copies = []
-
+def copier(copies, sems):
     def copy(src, dst):
         copies.append(pltpu.make_async_copy(src, dst, sems.at[len(copies)]))
         copies[-1].start()
 
-    at = 0
+    return copy
+
+
+def spot(outer, inner, o, n):
+    place = {outer: sender(outer, HOPS[o]), inner: sender(inner, HOPS[n])}
+    return place["y"], place["x"]
+
+
+def put_values(copy, values, unit, first, y, x):
+    for g in range(unit.shape[0]):
+        to = first + 4 * g
+        rows = pl.ds(pl.multiple_of(x * 32, 32), 32)
+        copy(unit.at[g, 6:10], values.at[to : to + 4, y, rows])
+
+
+def line_keys(lined, sorted_, g):
+    for y in range(SIDE):
+        parts = [sorted_[y * SIDE + x, g] for x in range(SIDE)]
+        for k, part in enumerate(regroup(parts)):
+            lined[g, k, :, 128 * y : 128 * y + 128] = part
+
+
+def sort_keys(sorted_, pieces, outer, inner):
     for o in range(len(HOPS)):
-        mine = pieces[at : at + counts[o]]
-        at += len(mine)
+        mine = [pieces.pop(0) for _ in range(2 if o else 1)]
         units = [p.at[k] for p in mine for k in range(p.shape[0])]
         for n, unit in enumerate(units):
-            place = {outer: sender(outer, HOPS[o]), inner: sender(inner, HOPS[n])}
-            rows = pl.ds(pl.multiple_of(place["x"] * 32, 32), 32)
-            slot = place["y"] * SIDE + place["x"]
-            for g in range(groups):
-                to = first + 4 * g
-                copy(unit.at[g, 6:10], values.at[to : to + 4, place["y"], rows])
-                sorted_[slot, g] = unit[g, 0:6].reshape(192, 128)
-    for g in range(groups):
-        for y in range(SIDE):
-            parts = [sorted_[y * SIDE + x, g] for x in range(SIDE)]
-            for k, part in enumerate(regroup(parts)):
-                lined[g, :, 512 * k + 128 * y : 512 * k + 128 * y + 128] = part
-        at = (first + 4 * g) * 512
-        copy(lined.at[g], keys.at[:, at : at + 2048])
+            y, x = spot(outer, inner, o, n)
+            for g in range(sorted_.shape[1]):
+                sorted_[y * SIDE + x, g] = unit[g, 0:6].reshape(192, 128)
+
+
+def early_kernel(*refs):
+    pieces, values, sems = list(refs[:8]), refs[8], refs[9]
+    copies = []
+    copy = copier(copies, sems)
+    for h, (outer, inner) in enumerate(("xy", "yx")):
+        first = (1 - h) * values.shape[0] // 2
+        for o in range(4):
+            piece = pieces.pop(0)
+            for n in range(piece.shape[0]):
+                put_values(copy, values, piece.at[n], first, *spot(outer, inner, o, n))
     for each in copies:
         each.wait()
 
 
-def join(got, first, outer, inner, before=()):
-    pieces = sum(got, [])
-    groups = got[0][0].shape[1]
-    n = len(pieces)
+def line_kernel(*refs):
+    pieces, lined, sorted_ = list(refs[:-2]), refs[-2], refs[-1]
+    sort_keys(sorted_, pieces, "x", "y")
+    for g in range(lined.shape[0]):
+        line_keys(lined, sorted_, g)
+
+
+def join_kernel(*refs):
+    y_rest, x_pieces, y_lined = refs[:3], list(refs[3:10]), refs[10]
+    keys, values, sorted_, lined, sems = refs[12:]
+    groups = lined.shape[0]
+    copies = []
+    copy = copier(copies, sems)
+    for g in range(groups):
+        for k in range(4):
+            at = (4 * (groups + g) + k) * 512
+            copy(y_lined.at[g, k], keys.at[:, at : at + 512])
+    for (outer, inner), first, rest in (("xy", 4 * groups, y_rest), ("yx", 0, x_pieces[2::2])):
+        for o, piece in enumerate(rest):
+            for n in range(piece.shape[0]):
+                put_values(copy, values, piece.at[n], first, *spot(outer, inner, o + 1, n + 1))
+    sort_keys(sorted_, x_pieces, "y", "x")
+    for g in range(groups):
+        line_keys(lined, sorted_, g)
+        for k in range(4):
+            at = (4 * g + k) * 512
+            copy(lined.at[g, k], keys.at[:, at : at + 512])
+    for each in copies:
+        each.wait()
+
+
+def finish(y_got, x_got):
+    groups = y_got[0][0].shape[1]
+    keys, values = shape(192, 2 * groups * 2048), shape(2 * groups * 4, SIDE, 128, 128)
+    lined = (groups, 4, 192, 512)
+    sorting = VMEM((SIDE * SIDE, groups, 192, 128), BF16)
+    sems = pltpu.SemaphoreType.DMA
+    started = call(
+        early_kernel,
+        values,
+        [p[0] for p in y_got + x_got],
+        out_space=pltpu.HBM,
+        limit=MIB,
+        scratch=[sems((2 * 7 * groups,))],
+        nbytes=2 * MIB,
+    )
+    y_lined = call(
+        line_kernel, shape(*lined), sum(y_got, []), limit=4 * MIB, scratch=[sorting], nbytes=3 * MIB
+    )
+    args = [p[1] for p in y_got[1:]] + sum(x_got, []) + [y_lined, started]
     return call(
-        functools.partial(join_kernel, first, outer, inner, tuple(map(len, got))),
-        (shape(192, 2 * groups * 2048), shape(2 * groups * 4, SIDE, 128, 128)),
-        (*pieces, *before),
-        in_specs=whole(n) + whole(len(before), pltpu.HBM),
+        join_kernel,
+        (keys, values),
+        args,
+        in_specs=whole(len(args) - 1) + whole(1, pltpu.HBM),
         out_space=pltpu.HBM,
-        limit=8 * MIB,
-        scratch=[
-            VMEM((SIDE * SIDE, groups, 192, 128), BF16),
-            VMEM((groups, 192, 2048), BF16),
-            pltpu.SemaphoreType.DMA((groups * (SIDE * SIDE + 1),)),
-        ],
-        alias={n + k: k for k in range(len(before))},
-        nbytes=4 * MIB,
+        limit=6 * MIB,
+        scratch=[sorting, VMEM(lined, BF16), sems((groups * (8 + 18),))],
+        alias={len(args) - 1: 1},
+        nbytes=6 * MIB,
     )
 
 
@@ -218,8 +278,7 @@
         for a in "yx":
             piece = expand(near[a][1:] if i else near[a], heads[OTHER[a]][i])
             got[a][i] = [ahead[a][i], named_move(piece, OTHER[a], i)] if i else [piece]
-    outs = join(got["y"], half, "x", "y")
-    keys, values = join(got["x"], 0, "y", "x", outs)
+    keys, values = finish(got["y"], got["x"])
     return keys[None, None], values.reshape(1, -1, 1, 128)
 
 

time: 152 us -> 131 us (0.86)
  the two profiles are of different devices: /device:TPU:14 before, /device:TPU:1 now
where the time goes in v6:
time: 131 us; the launch traced here: 129 us
  waiting for transfers between devices  66.8 us (51%)
  starting transfers between devices  47.6 us (36%)
  Pallas kernels  13.4 us (10%)
    ppermute x24, waiting for transfers between devices, move(): return lax.ppermute(array, 'tp', pairs)  56.5 us
    ppermute x24, starting transfers between devices, move(): return lax.ppermute(array, 'tp', pairs)  37.5 us
    pallas_call x18, Pallas kernels, call(): pl.pallas_call(kernel, out_shape=outs, in_specs=in_specs or whole(len(arg...  13.4 us
    all_to_all x1, waiting for transfers between devices, shards(): mine = lax.all_to_all(rows, 'seq', split_axis=0, concat_axis=0, tiled=True)  10.3 us
    all_to_all x1, starting transfers between devices, shards(): mine = lax.all_to_all(rows, 'seq', split_axis=0, concat_axis=0, tiled=True)  10.1 us
  transfers between devices with their start and end apart: 25, of which 16 were waited for; matrix products, arithmetic and copies ran while one was open for 0% of the time, Pallas kernels for 6%

profile of v6, /device:TPU:1, one launch (start us, length us, event | category | flops | bytes accessed | tf_op | source)
XLA Modules:
  0.0 128.7 jit_solution(12519718359599901239)
XLA Ops:
  0.6 2.4 %shard_map.68 = (bf16[16,144,128]{2,1,0:T(8,128)(2,1)}, bf16[1024,128]{1,0:T(8,128)(2,1)}) custom-call(bf16[16,32,512]{2,1,0:T(8,128)(2,1)} %lat_in.1, bf16[16,32,64]{2,1,0:T(8,128)(2,1)} %rot_in.1, f32[1,512]{1,0:T(1,128)} %bitcast.8, bf16[512,128]{1,0:T(8,128)(2,1)} %bitcast.6, bf16[512,128]{1,0:T(8,128)(2,1)} %bitcast.7), custom_call_target="tpu_custom_call" | custom-call | bytes 1048576 | tf_op jit(solution)/shard_map/pallas_call | solution.py:43
  3.1 10.1 %all-to-all-start = ((bf16[16,144,128]{2,1,0:T(8,128)(2,1)}), bf16[16,144,128]{2,1,0:T(8,128)(2,1)S(1)}, u32[]{:S(2)}, u32[]{:S(2)}) async-start(bf16[16,144,128]{2,1,0:T(8,128)(2,1)} %get-tuple-element.8), calls=%async_computation | async-start | bytes 1179648 | tf_op jit(solution)/shard_map/all_to_all | solution.py:263
  13.2 2.5 %collective-permute-start = (bf16[1024,128]{1,0:T(8,128)(2,1)}, bf16[1024,128]{1,0:T(8,128)(2,1)S(1)}, u32[]{:S(2)}, u32[]{:S(2)}) collective-permute-start(bf16[1024,128]{1,0:T(8,128)(2,1)} %get-tuple-element.9.refs_4_), channel_id=1, source_target_pairs={{0,3},{1,0},{2,1},{3,2},{4,7},{5,4},{6,5},{7,6},{8,11},{9,8},{10,9... | collective-permute-start | bytes 786440 | tf_op jit(solution)/shard_map/ppermute | solution.py:25
  15.7 5.8 %collective-permute-done.refs_3_.refs_1_ = bf16[1024,128]{1,0:T(8,128)(2,1)S(1)} collective-permute-done((bf16[1024,128]{1,0:T(8,128)(2,1)}, bf16[1024,128]{1,0:T(8,128)(2,1)S(1)}, u32[]{:S(2)}, u32[]{:S(2)}) %collective-permute-start) | collective-permute-done | bytes 262176 | tf_op jit(solution)/shard_map/ppermute | solution.py:25
  21.5 10.3 %all-to-all-done = bf16[16,144,128]{2,1,0:T(8,128)(2,1)S(1)} async-done(((bf16[16,144,128]{2,1,0:T(8,128)(2,1)}), bf16[16,144,128]{2,1,0:T(8,128)(2,1)S(1)}, u32[]{:S(2)}, u32[]{:S(2)}) %all-to-all-start) | async-done | bytes 589856 | tf_op jit(solution)/shard_map/all_to_all | solution.py:263
  31.8 3.0 %collective-permute-start.3 = (bf16[8,144,128]{2,1,0:T(8,128)(2,1)S(1)}, bf16[8,144,128]{2,1,0:T(8,128)(2,1)S(1)}, u32[]{:S(2)}, u32[]{:S(2)}) collective-permute-start(bf16[8,144,128]{2,1,0:T(8,128)(2,1)S(1)} %get-tuple-element.15.refs_0_), channel_id=1, source_target_pairs={{0,8},{1,9},{2,10},{3,11},{4,12},{5,13},{6,14},{7,15},{8,0},{9,1},... | collective-permute-start | bytes 884744 | tf_op jit(solution)/shard_map/ppermute | solution.py:25
  38.2 9.6 %collective-permute-done.18.refs_1_.refs_3_ = bf16[1024,128]{1,0:T(8,128)(2,1)S(1)} collective-permute-done((bf16[1024,128]{1,0:T(8,128)(2,1)S(1)}, bf16[1024,128]{1,0:T(8,128)(2,1)S(1)}, u32[]{:S(2)}, u32[]{:S(2)}) %collective-permute-start.18) | collective-permute-done | bytes 262176 | tf_op jit(solution)/shard_map/ppermute | solution.py:25
  47.8 8.2 %collective-permute-start.12 = (bf16[1024,128]{1,0:T(8,128)(2,1)S(1)}, bf16[1024,128]{1,0:T(8,128)(2,1)S(1)}, u32[]{:S(2)}, u32[]{:S(2)}) collective-permute-start(bf16[1024,128]{1,0:T(8,128)(2,1)S(1)} %copy-done), channel_id=1, source_target_pairs={{0,12},{1,13},{2,14},{3,15},{4,0},{5,1},{6,2},{7,3},{8,4},{9,5},{1... | collective-permute-start | bytes 786440 | tf_op jit(solution)/shard_map/ppermute | solution.py:25
  56.0 2.7 %collective-permute-start.7 = (bf16[1024,128]{1,0:T(8,128)(2,1)S(1)}, bf16[1024,128]{1,0:T(8,128)(2,1)S(1)}, u32[]{:S(2)}, u32[]{:S(2)}) collective-permute-start(bf16[1024,128]{1,0:T(8,128)(2,1)S(1)} %copy-done), channel_id=1, source_target_pairs={{0,2},{1,3},{2,0},{3,1},{4,6},{5,7},{6,4},{7,5},{8,10},{9,11},{10,... | collective-permute-start | bytes 786440 | tf_op jit(solution)/shard_map/ppermute | solution.py:25
  59.9 1.5 %collective-permute-start.4 = (bf16[3,2,10,32,128]{4,3,2,1,0:T(8,128)(2,1)S(1)}, bf16[3,2,10,32,128]{4,3,2,1,0:T(8,128)(2,1)S(1)}, u32[]{:S(2)}, u32[]{:S(2)}) collective-permute-start(bf16[3,2,10,32,128]{4,3,2,1,0:T(8,128)(2,1)S(1)} %shard_map.69), channel_id=1, source_target_pairs={{0,1},{1,2},{2,3},{3,0},{4,5},{5,6},{6,7},{7,4},{8,9},{9,10},{10,1... | collective-permute-start | bytes 1474568 | tf_op jit(solution)/shard_map/ppermute | solution.py:25
  61.8 2.7 %collective-permute-start.11 = (bf16[8,144,128]{2,1,0:T(8,128)(2,1)S(1)}, bf16[8,144,128]{2,1,0:T(8,128)(2,1)S(1)}, u32[]{:S(2)}, u32[]{:S(2)}) collective-permute-start(bf16[8,144,128]{2,1,0:T(8,128)(2,1)S(1)} %get-tuple-element.14.refs_0_), channel_id=1, source_target_pairs={{0,2},{1,3},{2,0},{3,1},{4,6},{5,7},{6,4},{7,5},{8,10},{9,11},{10,... | collective-permute-start | bytes 884744 | tf_op jit(solution)/shard_map/ppermute | solution.py:25
  65.3 2.4 %collective-permute-start.10 = (bf16[8,144,128]{2,1,0:T(8,128)(2,1)S(1)}, bf16[8,144,128]{2,1,0:T(8,128)(2,1)S(1)}, u32[]{:S(2)}, u32[]{:S(2)}) collective-permute-start(bf16[8,144,128]{2,1,0:T(8,128)(2,1)S(1)} %get-tuple-element.14.refs_0_), channel_id=1, source_target_pairs={{0,3},{1,0},{2,1},{3,2},{4,7},{5,4},{6,5},{7,6},{8,11},{9,8},{10,9... | collective-permute-start | bytes 884744 | tf_op jit(solution)/shard_map/ppermute | solution.py:25
  67.7 3.6 %collective-permute-done.5.refs_3_.refs_1_ = bf16[1024,128]{1,0:T(8,128)(2,1)S(1)} collective-permute-done((bf16[1024,128]{1,0:T(8,128)(2,1)S(1)}, bf16[1024,128]{1,0:T(8,128)(2,1)S(1)}, u32[]{:S(2)}, u32[]{:S(2)}) %collective-permute-start.5) | collective-permute-done | bytes 262176 | tf_op jit(solution)/shard_map/ppermute | solution.py:25
  72.5 2.4 %collective-permute-done.21.refs_1_ = bf16[1,2,10,32,128]{4,3,2,1,0:T(8,128)(2,1)S(1)} collective-permute-done((bf16[1,2,10,32,128]{4,3,2,1,0:T(8,128)(2,1)S(1)}, bf16[1,2,10,32,128]{4,3,2,1,0:T(8,128)(2,1)S(1)}, u32[]{:S(2)}, u32[]{:S(2)}) %collective-permute-start.21) | collective-permute-done | bytes 163872 | tf_op jit(solution)/shard_map/ppermute | solution.py:25
  76.1 5.0 %collective-permute-done.22.refs_3_.refs_2_ = bf16[1,2,10,32,128]{4,3,2,1,0:T(8,128)(2,1)S(1)} collective-permute-done((bf16[1,2,10,32,128]{4,3,2,1,0:T(8,128)(2,1)S(1)}, bf16[1,2,10,32,128]{4,3,2,1,0:T(8,128)(2,1)S(1)}, u32[]{:S(2)}, u32[]{:S(2)}) %collective-permute-start.22) | collective-permute-done | bytes 163872 | tf_op jit(solution)/shard_map/ppermute | solution.py:25
  81.2 1.7 %collective-permute-start.23 = (bf16[1,2,10,32,128]{4,3,2,1,0:T(8,128)(2,1)S(1)}, bf16[1,2,10,32,128]{4,3,2,1,0:T(8,128)(2,1)S(1)}, u32[]{:S(2)}, u32[]{:S(2)}) collective-permute-start(bf16[1,2,10,32,128]{4,3,2,1,0:T(8,128)(2,1)S(1)} %shard_map.82), channel_id=1, source_target_pairs={{0,2},{1,3},{2,0},{3,1},{4,6},{5,7},{6,4},{7,5},{8,10},{9,11},{10,... | collective-permute-start | bytes 491528 | tf_op jit(solution)/shard_map/ppermute | solution.py:25
  82.8 8.5 %collective-permute-done.11.refs_3_.refs_2_ = bf16[8,144,128]{2,1,0:T(8,128)(2,1)S(1)} collective-permute-done((bf16[8,144,128]{2,1,0:T(8,128)(2,1)S(1)}, bf16[8,144,128]{2,1,0:T(8,128)(2,1)S(1)}, u32[]{:S(2)}, u32[]{:S(2)}) %collective-permute-start.11) | collective-permute-done | bytes 294944 | tf_op jit(solution)/shard_map/ppermute | solution.py:25
  91.3 2.7 %collective-permute-start.16 = (bf16[1,2,10,32,128]{4,3,2,1,0:T(8,128)(2,1)S(1)}, bf16[1,2,10,32,128]{4,3,2,1,0:T(8,128)(2,1)S(1)}, u32[]{:S(2)}, u32[]{:S(2)}) collective-permute-start(bf16[1,2,10,32,128]{4,3,2,1,0:T(8,128)(2,1)S(1)} %shard_map.75), channel_id=1, source_target_pairs={{0,12},{1,13},{2,14},{3,15},{4,0},{5,1},{6,2},{7,3},{8,4},{9,5},{1... | collective-permute-start | bytes 491528 | tf_op jit(solution)/shard_map/ppermute | solution.py:25
  94.0 4.4 %collective-permute-done.9.refs_1_.refs_0_ = bf16[8,144,128]{2,1,0:T(8,128)(2,1)S(1)} collective-permute-done((bf16[8,144,128]{2,1,0:T(8,128)(2,1)S(1)}, bf16[8,144,128]{2,1,0:T(8,128)(2,1)S(1)}, u32[]{:S(2)}, u32[]{:S(2)}) %collective-permute-start.9) | collective-permute-done | bytes 294944 | tf_op jit(solution)/shard_map/ppermute | solution.py:25
  101.1 2.7 %collective-permute-start.8 = (bf16[3,2,10,32,128]{4,3,2,1,0:T(8,128)(2,1)S(1)}, bf16[3,2,10,32,128]{4,3,2,1,0:T(8,128)(2,1)S(1)}, u32[]{:S(2)}, u32[]{:S(2)}) collective-permute-start(bf16[3,2,10,32,128]{4,3,2,1,0:T(8,128)(2,1)S(1)} %shard_map.71), channel_id=1, source_target_pairs={{0,2},{1,3},{2,0},{3,1},{4,6},{5,7},{6,4},{7,5},{8,10},{9,11},{10,... | collective-permute-start | bytes 1474568 | tf_op jit(solution)/shard_map/ppermute | solution.py:25
  105.1 1.5 %collective-permute-start.17 = (bf16[3,2,10,32,128]{4,3,2,1,0:T(8,128)(2,1)S(1)}, bf16[3,2,10,32,128]{4,3,2,1,0:T(8,128)(2,1)S(1)}, u32[]{:S(2)}, u32[]{:S(2)}) collective-permute-start(bf16[3,2,10,32,128]{4,3,2,1,0:T(8,128)(2,1)S(1)} %shard_map.76), channel_id=1, source_target_pairs={{0,12},{1,13},{2,14},{3,15},{4,0},{5,1},{6,2},{7,3},{8,4},{9,5},{1... | collective-permute-start | bytes 1474568 | tf_op jit(solution)/shard_map/ppermute | solution.py:25
  109.7 3.3 %collective-permute-done.6.refs_4_.refs_1_ = bf16[3,2,10,32,128]{4,3,2,1,0:T(8,128)(2,1)S(1)} collective-permute-done((bf16[3,2,10,32,128]{4,3,2,1,0:T(8,128)(2,1)S(1)}, bf16[3,2,10,32,128]{4,3,2,1,0:T(8,128)(2,1)S(1)}, u32[]{:S(2)}, u32[]{:S(2)}) %collective-permute-start.6) | collective-permute-done | bytes 491552 | tf_op jit(solution)/shard_map/ppermute | solution.py:25
  116.9 8.9 %collective-permute-done.20.refs_9_ = bf16[3,2,10,32,128]{4,3,2,1,0:T(8,128)(2,1)S(1)} collective-permute-done((bf16[3,2,10,32,128]{4,3,2,1,0:T(8,128)(2,1)S(1)}, bf16[3,2,10,32,128]{4,3,2,1,0:T(8,128)(2,1)S(1)}, u32[]{:S(2)}, u32[]{:S(2)}) %collective-permute-start.20) | collective-permute-done | bytes 491552 | tf_op jit(solution)/shard_map/ppermute | solution.py:25
  125.8 2.8 %shard_map.85 = (bf16[192,8192]{1,0:T(8,128)(2,1)}, bf16[16,4,128,128]{3,2,1,0:T(8,128)(2,1)}) custom-call(bf16[3,2,10,32,128]{4,3,2,1,0:T(8,128)(2,1)S(1)} %collective-permute-done.4.refs_2_.refs_0_, bf16[3,2,10,32,128]{4,3,2,1,0:T(8,128)(2,1)S(1)} %collective-permute-done.6.refs_4_.refs_1_, ...), custom_call_target="tpu_custom_call", output_to_operand_aliasing={{1}: (11, {})} | custom-call | bytes 6291456 | tf_op jit(solution)/shard_map/pallas_call | solution.py:43
  (47 shorter events, 19.1 us)
Async XLA Ops:
  3.1 28.7 %all-to-all-start = ((bf16[16,144,128]{2,1,0:T(8,128)(2,1)}), bf16[16,144,128]{2,1,0:T(8,128)(2,1)S(1)}, u32[]{:S(2)}, u32[]{:S(2)}) async-start(bf16[16,144,128]{2,1,0:T(8,128)(2,1)} %get-tuple-element.8), calls=%async_computation | async-start | bytes 1179648 | tf_op jit(solution)/shard_map/all_to_all | solution.py:263
  13.2 8.3 %collective-permute-start = (bf16[1024,128]{1,0:T(8,128)(2,1)}, bf16[1024,128]{1,0:T(8,128)(2,1)S(1)}, u32[]{:S(2)}, u32[]{:S(2)}) collective-permute-start(bf16[1024,128]{1,0:T(8,128)(2,1)} %get-tuple-element.9.refs_4_), channel_id=1, source_target_pairs={{0,3},{1,0},{2,1},{3,2},{4,7},{5,4},{6,5},{7,6},{8,11},{9,8},{10,9... | collective-permute-start | bytes 786440 | tf_op jit(solution)/shard_map/ppermute | solution.py:25
  31.8 24.2 %collective-permute-start.3 = (bf16[8,144,128]{2,1,0:T(8,128)(2,1)S(1)}, bf16[8,144,128]{2,1,0:T(8,128)(2,1)S(1)}, u32[]{:S(2)}, u32[]{:S(2)}) collective-permute-start(bf16[8,144,128]{2,1,0:T(8,128)(2,1)S(1)} %get-tuple-element.15.refs_0_), channel_id=1, source_target_pairs={{0,8},{1,9},{2,10},{3,11},{4,12},{5,13},{6,14},{7,15},{8,0},{9,1},... | collective-permute-start | bytes 884744 | tf_op jit(solution)/shard_map/ppermute | solution.py:25
  34.8 23.9 %collective-permute-start.2 = (bf16[8,144,128]{2,1,0:T(8,128)(2,1)S(1)}, bf16[8,144,128]{2,1,0:T(8,128)(2,1)S(1)}, u32[]{:S(2)}, u32[]{:S(2)}) collective-permute-start(bf16[8,144,128]{2,1,0:T(8,128)(2,1)S(1)} %get-tuple-element.15.refs_0_), channel_id=1, source_target_pairs={{0,12},{1,13},{2,14},{3,15},{4,0},{5,1},{6,2},{7,3},{8,4},{9,5},{1... | collective-permute-start | bytes 884744 | tf_op jit(solution)/shard_map/ppermute | solution.py:25
  35.6 12.2 %collective-permute-start.18 = (bf16[1024,128]{1,0:T(8,128)(2,1)S(1)}, bf16[1024,128]{1,0:T(8,128)(2,1)S(1)}, u32[]{:S(2)}, u32[]{:S(2)}) collective-permute-start(bf16[1024,128]{1,0:T(8,128)(2,1)S(1)} %copy-done), channel_id=1, source_target_pairs={{0,8},{1,9},{2,10},{3,11},{4,12},{5,13},{6,14},{7,15},{8,0},{9,1},... | collective-permute-start | bytes 786440 | tf_op jit(solution)/shard_map/ppermute | solution.py:25
  37.0 22.4 %collective-permute-start.1 = (bf16[8,144,128]{2,1,0:T(8,128)(2,1)S(1)}, bf16[8,144,128]{2,1,0:T(8,128)(2,1)S(1)}, u32[]{:S(2)}, u32[]{:S(2)}) collective-permute-start(bf16[8,144,128]{2,1,0:T(8,128)(2,1)S(1)} %get-tuple-element.15.refs_0_), channel_id=1, source_target_pairs={{0,4},{1,5},{2,6},{3,7},{4,8},{5,9},{6,10},{7,11},{8,12},{9,13},{1... | collective-permute-start | bytes 884744 | tf_op jit(solution)/shard_map/ppermute | solution.py:25
  37.0 22.9 %collective-permute-start.15 = (bf16[1024,128]{1,0:T(8,128)(2,1)S(1)}, bf16[1024,128]{1,0:T(8,128)(2,1)S(1)}, u32[]{:S(2)}, u32[]{:S(2)}) collective-permute-start(bf16[1024,128]{1,0:T(8,128)(2,1)S(1)} %copy-done), channel_id=1, source_target_pairs={{0,4},{1,5},{2,6},{3,7},{4,8},{5,9},{6,10},{7,11},{8,12},{9,13},{1... | collective-permute-start | bytes 786440 | tf_op jit(solution)/shard_map/ppermute | solution.py:25
  47.8 14.0 %collective-permute-start.12 = (bf16[1024,128]{1,0:T(8,128)(2,1)S(1)}, bf16[1024,128]{1,0:T(8,128)(2,1)S(1)}, u32[]{:S(2)}, u32[]{:S(2)}) collective-permute-start(bf16[1024,128]{1,0:T(8,128)(2,1)S(1)} %copy-done), channel_id=1, source_target_pairs={{0,12},{1,13},{2,14},{3,15},{4,0},{5,1},{6,2},{7,3},{8,4},{9,5},{1... | collective-permute-start | bytes 786440 | tf_op jit(solution)/shard_map/ppermute | solution.py:25
  56.0 9.3 %collective-permute-start.7 = (bf16[1024,128]{1,0:T(8,128)(2,1)S(1)}, bf16[1024,128]{1,0:T(8,128)(2,1)S(1)}, u32[]{:S(2)}, u32[]{:S(2)}) collective-permute-start(bf16[1024,128]{1,0:T(8,128)(2,1)S(1)} %copy-done), channel_id=1, source_target_pairs={{0,2},{1,3},{2,0},{3,1},{4,6},{5,7},{6,4},{7,5},{8,10},{9,11},{10,... | collective-permute-start | bytes 786440 | tf_op jit(solution)/shard_map/ppermute | solution.py:25
  58.7 12.6 %collective-permute-start.5 = (bf16[1024,128]{1,0:T(8,128)(2,1)S(1)}, bf16[1024,128]{1,0:T(8,128)(2,1)S(1)}, u32[]{:S(2)}, u32[]{:S(2)}) collective-permute-start(bf16[1024,128]{1,0:T(8,128)(2,1)S(1)} %copy-done), channel_id=1, source_target_pairs={{0,1},{1,2},{2,3},{3,0},{4,5},{5,6},{6,7},{7,4},{8,9},{9,10},{10,1... | collective-permute-start | bytes 786440 | tf_op jit(solution)/shard_map/ppermute | solution.py:25
  59.4 15.5 %collective-permute-start.21 = (bf16[1,2,10,32,128]{4,3,2,1,0:T(8,128)(2,1)S(1)}, bf16[1,2,10,32,128]{4,3,2,1,0:T(8,128)(2,1)S(1)}, u32[]{:S(2)}, u32[]{:S(2)}) collective-permute-start(bf16[1,2,10,32,128]{4,3,2,1,0:T(8,128)(2,1)S(1)} %shard_map.80), channel_id=1, source_target_pairs={{0,1},{1,2},{2,3},{3,0},{4,5},{5,6},{6,7},{7,4},{8,9},{9,10},{10,1... | collective-permute-start | bytes 491528 | tf_op jit(solution)/shard_map/ppermute | solution.py:25
  59.9 46.7 %collective-permute-start.4 = (bf16[3,2,10,32,128]{4,3,2,1,0:T(8,128)(2,1)S(1)}, bf16[3,2,10,32,128]{4,3,2,1,0:T(8,128)(2,1)S(1)}, u32[]{:S(2)}, u32[]{:S(2)}) collective-permute-start(bf16[3,2,10,32,128]{4,3,2,1,0:T(8,128)(2,1)S(1)} %shard_map.69), channel_id=1, source_target_pairs={{0,1},{1,2},{2,3},{3,0},{4,5},{5,6},{6,7},{7,4},{8,9},{9,10},{10,1... | collective-permute-start | bytes 1474568 | tf_op jit(solution)/shard_map/ppermute | solution.py:25
  61.8 29.5 %collective-permute-start.11 = (bf16[8,144,128]{2,1,0:T(8,128)(2,1)S(1)}, bf16[8,144,128]{2,1,0:T(8,128)(2,1)S(1)}, u32[]{:S(2)}, u32[]{:S(2)}) collective-permute-start(bf16[8,144,128]{2,1,0:T(8,128)(2,1)S(1)} %get-tuple-element.14.refs_0_), channel_id=1, source_target_pairs={{0,2},{1,3},{2,0},{3,1},{4,6},{5,7},{6,4},{7,5},{8,10},{9,11},{10,... | collective-permute-start | bytes 884744 | tf_op jit(solution)/shard_map/ppermute | solution.py:25
  65.3 26.0 %collective-permute-start.10 = (bf16[8,144,128]{2,1,0:T(8,128)(2,1)S(1)}, bf16[8,144,128]{2,1,0:T(8,128)(2,1)S(1)}, u32[]{:S(2)}, u32[]{:S(2)}) collective-permute-start(bf16[8,144,128]{2,1,0:T(8,128)(2,1)S(1)} %get-tuple-element.14.refs_0_), channel_id=1, source_target_pairs={{0,3},{1,0},{2,1},{3,2},{4,7},{5,4},{6,5},{7,6},{8,11},{9,8},{10,9... | collective-permute-start | bytes 884744 | tf_op jit(solution)/shard_map/ppermute | solution.py:25
  71.3 27.1 %collective-permute-start.9 = (bf16[8,144,128]{2,1,0:T(8,128)(2,1)S(1)}, bf16[8,144,128]{2,1,0:T(8,128)(2,1)S(1)}, u32[]{:S(2)}, u32[]{:S(2)}) collective-permute-start(bf16[8,144,128]{2,1,0:T(8,128)(2,1)S(1)} %get-tuple-element.14.refs_0_), channel_id=1, source_target_pairs={{0,1},{1,2},{2,3},{3,0},{4,5},{5,6},{6,7},{7,4},{8,9},{9,10},{10,1... | collective-permute-start | bytes 884744 | tf_op jit(solution)/shard_map/ppermute | solution.py:25
  81.2 20.0 %collective-permute-start.23 = (bf16[1,2,10,32,128]{4,3,2,1,0:T(8,128)(2,1)S(1)}, bf16[1,2,10,32,128]{4,3,2,1,0:T(8,128)(2,1)S(1)}, u32[]{:S(2)}, u32[]{:S(2)}) collective-permute-start(bf16[1,2,10,32,128]{4,3,2,1,0:T(8,128)(2,1)S(1)} %shard_map.82), channel_id=1, source_target_pairs={{0,2},{1,3},{2,0},{3,1},{4,6},{5,7},{6,4},{7,5},{8,10},{9,11},{10,... | collective-permute-start | bytes 491528 | tf_op jit(solution)/shard_map/ppermute | solution.py:25
  91.3 9.8 %collective-permute-start.13 = (bf16[1,2,10,32,128]{4,3,2,1,0:T(8,128)(2,1)S(1)}, bf16[1,2,10,32,128]{4,3,2,1,0:T(8,128)(2,1)S(1)}, u32[]{:S(2)}, u32[]{:S(2)}) collective-permute-start(bf16[1,2,10,32,128]{4,3,2,1,0:T(8,128)(2,1)S(1)} %shard_map.73), channel_id=1, source_target_pairs={{0,4},{1,5},{2,6},{3,7},{4,8},{5,9},{6,10},{7,11},{8,12},{9,13},{1... | collective-permute-start | bytes 491528 | tf_op jit(solution)/shard_map/ppermute | solution.py:25
  91.3 12.6 %collective-permute-start.16 = (bf16[1,2,10,32,128]{4,3,2,1,0:T(8,128)(2,1)S(1)}, bf16[1,2,10,32,128]{4,3,2,1,0:T(8,128)(2,1)S(1)}, u32[]{:S(2)}, u32[]{:S(2)}) collective-permute-start(bf16[1,2,10,32,128]{4,3,2,1,0:T(8,128)(2,1)S(1)} %shard_map.75), channel_id=1, source_target_pairs={{0,12},{1,13},{2,14},{3,15},{4,0},{5,1},{6,2},{7,3},{8,4},{9,5},{1... | collective-permute-start | bytes 491528 | tf_op jit(solution)/shard_map/ppermute | solution.py:25
  98.4 6.7 %collective-permute-start.19 = (bf16[1,2,10,32,128]{4,3,2,1,0:T(8,128)(2,1)S(1)}, bf16[1,2,10,32,128]{4,3,2,1,0:T(8,128)(2,1)S(1)}, u32[]{:S(2)}, u32[]{:S(2)}) collective-permute-start(bf16[1,2,10,32,128]{4,3,2,1,0:T(8,128)(2,1)S(1)} %shard_map.77), channel_id=1, source_target_pairs={{0,8},{1,9},{2,10},{3,11},{4,12},{5,13},{6,14},{7,15},{8,0},{9,1},... | collective-permute-start | bytes 491528 | tf_op jit(solution)/shard_map/ppermute | solution.py:25
  101.1 11.8 %collective-permute-start.6 = (bf16[3,2,10,32,128]{4,3,2,1,0:T(8,128)(2,1)S(1)}, bf16[3,2,10,32,128]{4,3,2,1,0:T(8,128)(2,1)S(1)}, u32[]{:S(2)}, u32[]{:S(2)}) collective-permute-start(bf16[3,2,10,32,128]{4,3,2,1,0:T(8,128)(2,1)S(1)} %shard_map.70), channel_id=1, source_target_pairs={{0,3},{1,0},{2,1},{3,2},{4,7},{5,4},{6,5},{7,6},{8,11},{9,8},{10,9... | collective-permute-start | bytes 1474568 | tf_op jit(solution)/shard_map/ppermute | solution.py:25
  101.1 12.9 %collective-permute-start.8 = (bf16[3,2,10,32,128]{4,3,2,1,0:T(8,128)(2,1)S(1)}, bf16[3,2,10,32,128]{4,3,2,1,0:T(8,128)(2,1)S(1)}, u32[]{:S(2)}, u32[]{:S(2)}) collective-permute-start(bf16[3,2,10,32,128]{4,3,2,1,0:T(8,128)(2,1)S(1)} %shard_map.71), channel_id=1, source_target_pairs={{0,2},{1,3},{2,0},{3,1},{4,6},{5,7},{6,4},{7,5},{8,10},{9,11},{10,... | collective-permute-start | bytes 1474568 | tf_op jit(solution)/shard_map/ppermute | solution.py:25
  103.9 13.0 %collective-permute-start.14 = (bf16[3,2,10,32,128]{4,3,2,1,0:T(8,128)(2,1)S(1)}, bf16[3,2,10,32,128]{4,3,2,1,0:T(8,128)(2,1)S(1)}, u32[]{:S(2)}, u32[]{:S(2)}) collective-permute-start(bf16[3,2,10,32,128]{4,3,2,1,0:T(8,128)(2,1)S(1)} %shard_map.74), channel_id=1, source_target_pairs={{0,4},{1,5},{2,6},{3,7},{4,8},{5,9},{6,10},{7,11},{8,12},{9,13},{1... | collective-permute-start | bytes 1474568 | tf_op jit(solution)/shard_map/ppermute | solution.py:25
  105.1 11.8 %collective-permute-start.17 = (bf16[3,2,10,32,128]{4,3,2,1,0:T(8,128)(2,1)S(1)}, bf16[3,2,10,32,128]{4,3,2,1,0:T(8,128)(2,1)S(1)}, u32[]{:S(2)}, u32[]{:S(2)}) collective-permute-start(bf16[3,2,10,32,128]{4,3,2,1,0:T(8,128)(2,1)S(1)} %shard_map.76), channel_id=1, source_target_pairs={{0,12},{1,13},{2,14},{3,15},{4,0},{5,1},{6,2},{7,3},{8,4},{9,5},{1... | collective-permute-start | bytes 1474568 | tf_op jit(solution)/shard_map/ppermute | solution.py:25
  106.6 19.2 %collective-permute-start.20 = (bf16[3,2,10,32,128]{4,3,2,1,0:T(8,128)(2,1)S(1)}, bf16[3,2,10,32,128]{4,3,2,1,0:T(8,128)(2,1)S(1)}, u32[]{:S(2)}, u32[]{:S(2)}) collective-permute-start(bf16[3,2,10,32,128]{4,3,2,1,0:T(8,128)(2,1)S(1)} %shard_map.78), channel_id=1, source_target_pairs={{0,8},{1,9},{2,10},{3,11},{4,12},{5,13},{6,14},{7,15},{8,0},{9,1},... | collective-permute-start | bytes 1474568 | tf_op jit(solution)/shard_map/ppermute | solution.py:25
  (2 other events, 38.8 us)

commit v7 on v6

--- a/solution.py
+++ b/solution.py
@@ -112,9 +112,8 @@
     )
 
 
-def expand_kernel(n, *refs):
-    rows, head, out = refs[:n], refs[n], refs[n + 1]
-    w = jnp.concatenate([head[0:512, :], head[512:1024, :]], axis=-1)
+def expand_kernel(n, m, *refs):
+    rows, heads, outs = refs[:n], refs[n : n + m], refs[n + m :]
     for i in range(n):
         a = rows[i]
         for g in range(a.shape[0] // 4):
@@ -122,22 +121,25 @@
             lhs = jnp.concatenate(
                 [four[:, 32 * j : 32 * j + 32].reshape(128, 128) for j in range(4)], axis=-1
             )
-            wide = jnp.dot(lhs, w, preferred_element_type=jnp.float32).astype(BF16)
-            out[i, g, 0:4] = wide[:, 0:128].T.reshape(4, 32, 128)
             turned = jnp.concatenate(regroup([four[k, 128:144] for k in range(4)]), axis=0)
-            out[i, g, 4:6] = turned.reshape(2, 32, 128)
-            out[i, g, 6:10] = wide[:, 128:256].reshape(4, 32, 128)
-
-
-def expand(rows, head):
-    n, s = len(rows), rows[0].shape[0]
-    return call(
-        functools.partial(expand_kernel, n),
-        shape(n, s // 4, 10, 32, 128),
-        (*rows, head),
+            for head, out in zip(heads, outs):
+                w = jnp.concatenate([head[0:512, :], head[512:1024, :]], axis=-1)
+                wide = jnp.dot(lhs, w, preferred_element_type=jnp.float32).astype(BF16)
+                out[i, g, 0:4] = wide[:, 0:128].T.reshape(4, 32, 128)
+                out[i, g, 4:6] = turned.reshape(2, 32, 128)
+                out[i, g, 6:10] = wide[:, 128:256].reshape(4, 32, 128)
+
+
+def expand(rows, heads):
+    n, m, s = len(rows), len(heads), rows[0].shape[0]
+    outs = call(
+        functools.partial(expand_kernel, n, m),
+        (shape(n, s // 4, 10, 32, 128),) * m,
+        (*rows, *heads),
         limit=4 * MIB,
-        flops=n * s * 32 * 512 * 256 * 2,
-    )
+        flops=m * n * s * 32 * 512 * 256 * 2,
+    )
+    return list(outs)
 
 
 def copier(copies, sems):
@@ -177,8 +179,23 @@
                 sorted_[y * SIDE + x, g] = unit[g, 0:6].reshape(192, 128)
 
 
+def put_keys(copy, keys, lined, o, g):
+    y = sender("y", HOPS[o])
+    for k in range(4):
+        lanes = pl.ds(pl.multiple_of((4 * g + k) * 512 + y * 128, 128), 128)
+        copy(lined.at[k], keys.at[:, lanes])
+
+
+def line_row(sorted_, lined, units, g):
+    for n, unit in enumerate(units):
+        sorted_[sender("x", HOPS[n])] = unit[g, 0:6].reshape(192, 128)
+    for k, part in enumerate(regroup([sorted_[x] for x in range(SIDE)])):
+        lined[k] = part
+
+
 def early_kernel(*refs):
-    pieces, values, sems = list(refs[:8]), refs[8], refs[9]
+    pieces, (keys, values, sorted_, lined, sems) = list(refs[:8]), refs[8:]
+    local = pieces[4]
     copies = []
     copy = copier(copies, sems)
     for h, (outer, inner) in enumerate(("xy", "yx")):
@@ -187,6 +204,9 @@
             piece = pieces.pop(0)
             for n in range(piece.shape[0]):
                 put_values(copy, values, piece.at[n], first, *spot(outer, inner, o, n))
+    for g in range(local.shape[1]):
+        line_row(sorted_.at[g], lined.at[g], [local.at[n] for n in range(4)], g)
+        put_keys(copy, keys, lined.at[g], 0, g)
     for each in copies:
         each.wait()
 
@@ -199,25 +219,25 @@
 
 
 def join_kernel(*refs):
-    y_rest, x_pieces, y_lined = refs[:3], list(refs[3:10]), refs[10]
+    y_rest, x_pieces, y_lined = refs[:3], refs[3:9], refs[9]
     keys, values, sorted_, lined, sems = refs[12:]
-    groups = lined.shape[0]
+    groups = y_lined.shape[0]
     copies = []
     copy = copier(copies, sems)
     for g in range(groups):
         for k in range(4):
             at = (4 * (groups + g) + k) * 512
             copy(y_lined.at[g, k], keys.at[:, at : at + 512])
-    for (outer, inner), first, rest in (("xy", 4 * groups, y_rest), ("yx", 0, x_pieces[2::2])):
+    for (outer, inner), first, rest in (("xy", 4 * groups, y_rest), ("yx", 0, x_pieces[1::2])):
         for o, piece in enumerate(rest):
             for n in range(piece.shape[0]):
                 put_values(copy, values, piece.at[n], first, *spot(outer, inner, o + 1, n + 1))
-    sort_keys(sorted_, x_pieces, "y", "x")
-    for g in range(groups):
-        line_keys(lined, sorted_, g)
-        for k in range(4):
-            at = (4 * g + k) * 512
-            copy(lined.at[g, k], keys.at[:, at : at + 512])
+    for o in (3, 1, 2):
+        own, rest = x_pieces[2 * o - 2], x_pieces[2 * o - 1]
+        units = [own.at[0]] + [rest.at[n] for n in range(3)]
+        for g in range(groups):
+            line_row(sorted_.at[o - 1, g], lined.at[o - 1, g], units, g)
+            put_keys(copy, keys, lined.at[o - 1, g], o, g)
     for each in copies:
         each.wait()
 
@@ -225,31 +245,35 @@
 def finish(y_got, x_got):
     groups = y_got[0][0].shape[1]
     keys, values = shape(192, 2 * groups * 2048), shape(2 * groups * 4, SIDE, 128, 128)
-    lined = (groups, 4, 192, 512)
-    sorting = VMEM((SIDE * SIDE, groups, 192, 128), BF16)
+    block = (groups, 4, 192, 128)
     sems = pltpu.SemaphoreType.DMA
     started = call(
         early_kernel,
-        values,
+        (keys, values),
         [p[0] for p in y_got + x_got],
         out_space=pltpu.HBM,
-        limit=MIB,
-        scratch=[sems((2 * 7 * groups,))],
+        limit=2 * MIB,
+        scratch=[VMEM(block, BF16), VMEM(block, BF16), sems((groups * (14 + 4),))],
         nbytes=2 * MIB,
     )
     y_lined = call(
-        line_kernel, shape(*lined), sum(y_got, []), limit=4 * MIB, scratch=[sorting], nbytes=3 * MIB
-    )
-    args = [p[1] for p in y_got[1:]] + sum(x_got, []) + [y_lined, started]
+        line_kernel,
+        shape(groups, 4, 192, 512),
+        sum(y_got, []),
+        limit=4 * MIB,
+        scratch=[VMEM((SIDE * SIDE, groups, 192, 128), BF16)],
+        nbytes=3 * MIB,
+    )
+    args = [p[1] for p in y_got[1:]] + sum(x_got[1:], []) + [y_lined, *started]
     return call(
         join_kernel,
         (keys, values),
         args,
-        in_specs=whole(len(args) - 1) + whole(1, pltpu.HBM),
+        in_specs=whole(len(args) - 2) + whole(2, pltpu.HBM),
         out_space=pltpu.HBM,
         limit=6 * MIB,
-        scratch=[sorting, VMEM(lined, BF16), sems((groups * (8 + 18),))],
-        alias={len(args) - 1: 1},
+        scratch=[VMEM((3, *block), BF16), VMEM((3, *block), BF16), sems((groups * (4 + 18 + 12),))],
+        alias={len(args) - 2: 0, len(args) - 1: 1},
         nbytes=6 * MIB,
     )
 
@@ -270,13 +294,14 @@
             near[a].append(named_move(near[a][0], a, i))
     got = {"x": [None] * 4, "y": [None] * 4}
     ahead = {"x": [None] * 4, "y": [None] * 4}
+    for a in "yx":
+        ahead[a][1:] = expand(near[a][:1], heads[OTHER[a]][1:])
     for i in (3, 1, 2):
         for a in "yx":
-            ahead[a][i] = expand(near[a][:1], heads[OTHER[a]][i])
             ahead[a][i] = named_move(ahead[a][i], OTHER[a], i)
     for i in (3, 1, 2, 0):
         for a in "yx":
-            piece = expand(near[a][1:] if i else near[a], heads[OTHER[a]][i])
+            (piece,) = expand(near[a][1:] if i else near[a], heads[OTHER[a]][i : i + 1])
             got[a][i] = [ahead[a][i], named_move(piece, OTHER[a], i)] if i else [piece]
     keys, values = finish(got["y"], got["x"])
     return keys[None, None], values.reshape(1, -1, 1, 128)

time: 131 us -> 115 us (0.88)
  the two profiles are of different devices: /device:TPU:1 before, /device:TPU:24 now
where the time goes in v7:
time: 115 us; the launch traced here: 114 us
  waiting for transfers between devices  52.6 us (46%)
  starting transfers between devices  48.5 us (42%)
  Pallas kernels  12.5 us (11%)
    ppermute x24, waiting for transfers between devices, move(): return lax.ppermute(array, 'tp', pairs)  44.7 us
    ppermute x24, starting transfers between devices, move(): return lax.ppermute(array, 'tp', pairs)  39.8 us
    pallas_call x14, Pallas kernels, call(): pl.pallas_call(kernel, out_shape=outs, in_specs=in_specs or whole(len(arg...  12.5 us
    all_to_all x1, starting transfers between devices, shards(): mine = lax.all_to_all(rows, 'seq', split_axis=0, concat_axis=0, tiled=True)  8.71 us
    all_to_all x1, waiting for transfers between devices, shards(): mine = lax.all_to_all(rows, 'seq', split_axis=0, concat_axis=0, tiled=True)  7.9 us
  transfers between devices with their start and end apart: 25, of which 11 were waited for; matrix products, arithmetic and copies ran while one was open for 0% of the time, Pallas kernels for 6%

profile of v7, /device:TPU:24, one launch (start us, length us, event | category | flops | bytes accessed | tf_op | source)
XLA Modules:
  0.0 114.5 jit_solution(17709510237841767257)
XLA Ops:
  0.6 2.4 %shard_map.68 = (bf16[16,144,128]{2,1,0:T(8,128)(2,1)}, bf16[1024,128]{1,0:T(8,128)(2,1)}) custom-call(bf16[16,32,512]{2,1,0:T(8,128)(2,1)} %lat_in.1, bf16[16,32,64]{2,1,0:T(8,128)(2,1)} %rot_in.1, f32[1,512]{1,0:T(1,128)} %bitcast.9, bf16[512,128]{1,0:T(8,128)(2,1)} %bitcast.7, bf16[512,128]{1,0:T(8,128)(2,1)} %bitcast.8), custom_call_target="tpu_custom_call" | custom-call | bytes 1048576 | tf_op jit(solution)/shard_map/pallas_call | solution.py:43
  3.1 8.7 %all-to-all-start = ((bf16[16,144,128]{2,1,0:T(8,128)(2,1)}), bf16[16,144,128]{2,1,0:T(8,128)(2,1)S(1)}, u32[]{:S(2)}, u32[]{:S(2)}) async-start(bf16[16,144,128]{2,1,0:T(8,128)(2,1)} %get-tuple-element.16), calls=%async_computation | async-start | bytes 1179648 | tf_op jit(solution)/shard_map/all_to_all | solution.py:287
  11.8 2.8 %collective-permute-start = (bf16[1024,128]{1,0:T(8,128)(2,1)}, bf16[1024,128]{1,0:T(8,128)(2,1)S(1)}, u32[]{:S(2)}, u32[]{:S(2)}) collective-permute-start(bf16[1024,128]{1,0:T(8,128)(2,1)} %get-tuple-element.17.refs_4_), channel_id=1, source_target_pairs={{0,3},{1,0},{2,1},{3,2},{4,7},{5,4},{6,5},{7,6},{8,11},{9,8},{10,9... | collective-permute-start | bytes 786440 | tf_op jit(solution)/shard_map/ppermute | solution.py:25
  14.7 6.4 %collective-permute-done.refs_3_.refs_1_ = bf16[1024,128]{1,0:T(8,128)(2,1)S(1)} collective-permute-done((bf16[1024,128]{1,0:T(8,128)(2,1)}, bf16[1024,128]{1,0:T(8,128)(2,1)S(1)}, u32[]{:S(2)}, u32[]{:S(2)}) %collective-permute-start) | collective-permute-done | bytes 262176 | tf_op jit(solution)/shard_map/ppermute | solution.py:25
  21.0 7.9 %all-to-all-done = bf16[16,144,128]{2,1,0:T(8,128)(2,1)S(1)} async-done(((bf16[16,144,128]{2,1,0:T(8,128)(2,1)}), bf16[16,144,128]{2,1,0:T(8,128)(2,1)S(1)}, u32[]{:S(2)}, u32[]{:S(2)}) %all-to-all-start) | async-done | bytes 589856 | tf_op jit(solution)/shard_map/all_to_all | solution.py:287
  30.3 3.0 %collective-permute-start.7 = (bf16[1024,128]{1,0:T(8,128)(2,1)S(1)}, bf16[1024,128]{1,0:T(8,128)(2,1)S(1)}, u32[]{:S(2)}, u32[]{:S(2)}) collective-permute-start(bf16[1024,128]{1,0:T(8,128)(2,1)S(1)} %copy-done), channel_id=1, source_target_pairs={{0,2},{1,3},{2,0},{3,1},{4,6},{5,7},{6,4},{7,5},{8,10},{9,11},{10,... | collective-permute-start | bytes 786440 | tf_op jit(solution)/shard_map/ppermute | solution.py:25
  33.9 3.2 %collective-permute-start.1 = (bf16[8,144,128]{2,1,0:T(8,128)(2,1)S(1)}, bf16[8,144,128]{2,1,0:T(8,128)(2,1)S(1)}, u32[]{:S(2)}, u32[]{:S(2)}) collective-permute-start(bf16[8,144,128]{2,1,0:T(8,128)(2,1)S(1)} %get-tuple-element.31.refs_0_), channel_id=1, source_target_pairs={{0,4},{1,5},{2,6},{3,7},{4,8},{5,9},{6,10},{7,11},{8,12},{9,13},{1... | collective-permute-start | bytes 884744 | tf_op jit(solution)/shard_map/ppermute | solution.py:25
  37.2 3.3 %collective-permute-done.7.refs_3_ = bf16[1024,128]{1,0:T(8,128)(2,1)S(1)} collective-permute-done((bf16[1024,128]{1,0:T(8,128)(2,1)S(1)}, bf16[1024,128]{1,0:T(8,128)(2,1)S(1)}, u32[]{:S(2)}, u32[]{:S(2)}) %collective-permute-start.7) | collective-permute-done | bytes 262176 | tf_op jit(solution)/shard_map/ppermute | solution.py:25
  40.5 2.3 %collective-permute-start.11 = (bf16[1024,128]{1,0:T(8,128)(2,1)S(1)}, bf16[1024,128]{1,0:T(8,128)(2,1)S(1)}, u32[]{:S(2)}, u32[]{:S(2)}) collective-permute-start(bf16[1024,128]{1,0:T(8,128)(2,1)S(1)} %copy-done), channel_id=1, source_target_pairs={{0,8},{1,9},{2,10},{3,11},{4,12},{5,13},{6,14},{7,15},{8,0},{9,1},... | collective-permute-start | bytes 786440 | tf_op jit(solution)/shard_map/ppermute | solution.py:25
  42.8 3.8 %collective-permute-done.5.refs_3_.refs_2_ = bf16[1024,128]{1,0:T(8,128)(2,1)S(1)} collective-permute-done((bf16[1024,128]{1,0:T(8,128)(2,1)S(1)}, bf16[1024,128]{1,0:T(8,128)(2,1)S(1)}, u32[]{:S(2)}, u32[]{:S(2)}) %collective-permute-start.5) | collective-permute-done | bytes 262176 | tf_op jit(solution)/shard_map/ppermute | solution.py:25
  46.6 2.2 %collective-permute-start.10 = (bf16[1024,128]{1,0:T(8,128)(2,1)S(1)}, bf16[1024,128]{1,0:T(8,128)(2,1)S(1)}, u32[]{:S(2)}, u32[]{:S(2)}) collective-permute-start(bf16[1024,128]{1,0:T(8,128)(2,1)S(1)} %copy-done), channel_id=1, source_target_pairs={{0,4},{1,5},{2,6},{3,7},{4,8},{5,9},{6,10},{7,11},{8,12},{9,13},{1... | collective-permute-start | bytes 786440 | tf_op jit(solution)/shard_map/ppermute | solution.py:25
  51.5 3.1 %collective-permute-start.15 = (bf16[8,144,128]{2,1,0:T(8,128)(2,1)S(1)}, bf16[8,144,128]{2,1,0:T(8,128)(2,1)S(1)}, u32[]{:S(2)}, u32[]{:S(2)}) collective-permute-start(bf16[8,144,128]{2,1,0:T(8,128)(2,1)S(1)} %get-tuple-element.30.refs_0_), channel_id=1, source_target_pairs={{0,2},{1,3},{2,0},{3,1},{4,6},{5,7},{6,4},{7,5},{8,10},{9,11},{10,... | collective-permute-start | bytes 884744 | tf_op jit(solution)/shard_map/ppermute | solution.py:25
  56.3 2.1 %collective-permute-start.14 = (bf16[8,144,128]{2,1,0:T(8,128)(2,1)S(1)}, bf16[8,144,128]{2,1,0:T(8,128)(2,1)S(1)}, u32[]{:S(2)}, u32[]{:S(2)}) collective-permute-start(bf16[8,144,128]{2,1,0:T(8,128)(2,1)S(1)} %get-tuple-element.30.refs_0_), channel_id=1, source_target_pairs={{0,3},{1,0},{2,1},{3,2},{4,7},{5,4},{6,5},{7,6},{8,11},{9,8},{10,9... | collective-permute-start | bytes 884744 | tf_op jit(solution)/shard_map/ppermute | solution.py:25
  59.8 1.9 %collective-permute-start.22 = (bf16[1,2,10,32,128]{4,3,2,1,0:T(8,128)(2,1)S(1)}, bf16[1,2,10,32,128]{4,3,2,1,0:T(8,128)(2,1)S(1)}, u32[]{:S(2)}, u32[]{:S(2)}) collective-permute-start(bf16[1,2,10,32,128]{4,3,2,1,0:T(8,128)(2,1)S(1)} %get-tuple-element.24), channel_id=1, source_target_pairs={{0,3},{1,0},{2,1},{3,2},{4,7},{5,4},{6,5},{7,6},{8,11},{9,8},{10,9... | collective-permute-start | bytes 491528 | tf_op jit(solution)/shard_map/ppermute | solution.py:25
  62.2 10.3 %collective-permute-done.22.refs_3_.refs_2_ = bf16[1,2,10,32,128]{4,3,2,1,0:T(8,128)(2,1)S(1)} collective-permute-done((bf16[1,2,10,32,128]{4,3,2,1,0:T(8,128)(2,1)S(1)}, bf16[1,2,10,32,128]{4,3,2,1,0:T(8,128)(2,1)S(1)}, u32[]{:S(2)}, u32[]{:S(2)}) %collective-permute-start.22) | collective-permute-done | bytes 163872 | tf_op jit(solution)/shard_map/ppermute | solution.py:25
  72.5 2.2 %collective-permute-start.23 = (bf16[1,2,10,32,128]{4,3,2,1,0:T(8,128)(2,1)S(1)}, bf16[1,2,10,32,128]{4,3,2,1,0:T(8,128)(2,1)S(1)}, u32[]{:S(2)}, u32[]{:S(2)}) collective-permute-start(bf16[1,2,10,32,128]{4,3,2,1,0:T(8,128)(2,1)S(1)} %get-tuple-element.25), channel_id=1, source_target_pairs={{0,2},{1,3},{2,0},{3,1},{4,6},{5,7},{6,4},{7,5},{8,10},{9,11},{10,... | collective-permute-start | bytes 491528 | tf_op jit(solution)/shard_map/ppermute | solution.py:25
  74.7 2.2 %collective-permute-start.12 = (bf16[1,2,10,32,128]{4,3,2,1,0:T(8,128)(2,1)S(1)}, bf16[1,2,10,32,128]{4,3,2,1,0:T(8,128)(2,1)S(1)}, u32[]{:S(2)}, u32[]{:S(2)}) collective-permute-start(bf16[1,2,10,32,128]{4,3,2,1,0:T(8,128)(2,1)S(1)} %get-tuple-element.20), channel_id=1, source_target_pairs={{0,4},{1,5},{2,6},{3,7},{4,8},{5,9},{6,10},{7,11},{8,12},{9,13},{1... | collective-permute-start | bytes 491528 | tf_op jit(solution)/shard_map/ppermute | solution.py:25
  76.9 6.3 %collective-permute-done.13.refs_0_.refs_1_ = bf16[8,144,128]{2,1,0:T(8,128)(2,1)S(1)} collective-permute-done((bf16[8,144,128]{2,1,0:T(8,128)(2,1)S(1)}, bf16[8,144,128]{2,1,0:T(8,128)(2,1)S(1)}, u32[]{:S(2)}, u32[]{:S(2)}) %collective-permute-start.13) | collective-permute-done | bytes 294944 | tf_op jit(solution)/shard_map/ppermute | solution.py:25
  83.2 1.8 %collective-permute-start.19 = (bf16[1,2,10,32,128]{4,3,2,1,0:T(8,128)(2,1)S(1)}, bf16[1,2,10,32,128]{4,3,2,1,0:T(8,128)(2,1)S(1)}, u32[]{:S(2)}, u32[]{:S(2)}) collective-permute-start(bf16[1,2,10,32,128]{4,3,2,1,0:T(8,128)(2,1)S(1)} %get-tuple-element.22), channel_id=1, source_target_pairs={{0,8},{1,9},{2,10},{3,11},{4,12},{5,13},{6,14},{7,15},{8,0},{9,1},... | collective-permute-start | bytes 491528 | tf_op jit(solution)/shard_map/ppermute | solution.py:25
  90.2 1.8 %collective-permute-start.18 = (bf16[3,2,10,32,128]{4,3,2,1,0:T(8,128)(2,1)S(1)}, bf16[3,2,10,32,128]{4,3,2,1,0:T(8,128)(2,1)S(1)}, u32[]{:S(2)}, u32[]{:S(2)}) collective-permute-start(bf16[3,2,10,32,128]{4,3,2,1,0:T(8,128)(2,1)S(1)} %shard_map.74), channel_id=1, source_target_pairs={{0,12},{1,13},{2,14},{3,15},{4,0},{5,1},{6,2},{7,3},{8,4},{9,5},{1... | collective-permute-start | bytes 1474568 | tf_op jit(solution)/shard_map/ppermute | solution.py:25
  92.1 4.1 %collective-permute-start.20 = (bf16[3,2,10,32,128]{4,3,2,1,0:T(8,128)(2,1)S(1)}, bf16[3,2,10,32,128]{4,3,2,1,0:T(8,128)(2,1)S(1)}, u32[]{:S(2)}, u32[]{:S(2)}) collective-permute-start(bf16[3,2,10,32,128]{4,3,2,1,0:T(8,128)(2,1)S(1)} %shard_map.75), channel_id=1, source_target_pairs={{0,8},{1,9},{2,10},{3,11},{4,12},{5,13},{6,14},{7,15},{8,0},{9,1},... | collective-permute-start | bytes 1474568 | tf_op jit(solution)/shard_map/ppermute | solution.py:25
  98.7 3.8 %collective-permute-done.6.refs_4_.refs_1_ = bf16[3,2,10,32,128]{4,3,2,1,0:T(8,128)(2,1)S(1)} collective-permute-done((bf16[3,2,10,32,128]{4,3,2,1,0:T(8,128)(2,1)S(1)}, bf16[3,2,10,32,128]{4,3,2,1,0:T(8,128)(2,1)S(1)}, u32[]{:S(2)}, u32[]{:S(2)}) %collective-permute-start.6) | collective-permute-done | bytes 491552 | tf_op jit(solution)/shard_map/ppermute | solution.py:25
  103.9 7.8 %collective-permute-done.18.refs_6_ = bf16[3,2,10,32,128]{4,3,2,1,0:T(8,128)(2,1)S(1)} collective-permute-done((bf16[3,2,10,32,128]{4,3,2,1,0:T(8,128)(2,1)S(1)}, bf16[3,2,10,32,128]{4,3,2,1,0:T(8,128)(2,1)S(1)}, u32[]{:S(2)}, u32[]{:S(2)}) %collective-permute-start.18) | collective-permute-done | bytes 491552 | tf_op jit(solution)/shard_map/ppermute | solution.py:25
  111.7 2.6 %shard_map.81 = (bf16[192,8192]{1,0:T(8,128)(2,1)}, bf16[16,4,128,128]{3,2,1,0:T(8,128)(2,1)}) custom-call(bf16[3,2,10,32,128]{4,3,2,1,0:T(8,128)(2,1)S(1)} %collective-permute-done.4.refs_2_.refs_0_, bf16[3,2,10,32,128]{4,3,2,1,0:T(8,128)(2,1)S(1)} %collective-permute-done.6.refs_4_.refs_1_, ...), custom_call_target="tpu_custom_call", output_to_operand_aliasing={{0}: (10, {}), {1}: (11, {})} | custom-call | bytes 6291456 | tf_op jit(solution)/shard_map/pallas_call | solution.py:43
  (43 shorter events, 17.3 us)
Async XLA Ops:
  3.1 25.8 %all-to-all-start = ((bf16[16,144,128]{2,1,0:T(8,128)(2,1)}), bf16[16,144,128]{2,1,0:T(8,128)(2,1)S(1)}, u32[]{:S(2)}, u32[]{:S(2)}) async-start(bf16[16,144,128]{2,1,0:T(8,128)(2,1)} %get-tuple-element.16), calls=%async_computation | async-start | bytes 1179648 | tf_op jit(solution)/shard_map/all_to_all | solution.py:287
  11.8 9.2 %collective-permute-start = (bf16[1024,128]{1,0:T(8,128)(2,1)}, bf16[1024,128]{1,0:T(8,128)(2,1)S(1)}, u32[]{:S(2)}, u32[]{:S(2)}) collective-permute-start(bf16[1024,128]{1,0:T(8,128)(2,1)} %get-tuple-element.17.refs_4_), channel_id=1, source_target_pairs={{0,3},{1,0},{2,1},{3,2},{4,7},{5,4},{6,5},{7,6},{8,11},{9,8},{10,9... | collective-permute-start | bytes 786440 | tf_op jit(solution)/shard_map/ppermute | solution.py:25
  29.0 19.8 %collective-permute-start.3 = (bf16[8,144,128]{2,1,0:T(8,128)(2,1)S(1)}, bf16[8,144,128]{2,1,0:T(8,128)(2,1)S(1)}, u32[]{:S(2)}, u32[]{:S(2)}) collective-permute-start(bf16[8,144,128]{2,1,0:T(8,128)(2,1)S(1)} %get-tuple-element.31.refs_0_), channel_id=1, source_target_pairs={{0,8},{1,9},{2,10},{3,11},{4,12},{5,13},{6,14},{7,15},{8,0},{9,1},... | collective-permute-start | bytes 884744 | tf_op jit(solution)/shard_map/ppermute | solution.py:25
  30.3 10.2 %collective-permute-start.7 = (bf16[1024,128]{1,0:T(8,128)(2,1)S(1)}, bf16[1024,128]{1,0:T(8,128)(2,1)S(1)}, u32[]{:S(2)}, u32[]{:S(2)}) collective-permute-start(bf16[1024,128]{1,0:T(8,128)(2,1)S(1)} %copy-done), channel_id=1, source_target_pairs={{0,2},{1,3},{2,0},{3,1},{4,6},{5,7},{6,4},{7,5},{8,10},{9,11},{10,... | collective-permute-start | bytes 786440 | tf_op jit(solution)/shard_map/ppermute | solution.py:25
  33.3 13.3 %collective-permute-start.5 = (bf16[1024,128]{1,0:T(8,128)(2,1)S(1)}, bf16[1024,128]{1,0:T(8,128)(2,1)S(1)}, u32[]{:S(2)}, u32[]{:S(2)}) collective-permute-start(bf16[1024,128]{1,0:T(8,128)(2,1)S(1)} %copy-done), channel_id=1, source_target_pairs={{0,1},{1,2},{2,3},{3,0},{4,5},{5,6},{6,7},{7,4},{8,9},{9,10},{10,1... | collective-permute-start | bytes 786440 | tf_op jit(solution)/shard_map/ppermute | solution.py:25
  33.9 15.3 %collective-permute-start.2 = (bf16[8,144,128]{2,1,0:T(8,128)(2,1)S(1)}, bf16[8,144,128]{2,1,0:T(8,128)(2,1)S(1)}, u32[]{:S(2)}, u32[]{:S(2)}) collective-permute-start(bf16[8,144,128]{2,1,0:T(8,128)(2,1)S(1)} %get-tuple-element.31.refs_0_), channel_id=1, source_target_pairs={{0,12},{1,13},{2,14},{3,15},{4,0},{5,1},{6,2},{7,3},{8,4},{9,5},{1... | collective-permute-start | bytes 884744 | tf_op jit(solution)/shard_map/ppermute | solution.py:25
  33.9 16.4 %collective-permute-start.1 = (bf16[8,144,128]{2,1,0:T(8,128)(2,1)S(1)}, bf16[8,144,128]{2,1,0:T(8,128)(2,1)S(1)}, u32[]{:S(2)}, u32[]{:S(2)}) collective-permute-start(bf16[8,144,128]{2,1,0:T(8,128)(2,1)S(1)} %get-tuple-element.31.refs_0_), channel_id=1, source_target_pairs={{0,4},{1,5},{2,6},{3,7},{4,8},{5,9},{6,10},{7,11},{8,12},{9,13},{1... | collective-permute-start | bytes 884744 | tf_op jit(solution)/shard_map/ppermute | solution.py:25
  40.5 11.0 %collective-permute-start.11 = (bf16[1024,128]{1,0:T(8,128)(2,1)S(1)}, bf16[1024,128]{1,0:T(8,128)(2,1)S(1)}, u32[]{:S(2)}, u32[]{:S(2)}) collective-permute-start(bf16[1024,128]{1,0:T(8,128)(2,1)S(1)} %copy-done), channel_id=1, source_target_pairs={{0,8},{1,9},{2,10},{3,11},{4,12},{5,13},{6,14},{7,15},{8,0},{9,1},... | collective-permute-start | bytes 786440 | tf_op jit(solution)/shard_map/ppermute | solution.py:25
  46.6 9.7 %collective-permute-start.10 = (bf16[1024,128]{1,0:T(8,128)(2,1)S(1)}, bf16[1024,128]{1,0:T(8,128)(2,1)S(1)}, u32[]{:S(2)}, u32[]{:S(2)}) collective-permute-start(bf16[1024,128]{1,0:T(8,128)(2,1)S(1)} %copy-done), channel_id=1, source_target_pairs={{0,4},{1,5},{2,6},{3,7},{4,8},{5,9},{6,10},{7,11},{8,12},{9,13},{1... | collective-permute-start | bytes 786440 | tf_op jit(solution)/shard_map/ppermute | solution.py:25
  48.8 9.7 %collective-permute-start.9 = (bf16[1024,128]{1,0:T(8,128)(2,1)S(1)}, bf16[1024,128]{1,0:T(8,128)(2,1)S(1)}, u32[]{:S(2)}, u32[]{:S(2)}) collective-permute-start(bf16[1024,128]{1,0:T(8,128)(2,1)S(1)} %copy-done), channel_id=1, source_target_pairs={{0,12},{1,13},{2,14},{3,15},{4,0},{5,1},{6,2},{7,3},{8,4},{9,5},{1... | collective-permute-start | bytes 786440 | tf_op jit(solution)/shard_map/ppermute | solution.py:25
  49.2 10.6 %collective-permute-start.21 = (bf16[1,2,10,32,128]{4,3,2,1,0:T(8,128)(2,1)S(1)}, bf16[1,2,10,32,128]{4,3,2,1,0:T(8,128)(2,1)S(1)}, u32[]{:S(2)}, u32[]{:S(2)}) collective-permute-start(bf16[1,2,10,32,128]{4,3,2,1,0:T(8,128)(2,1)S(1)} %get-tuple-element.23), channel_id=1, source_target_pairs={{0,1},{1,2},{2,3},{3,0},{4,5},{5,6},{6,7},{7,4},{8,9},{9,10},{10,1... | collective-permute-start | bytes 491528 | tf_op jit(solution)/shard_map/ppermute | solution.py:25
  50.8 41.3 %collective-permute-start.4 = (bf16[3,2,10,32,128]{4,3,2,1,0:T(8,128)(2,1)S(1)}, bf16[3,2,10,32,128]{4,3,2,1,0:T(8,128)(2,1)S(1)}, u32[]{:S(2)}, u32[]{:S(2)}) collective-permute-start(bf16[3,2,10,32,128]{4,3,2,1,0:T(8,128)(2,1)S(1)} %shard_map.69), channel_id=1, source_target_pairs={{0,1},{1,2},{2,3},{3,0},{4,5},{5,6},{6,7},{7,4},{8,9},{9,10},{10,1... | collective-permute-start | bytes 1474568 | tf_op jit(solution)/shard_map/ppermute | solution.py:25
  51.5 23.2 %collective-permute-start.15 = (bf16[8,144,128]{2,1,0:T(8,128)(2,1)S(1)}, bf16[8,144,128]{2,1,0:T(8,128)(2,1)S(1)}, u32[]{:S(2)}, u32[]{:S(2)}) collective-permute-start(bf16[8,144,128]{2,1,0:T(8,128)(2,1)S(1)} %get-tuple-element.30.refs_0_), channel_id=1, source_target_pairs={{0,2},{1,3},{2,0},{3,1},{4,6},{5,7},{6,4},{7,5},{8,10},{9,11},{10,... | collective-permute-start | bytes 884744 | tf_op jit(solution)/shard_map/ppermute | solution.py:25
  56.3 20.6 %collective-permute-start.14 = (bf16[8,144,128]{2,1,0:T(8,128)(2,1)S(1)}, bf16[8,144,128]{2,1,0:T(8,128)(2,1)S(1)}, u32[]{:S(2)}, u32[]{:S(2)}) collective-permute-start(bf16[8,144,128]{2,1,0:T(8,128)(2,1)S(1)} %get-tuple-element.30.refs_0_), channel_id=1, source_target_pairs={{0,3},{1,0},{2,1},{3,2},{4,7},{5,4},{6,5},{7,6},{8,11},{9,8},{10,9... | collective-permute-start | bytes 884744 | tf_op jit(solution)/shard_map/ppermute | solution.py:25
  58.5 24.7 %collective-permute-start.13 = (bf16[8,144,128]{2,1,0:T(8,128)(2,1)S(1)}, bf16[8,144,128]{2,1,0:T(8,128)(2,1)S(1)}, u32[]{:S(2)}, u32[]{:S(2)}) collective-permute-start(bf16[8,144,128]{2,1,0:T(8,128)(2,1)S(1)} %get-tuple-element.30.refs_0_), channel_id=1, source_target_pairs={{0,1},{1,2},{2,3},{3,0},{4,5},{5,6},{6,7},{7,4},{8,9},{9,10},{10,1... | collective-permute-start | bytes 884744 | tf_op jit(solution)/shard_map/ppermute | solution.py:25
  59.8 12.7 %collective-permute-start.22 = (bf16[1,2,10,32,128]{4,3,2,1,0:T(8,128)(2,1)S(1)}, bf16[1,2,10,32,128]{4,3,2,1,0:T(8,128)(2,1)S(1)}, u32[]{:S(2)}, u32[]{:S(2)}) collective-permute-start(bf16[1,2,10,32,128]{4,3,2,1,0:T(8,128)(2,1)S(1)} %get-tuple-element.24), channel_id=1, source_target_pairs={{0,3},{1,0},{2,1},{3,2},{4,7},{5,4},{6,5},{7,6},{8,11},{9,8},{10,9... | collective-permute-start | bytes 491528 | tf_op jit(solution)/shard_map/ppermute | solution.py:25
  72.5 14.7 %collective-permute-start.23 = (bf16[1,2,10,32,128]{4,3,2,1,0:T(8,128)(2,1)S(1)}, bf16[1,2,10,32,128]{4,3,2,1,0:T(8,128)(2,1)S(1)}, u32[]{:S(2)}, u32[]{:S(2)}) collective-permute-start(bf16[1,2,10,32,128]{4,3,2,1,0:T(8,128)(2,1)S(1)} %get-tuple-element.25), channel_id=1, source_target_pairs={{0,2},{1,3},{2,0},{3,1},{4,6},{5,7},{6,4},{7,5},{8,10},{9,11},{10,... | collective-permute-start | bytes 491528 | tf_op jit(solution)/shard_map/ppermute | solution.py:25
  74.7 13.7 %collective-permute-start.12 = (bf16[1,2,10,32,128]{4,3,2,1,0:T(8,128)(2,1)S(1)}, bf16[1,2,10,32,128]{4,3,2,1,0:T(8,128)(2,1)S(1)}, u32[]{:S(2)}, u32[]{:S(2)}) collective-permute-start(bf16[1,2,10,32,128]{4,3,2,1,0:T(8,128)(2,1)S(1)} %get-tuple-element.20), channel_id=1, source_target_pairs={{0,4},{1,5},{2,6},{3,7},{4,8},{5,9},{6,10},{7,11},{8,12},{9,13},{1... | collective-permute-start | bytes 491528 | tf_op jit(solution)/shard_map/ppermute | solution.py:25
  76.9 11.5 %collective-permute-start.17 = (bf16[1,2,10,32,128]{4,3,2,1,0:T(8,128)(2,1)S(1)}, bf16[1,2,10,32,128]{4,3,2,1,0:T(8,128)(2,1)S(1)}, u32[]{:S(2)}, u32[]{:S(2)}) collective-permute-start(bf16[1,2,10,32,128]{4,3,2,1,0:T(8,128)(2,1)S(1)} %get-tuple-element.21), channel_id=1, source_target_pairs={{0,12},{1,13},{2,14},{3,15},{4,0},{5,1},{6,2},{7,3},{8,4},{9,5},{1... | collective-permute-start | bytes 491528 | tf_op jit(solution)/shard_map/ppermute | solution.py:25
  87.2 16.7 %collective-permute-start.16 = (bf16[3,2,10,32,128]{4,3,2,1,0:T(8,128)(2,1)S(1)}, bf16[3,2,10,32,128]{4,3,2,1,0:T(8,128)(2,1)S(1)}, u32[]{:S(2)}, u32[]{:S(2)}) collective-permute-start(bf16[3,2,10,32,128]{4,3,2,1,0:T(8,128)(2,1)S(1)} %shard_map.73), channel_id=1, source_target_pairs={{0,4},{1,5},{2,6},{3,7},{4,8},{5,9},{6,10},{7,11},{8,12},{9,13},{1... | collective-permute-start | bytes 1474568 | tf_op jit(solution)/shard_map/ppermute | solution.py:25
  88.4 14.0 %collective-permute-start.6 = (bf16[3,2,10,32,128]{4,3,2,1,0:T(8,128)(2,1)S(1)}, bf16[3,2,10,32,128]{4,3,2,1,0:T(8,128)(2,1)S(1)}, u32[]{:S(2)}, u32[]{:S(2)}) collective-permute-start(bf16[3,2,10,32,128]{4,3,2,1,0:T(8,128)(2,1)S(1)} %shard_map.70), channel_id=1, source_target_pairs={{0,3},{1,0},{2,1},{3,2},{4,7},{5,4},{6,5},{7,6},{8,11},{9,8},{10,9... | collective-permute-start | bytes 1474568 | tf_op jit(solution)/shard_map/ppermute | solution.py:25
  88.4 14.0 %collective-permute-start.8 = (bf16[3,2,10,32,128]{4,3,2,1,0:T(8,128)(2,1)S(1)}, bf16[3,2,10,32,128]{4,3,2,1,0:T(8,128)(2,1)S(1)}, u32[]{:S(2)}, u32[]{:S(2)}) collective-permute-start(bf16[3,2,10,32,128]{4,3,2,1,0:T(8,128)(2,1)S(1)} %shard_map.71), channel_id=1, source_target_pairs={{0,2},{1,3},{2,0},{3,1},{4,6},{5,7},{6,4},{7,5},{8,10},{9,11},{10,... | collective-permute-start | bytes 1474568 | tf_op jit(solution)/shard_map/ppermute | solution.py:25
  90.2 21.5 %collective-permute-start.18 = (bf16[3,2,10,32,128]{4,3,2,1,0:T(8,128)(2,1)S(1)}, bf16[3,2,10,32,128]{4,3,2,1,0:T(8,128)(2,1)S(1)}, u32[]{:S(2)}, u32[]{:S(2)}) collective-permute-start(bf16[3,2,10,32,128]{4,3,2,1,0:T(8,128)(2,1)S(1)} %shard_map.74), channel_id=1, source_target_pairs={{0,12},{1,13},{2,14},{3,15},{4,0},{5,1},{6,2},{7,3},{8,4},{9,5},{1... | collective-permute-start | bytes 1474568 | tf_op jit(solution)/shard_map/ppermute | solution.py:25
  92.1 19.7 %collective-permute-start.20 = (bf16[3,2,10,32,128]{4,3,2,1,0:T(8,128)(2,1)S(1)}, bf16[3,2,10,32,128]{4,3,2,1,0:T(8,128)(2,1)S(1)}, u32[]{:S(2)}, u32[]{:S(2)}) collective-permute-start(bf16[3,2,10,32,128]{4,3,2,1,0:T(8,128)(2,1)S(1)} %shard_map.75), channel_id=1, source_target_pairs={{0,8},{1,9},{2,10},{3,11},{4,12},{5,13},{6,14},{7,15},{8,0},{9,1},... | collective-permute-start | bytes 1474568 | tf_op jit(solution)/shard_map/ppermute | solution.py:25
  (2 other events, 34.3 us)

commit v8 on v7

--- a/solution.py
+++ b/solution.py
@@ -52,11 +52,18 @@
     )(*args)
 
 
+def run_all(copies):
+    for copy in copies:
+        copy.start()
+    for copy in copies:
+        copy.wait()
+
+
 def regroup(parts):
     return [jnp.concatenate([p[:, 32 * k : 32 * k + 32] for p in parts], axis=-1) for k in range(4)]
 
 
-def ready_kernel(lat_in, rot_in, gain_in, key_in, value_in, rows, weights, lat, rot, gain, sems):
+def ready_kernel(lat_in, rot_in, gain_in, rows, lat, rot, gain, sems):
     copies = [
         pltpu.make_async_copy(src, dst, sems.at[i])
         for i, (src, dst) in enumerate(
@@ -64,8 +71,6 @@
                 (lat_in, lat),
                 (gain_in, gain),
                 (rot_in, rot),
-                (key_in, weights.at[0:512, :]),
-                (value_in, weights.at[512:1024, :]),
             )
         )
     ]
@@ -91,24 +96,43 @@
             parts = [turned[64 * k + 16 * d : 64 * k + 16 * d + 16] for d in range(4)]
             for q, part in enumerate(regroup(parts)):
                 rows[b + q + 4 * k, 128:144, :] = part
-    copies[3].wait()
-    copies[4].wait()
-
-
-def ready(latents, rotary, gain, key_up, value_up):
+
+
+def ready(latents, rotary, gain):
     b = latents.shape[0]
     return call(
         ready_kernel,
-        (shape(b, 144, 128), shape(1024, 128)),
-        (latents, rotary, gain.reshape(1, -1), key_up.reshape(512, 128), value_up.reshape(512, 128)),
-        in_specs=whole(5, pltpu.HBM),
+        shape(b, 144, 128),
+        (latents, rotary, gain.reshape(1, -1)),
+        in_specs=whole(3, pltpu.HBM),
         limit=67043328,
         scratch=[
             VMEM(latents.shape, BF16),
             VMEM(rotary.shape, BF16),
             VMEM((1, 512), jnp.float32),
-            pltpu.SemaphoreType.DMA((5,)),
+            pltpu.SemaphoreType.DMA((3,)),
         ],
+    )
+
+
+def stack_kernel(key_in, value_in, after, weights, sems):
+    del after
+    run_all(
+        [
+            pltpu.make_async_copy(key_in, weights.at[0:512, :], sems.at[0]),
+            pltpu.make_async_copy(value_in, weights.at[512:1024, :], sems.at[1]),
+        ]
+    )
+
+
+def stack(key_up, value_up, after):
+    return call(
+        stack_kernel,
+        shape(1024, 128),
+        (key_up.reshape(512, 128), value_up.reshape(512, 128), after),
+        in_specs=whole(3, pltpu.HBM),
+        limit=60 * MIB,
+        scratch=[pltpu.SemaphoreType.DMA((2,))],
     )
 
 
@@ -283,7 +307,8 @@
 
 
 def shards(latents, rotary_rows, latent_gain, key_up, value_up):
-    rows, head = ready(latents, rotary_rows, latent_gain, key_up, value_up)
+    rows = ready(latents, rotary_rows, latent_gain)
+    head = stack(key_up, value_up, rows)
     mine = lax.all_to_all(rows, "seq", split_axis=0, concat_axis=0, tiled=True)
     heads = {a: [head] + [named_move(head, a, i, back=True) for i in (1, 2, 3)] for a in "xy"}
     mine, heads["x"][1] = lax.optimization_barrier((mine, heads["x"][1]))

time: 115 us -> 115 us (level)
  waiting for transfers between devices: 52.6 us -> 50.8 us
  Pallas kernels: 12.5 us -> 14.1 us
    all_to_all x1, waiting for transfers between devices: 7.9 us -> 6.13 us  [shards(): mine = lax.all_to_all(rows, 'seq', split_axis=0, concat_axis=0, tiled=True)]
    pallas_call x14 -> x15, Pallas kernels: 12.5 us -> 14.1 us  [call(): pl.pallas_call(kernel, out_shape=outs, in_specs=in_specs or whole(len(arg...]
  transfers between devices with their start and end apart: 25 -> 25, of which waited for: 11 -> 10; matrix products, arithmetic and copies ran while one was open for 0% -> 0% of each run, Pallas kernels for 6% -> 8%
where the time goes in v8:
time: 115 us; the launch traced here: 114 us
  waiting for transfers between devices  50.8 us (44%)
  starting transfers between devices  48.6 us (42%)
  Pallas kernels  14.1 us (12%)
    ppermute x24, waiting for transfers between devices, move(): return lax.ppermute(array, 'tp', pairs)  44.7 us
    ppermute x24, starting transfers between devices, move(): return lax.ppermute(array, 'tp', pairs)  40 us
    pallas_call x15, Pallas kernels, call(): pl.pallas_call(kernel, out_shape=outs, in_specs=in_specs or whole(len(arg...  14.1 us
    all_to_all x1, starting transfers between devices, shards(): mine = lax.all_to_all(rows, 'seq', split_axis=0, concat_axis=0, tiled=True)  8.58 us
    all_to_all x1, waiting for transfers between devices, shards(): mine = lax.all_to_all(rows, 'seq', split_axis=0, concat_axis=0, tiled=True)  6.13 us
  transfers between devices with their start and end apart: 25, of which 10 were waited for; matrix products, arithmetic and copies ran while one was open for 0% of the time, Pallas kernels for 8%

profile of v8, /device:TPU:24, one launch (start us, length us, event | category | flops | bytes accessed | tf_op | source)
XLA Modules:
  0.0 114.5 jit_solution(6653154228250525474)
XLA Ops:
  0.6 2.3 %shard_map.68.after = bf16[16,144,128]{2,1,0:T(8,128)(2,1)} custom-call(bf16[16,32,512]{2,1,0:T(8,128)(2,1)} %lat_in.1, bf16[16,32,64]{2,1,0:T(8,128)(2,1)} %rot_in.1, f32[1,512]{1,0:T(1,128)} %bitcast.9), custom_call_target="tpu_custom_call" | custom-call | bytes 1048576 | tf_op jit(solution)/shard_map/pallas_call | solution.py:43
  3.0 8.6 %all-to-all-start = ((bf16[16,144,128]{2,1,0:T(8,128)(2,1)}), bf16[16,144,128]{2,1,0:T(8,128)(2,1)S(1)}, u32[]{:S(2)}, u32[]{:S(2)}) async-start(bf16[16,144,128]{2,1,0:T(8,128)(2,1)} %shard_map.68.after), calls=%async_computation | async-start | bytes 1179648 | tf_op jit(solution)/shard_map/all_to_all | solution.py:312
  13.3 2.8 %collective-permute-start = (bf16[1024,128]{1,0:T(8,128)(2,1)}, bf16[1024,128]{1,0:T(8,128)(2,1)S(1)}, u32[]{:S(2)}, u32[]{:S(2)}) collective-permute-start(bf16[1024,128]{1,0:T(8,128)(2,1)} %shard_map.69.refs_4_), channel_id=1, source_target_pairs={{0,3},{1,0},{2,1},{3,2},{4,7},{5,4},{6,5},{7,6},{8,11},{9,8},{10,9... | collective-permute-start | bytes 786440 | tf_op jit(solution)/shard_map/ppermute | solution.py:25
  16.1 6.5 %collective-permute-done.refs_3_.refs_1_ = bf16[1024,128]{1,0:T(8,128)(2,1)S(1)} collective-permute-done((bf16[1024,128]{1,0:T(8,128)(2,1)}, bf16[1024,128]{1,0:T(8,128)(2,1)S(1)}, u32[]{:S(2)}, u32[]{:S(2)}) %collective-permute-start) | collective-permute-done | bytes 262176 | tf_op jit(solution)/shard_map/ppermute | solution.py:25
  22.6 6.1 %all-to-all-done = bf16[16,144,128]{2,1,0:T(8,128)(2,1)S(1)} async-done(((bf16[16,144,128]{2,1,0:T(8,128)(2,1)}), bf16[16,144,128]{2,1,0:T(8,128)(2,1)S(1)}, u32[]{:S(2)}, u32[]{:S(2)}) %all-to-all-start) | async-done | bytes 589856 | tf_op jit(solution)/shard_map/all_to_all | solution.py:312
  30.1 3.0 %collective-permute-start.7 = (bf16[1024,128]{1,0:T(8,128)(2,1)}, bf16[1024,128]{1,0:T(8,128)(2,1)S(1)}, u32[]{:S(2)}, u32[]{:S(2)}) collective-permute-start(bf16[1024,128]{1,0:T(8,128)(2,1)} %shard_map.69.refs_4_), channel_id=1, source_target_pairs={{0,2},{1,3},{2,0},{3,1},{4,6},{5,7},{6,4},{7,5},{8,10},{9,11},{10,... | collective-permute-start | bytes 786440 | tf_op jit(solution)/shard_map/ppermute | solution.py:25
  33.7 3.2 %collective-permute-start.1 = (bf16[8,144,128]{2,1,0:T(8,128)(2,1)S(1)}, bf16[8,144,128]{2,1,0:T(8,128)(2,1)S(1)}, u32[]{:S(2)}, u32[]{:S(2)}) collective-permute-start(bf16[8,144,128]{2,1,0:T(8,128)(2,1)S(1)} %get-tuple-element.27.refs_0_), channel_id=1, source_target_pairs={{0,4},{1,5},{2,6},{3,7},{4,8},{5,9},{6,10},{7,11},{8,12},{9,13},{1... | collective-permute-start | bytes 884744 | tf_op jit(solution)/shard_map/ppermute | solution.py:25
  36.9 3.6 %collective-permute-done.7.refs_3_ = bf16[1024,128]{1,0:T(8,128)(2,1)S(1)} collective-permute-done((bf16[1024,128]{1,0:T(8,128)(2,1)}, bf16[1024,128]{1,0:T(8,128)(2,1)S(1)}, u32[]{:S(2)}, u32[]{:S(2)}) %collective-permute-start.7) | collective-permute-done | bytes 262176 | tf_op jit(solution)/shard_map/ppermute | solution.py:25
  40.5 2.3 %collective-permute-start.11 = (bf16[1024,128]{1,0:T(8,128)(2,1)}, bf16[1024,128]{1,0:T(8,128)(2,1)S(1)}, u32[]{:S(2)}, u32[]{:S(2)}) collective-permute-start(bf16[1024,128]{1,0:T(8,128)(2,1)} %shard_map.69.refs_4_), channel_id=1, source_target_pairs={{0,8},{1,9},{2,10},{3,11},{4,12},{5,13},{6,14},{7,15},{8,0},{9,1},... | collective-permute-start | bytes 786440 | tf_op jit(solution)/shard_map/ppermute | solution.py:25
  42.8 3.8 %collective-permute-done.5.refs_3_.refs_2_ = bf16[1024,128]{1,0:T(8,128)(2,1)S(1)} collective-permute-done((bf16[1024,128]{1,0:T(8,128)(2,1)}, bf16[1024,128]{1,0:T(8,128)(2,1)S(1)}, u32[]{:S(2)}, u32[]{:S(2)}) %collective-permute-start.5) | collective-permute-done | bytes 262176 | tf_op jit(solution)/shard_map/ppermute | solution.py:25
  46.5 2.2 %collective-permute-start.10 = (bf16[1024,128]{1,0:T(8,128)(2,1)}, bf16[1024,128]{1,0:T(8,128)(2,1)S(1)}, u32[]{:S(2)}, u32[]{:S(2)}) collective-permute-start(bf16[1024,128]{1,0:T(8,128)(2,1)} %shard_map.69.refs_4_), channel_id=1, source_target_pairs={{0,4},{1,5},{2,6},{3,7},{4,8},{5,9},{6,10},{7,11},{8,12},{9,13},{1... | collective-permute-start | bytes 786440 | tf_op jit(solution)/shard_map/ppermute | solution.py:25
  51.4 3.1 %collective-permute-start.15 = (bf16[8,144,128]{2,1,0:T(8,128)(2,1)S(1)}, bf16[8,144,128]{2,1,0:T(8,128)(2,1)S(1)}, u32[]{:S(2)}, u32[]{:S(2)}) collective-permute-start(bf16[8,144,128]{2,1,0:T(8,128)(2,1)S(1)} %get-tuple-element.26.refs_0_), channel_id=1, source_target_pairs={{0,2},{1,3},{2,0},{3,1},{4,6},{5,7},{6,4},{7,5},{8,10},{9,11},{10,... | collective-permute-start | bytes 884744 | tf_op jit(solution)/shard_map/ppermute | solution.py:25
  54.5 1.9 %collective-permute-done.10.refs_2_.refs_3_ = bf16[1024,128]{1,0:T(8,128)(2,1)S(1)} collective-permute-done((bf16[1024,128]{1,0:T(8,128)(2,1)}, bf16[1024,128]{1,0:T(8,128)(2,1)S(1)}, u32[]{:S(2)}, u32[]{:S(2)}) %collective-permute-start.10) | collective-permute-done | bytes 262176 | tf_op jit(solution)/shard_map/ppermute | solution.py:25
  56.4 2.2 %collective-permute-start.14 = (bf16[8,144,128]{2,1,0:T(8,128)(2,1)S(1)}, bf16[8,144,128]{2,1,0:T(8,128)(2,1)S(1)}, u32[]{:S(2)}, u32[]{:S(2)}) collective-permute-start(bf16[8,144,128]{2,1,0:T(8,128)(2,1)S(1)} %get-tuple-element.26.refs_0_), channel_id=1, source_target_pairs={{0,3},{1,0},{2,1},{3,2},{4,7},{5,4},{6,5},{7,6},{8,11},{9,8},{10,9... | collective-permute-start | bytes 884744 | tf_op jit(solution)/shard_map/ppermute | solution.py:25
  59.8 2.1 %collective-permute-start.22 = (bf16[1,2,10,32,128]{4,3,2,1,0:T(8,128)(2,1)S(1)}, bf16[1,2,10,32,128]{4,3,2,1,0:T(8,128)(2,1)S(1)}, u32[]{:S(2)}, u32[]{:S(2)}) collective-permute-start(bf16[1,2,10,32,128]{4,3,2,1,0:T(8,128)(2,1)S(1)} %get-tuple-element.20), channel_id=1, source_target_pairs={{0,3},{1,0},{2,1},{3,2},{4,7},{5,4},{6,5},{7,6},{8,11},{9,8},{10,9... | collective-permute-start | bytes 491528 | tf_op jit(solution)/shard_map/ppermute | solution.py:25
  62.3 9.9 %collective-permute-done.22.refs_3_.refs_2_ = bf16[1,2,10,32,128]{4,3,2,1,0:T(8,128)(2,1)S(1)} collective-permute-done((bf16[1,2,10,32,128]{4,3,2,1,0:T(8,128)(2,1)S(1)}, bf16[1,2,10,32,128]{4,3,2,1,0:T(8,128)(2,1)S(1)}, u32[]{:S(2)}, u32[]{:S(2)}) %collective-permute-start.22) | collective-permute-done | bytes 163872 | tf_op jit(solution)/shard_map/ppermute | solution.py:25
  72.2 2.2 %collective-permute-start.23 = (bf16[1,2,10,32,128]{4,3,2,1,0:T(8,128)(2,1)S(1)}, bf16[1,2,10,32,128]{4,3,2,1,0:T(8,128)(2,1)S(1)}, u32[]{:S(2)}, u32[]{:S(2)}) collective-permute-start(bf16[1,2,10,32,128]{4,3,2,1,0:T(8,128)(2,1)S(1)} %get-tuple-element.21), channel_id=1, source_target_pairs={{0,2},{1,3},{2,0},{3,1},{4,6},{5,7},{6,4},{7,5},{8,10},{9,11},{10,... | collective-permute-start | bytes 491528 | tf_op jit(solution)/shard_map/ppermute | solution.py:25
  74.4 2.2 %collective-permute-start.12 = (bf16[1,2,10,32,128]{4,3,2,1,0:T(8,128)(2,1)S(1)}, bf16[1,2,10,32,128]{4,3,2,1,0:T(8,128)(2,1)S(1)}, u32[]{:S(2)}, u32[]{:S(2)}) collective-permute-start(bf16[1,2,10,32,128]{4,3,2,1,0:T(8,128)(2,1)S(1)} %get-tuple-element.16), channel_id=1, source_target_pairs={{0,4},{1,5},{2,6},{3,7},{4,8},{5,9},{6,10},{7,11},{8,12},{9,13},{1... | collective-permute-start | bytes 491528 | tf_op jit(solution)/shard_map/ppermute | solution.py:25
  76.7 6.5 %collective-permute-done.13.refs_0_.refs_1_ = bf16[8,144,128]{2,1,0:T(8,128)(2,1)S(1)} collective-permute-done((bf16[8,144,128]{2,1,0:T(8,128)(2,1)S(1)}, bf16[8,144,128]{2,1,0:T(8,128)(2,1)S(1)}, u32[]{:S(2)}, u32[]{:S(2)}) %collective-permute-start.13) | collective-permute-done | bytes 294944 | tf_op jit(solution)/shard_map/ppermute | solution.py:25
  90.0 2.0 %collective-permute-start.18 = (bf16[3,2,10,32,128]{4,3,2,1,0:T(8,128)(2,1)S(1)}, bf16[3,2,10,32,128]{4,3,2,1,0:T(8,128)(2,1)S(1)}, u32[]{:S(2)}, u32[]{:S(2)}) collective-permute-start(bf16[3,2,10,32,128]{4,3,2,1,0:T(8,128)(2,1)S(1)} %shard_map.75), channel_id=1, source_target_pairs={{0,12},{1,13},{2,14},{3,15},{4,0},{5,1},{6,2},{7,3},{8,4},{9,5},{1... | collective-permute-start | bytes 1474568 | tf_op jit(solution)/shard_map/ppermute | solution.py:25
  92.0 4.1 %collective-permute-start.20 = (bf16[3,2,10,32,128]{4,3,2,1,0:T(8,128)(2,1)S(1)}, bf16[3,2,10,32,128]{4,3,2,1,0:T(8,128)(2,1)S(1)}, u32[]{:S(2)}, u32[]{:S(2)}) collective-permute-start(bf16[3,2,10,32,128]{4,3,2,1,0:T(8,128)(2,1)S(1)} %shard_map.76), channel_id=1, source_target_pairs={{0,8},{1,9},{2,10},{3,11},{4,12},{5,13},{6,14},{7,15},{8,0},{9,1},... | collective-permute-start | bytes 1474568 | tf_op jit(solution)/shard_map/ppermute | solution.py:25
  98.7 3.8 %collective-permute-done.6.refs_4_.refs_1_ = bf16[3,2,10,32,128]{4,3,2,1,0:T(8,128)(2,1)S(1)} collective-permute-done((bf16[3,2,10,32,128]{4,3,2,1,0:T(8,128)(2,1)S(1)}, bf16[3,2,10,32,128]{4,3,2,1,0:T(8,128)(2,1)S(1)}, u32[]{:S(2)}, u32[]{:S(2)}) %collective-permute-start.6) | collective-permute-done | bytes 491552 | tf_op jit(solution)/shard_map/ppermute | solution.py:25
  103.9 7.8 %collective-permute-done.18.refs_6_ = bf16[3,2,10,32,128]{4,3,2,1,0:T(8,128)(2,1)S(1)} collective-permute-done((bf16[3,2,10,32,128]{4,3,2,1,0:T(8,128)(2,1)S(1)}, bf16[3,2,10,32,128]{4,3,2,1,0:T(8,128)(2,1)S(1)}, u32[]{:S(2)}, u32[]{:S(2)}) %collective-permute-start.18) | collective-permute-done | bytes 491552 | tf_op jit(solution)/shard_map/ppermute | solution.py:25
  111.7 2.6 %shard_map.82 = (bf16[192,8192]{1,0:T(8,128)(2,1)}, bf16[16,4,128,128]{3,2,1,0:T(8,128)(2,1)}) custom-call(bf16[3,2,10,32,128]{4,3,2,1,0:T(8,128)(2,1)S(1)} %collective-permute-done.4.refs_2_.refs_0_, bf16[3,2,10,32,128]{4,3,2,1,0:T(8,128)(2,1)S(1)} %collective-permute-done.6.refs_4_.refs_1_, ...), custom_call_target="tpu_custom_call", output_to_operand_aliasing={{0}: (10, {}), {1}: (11, {})} | custom-call | bytes 6291456 | tf_op jit(solution)/shard_map/pallas_call | solution.py:43
  (44 shorter events, 18.6 us)
Async XLA Ops:
  3.0 25.7 %all-to-all-start = ((bf16[16,144,128]{2,1,0:T(8,128)(2,1)}), bf16[16,144,128]{2,1,0:T(8,128)(2,1)S(1)}, u32[]{:S(2)}, u32[]{:S(2)}) async-start(bf16[16,144,128]{2,1,0:T(8,128)(2,1)} %shard_map.68.after), calls=%async_computation | async-start | bytes 1179648 | tf_op jit(solution)/shard_map/all_to_all | solution.py:312
  13.3 9.3 %collective-permute-start = (bf16[1024,128]{1,0:T(8,128)(2,1)}, bf16[1024,128]{1,0:T(8,128)(2,1)S(1)}, u32[]{:S(2)}, u32[]{:S(2)}) collective-permute-start(bf16[1024,128]{1,0:T(8,128)(2,1)} %shard_map.69.refs_4_), channel_id=1, source_target_pairs={{0,3},{1,0},{2,1},{3,2},{4,7},{5,4},{6,5},{7,6},{8,11},{9,8},{10,9... | collective-permute-start | bytes 786440 | tf_op jit(solution)/shard_map/ppermute | solution.py:25
  28.7 20.0 %collective-permute-start.3 = (bf16[8,144,128]{2,1,0:T(8,128)(2,1)S(1)}, bf16[8,144,128]{2,1,0:T(8,128)(2,1)S(1)}, u32[]{:S(2)}, u32[]{:S(2)}) collective-permute-start(bf16[8,144,128]{2,1,0:T(8,128)(2,1)S(1)} %get-tuple-element.27.refs_0_), channel_id=1, source_target_pairs={{0,8},{1,9},{2,10},{3,11},{4,12},{5,13},{6,14},{7,15},{8,0},{9,1},... | collective-permute-start | bytes 884744 | tf_op jit(solution)/shard_map/ppermute | solution.py:25
  30.1 10.4 %collective-permute-start.7 = (bf16[1024,128]{1,0:T(8,128)(2,1)}, bf16[1024,128]{1,0:T(8,128)(2,1)S(1)}, u32[]{:S(2)}, u32[]{:S(2)}) collective-permute-start(bf16[1024,128]{1,0:T(8,128)(2,1)} %shard_map.69.refs_4_), channel_id=1, source_target_pairs={{0,2},{1,3},{2,0},{3,1},{4,6},{5,7},{6,4},{7,5},{8,10},{9,11},{10,... | collective-permute-start | bytes 786440 | tf_op jit(solution)/shard_map/ppermute | solution.py:25
  33.1 13.5 %collective-permute-start.5 = (bf16[1024,128]{1,0:T(8,128)(2,1)}, bf16[1024,128]{1,0:T(8,128)(2,1)S(1)}, u32[]{:S(2)}, u32[]{:S(2)}) collective-permute-start(bf16[1024,128]{1,0:T(8,128)(2,1)} %shard_map.69.refs_4_), channel_id=1, source_target_pairs={{0,1},{1,2},{2,3},{3,0},{4,5},{5,6},{6,7},{7,4},{8,9},{9,10},{10,1... | collective-permute-start | bytes 786440 | tf_op jit(solution)/shard_map/ppermute | solution.py:25
  33.7 15.5 %collective-permute-start.2 = (bf16[8,144,128]{2,1,0:T(8,128)(2,1)S(1)}, bf16[8,144,128]{2,1,0:T(8,128)(2,1)S(1)}, u32[]{:S(2)}, u32[]{:S(2)}) collective-permute-start(bf16[8,144,128]{2,1,0:T(8,128)(2,1)S(1)} %get-tuple-element.27.refs_0_), channel_id=1, source_target_pairs={{0,12},{1,13},{2,14},{3,15},{4,0},{5,1},{6,2},{7,3},{8,4},{9,5},{1... | collective-permute-start | bytes 884744 | tf_op jit(solution)/shard_map/ppermute | solution.py:25
  33.7 16.6 %collective-permute-start.1 = (bf16[8,144,128]{2,1,0:T(8,128)(2,1)S(1)}, bf16[8,144,128]{2,1,0:T(8,128)(2,1)S(1)}, u32[]{:S(2)}, u32[]{:S(2)}) collective-permute-start(bf16[8,144,128]{2,1,0:T(8,128)(2,1)S(1)} %get-tuple-element.27.refs_0_), channel_id=1, source_target_pairs={{0,4},{1,5},{2,6},{3,7},{4,8},{5,9},{6,10},{7,11},{8,12},{9,13},{1... | collective-permute-start | bytes 884744 | tf_op jit(solution)/shard_map/ppermute | solution.py:25
  40.5 10.9 %collective-permute-start.11 = (bf16[1024,128]{1,0:T(8,128)(2,1)}, bf16[1024,128]{1,0:T(8,128)(2,1)S(1)}, u32[]{:S(2)}, u32[]{:S(2)}) collective-permute-start(bf16[1024,128]{1,0:T(8,128)(2,1)} %shard_map.69.refs_4_), channel_id=1, source_target_pairs={{0,8},{1,9},{2,10},{3,11},{4,12},{5,13},{6,14},{7,15},{8,0},{9,1},... | collective-permute-start | bytes 786440 | tf_op jit(solution)/shard_map/ppermute | solution.py:25
  46.5 9.9 %collective-permute-start.10 = (bf16[1024,128]{1,0:T(8,128)(2,1)}, bf16[1024,128]{1,0:T(8,128)(2,1)S(1)}, u32[]{:S(2)}, u32[]{:S(2)}) collective-permute-start(bf16[1024,128]{1,0:T(8,128)(2,1)} %shard_map.69.refs_4_), channel_id=1, source_target_pairs={{0,4},{1,5},{2,6},{3,7},{4,8},{5,9},{6,10},{7,11},{8,12},{9,13},{1... | collective-permute-start | bytes 786440 | tf_op jit(solution)/shard_map/ppermute | solution.py:25
  48.7 9.9 %collective-permute-start.9 = (bf16[1024,128]{1,0:T(8,128)(2,1)}, bf16[1024,128]{1,0:T(8,128)(2,1)S(1)}, u32[]{:S(2)}, u32[]{:S(2)}) collective-permute-start(bf16[1024,128]{1,0:T(8,128)(2,1)} %shard_map.69.refs_4_), channel_id=1, source_target_pairs={{0,12},{1,13},{2,14},{3,15},{4,0},{5,1},{6,2},{7,3},{8,4},{9,5},{1... | collective-permute-start | bytes 786440 | tf_op jit(solution)/shard_map/ppermute | solution.py:25
  49.2 10.6 %collective-permute-start.21 = (bf16[1,2,10,32,128]{4,3,2,1,0:T(8,128)(2,1)S(1)}, bf16[1,2,10,32,128]{4,3,2,1,0:T(8,128)(2,1)S(1)}, u32[]{:S(2)}, u32[]{:S(2)}) collective-permute-start(bf16[1,2,10,32,128]{4,3,2,1,0:T(8,128)(2,1)S(1)} %get-tuple-element.19), channel_id=1, source_target_pairs={{0,1},{1,2},{2,3},{3,0},{4,5},{5,6},{6,7},{7,4},{8,9},{9,10},{10,1... | collective-permute-start | bytes 491528 | tf_op jit(solution)/shard_map/ppermute | solution.py:25
  50.7 41.3 %collective-permute-start.4 = (bf16[3,2,10,32,128]{4,3,2,1,0:T(8,128)(2,1)S(1)}, bf16[3,2,10,32,128]{4,3,2,1,0:T(8,128)(2,1)S(1)}, u32[]{:S(2)}, u32[]{:S(2)}) collective-permute-start(bf16[3,2,10,32,128]{4,3,2,1,0:T(8,128)(2,1)S(1)} %shard_map.70), channel_id=1, source_target_pairs={{0,1},{1,2},{2,3},{3,0},{4,5},{5,6},{6,7},{7,4},{8,9},{9,10},{10,1... | collective-permute-start | bytes 1474568 | tf_op jit(solution)/shard_map/ppermute | solution.py:25
  51.4 23.1 %collective-permute-start.15 = (bf16[8,144,128]{2,1,0:T(8,128)(2,1)S(1)}, bf16[8,144,128]{2,1,0:T(8,128)(2,1)S(1)}, u32[]{:S(2)}, u32[]{:S(2)}) collective-permute-start(bf16[8,144,128]{2,1,0:T(8,128)(2,1)S(1)} %get-tuple-element.26.refs_0_), channel_id=1, source_target_pairs={{0,2},{1,3},{2,0},{3,1},{4,6},{5,7},{6,4},{7,5},{8,10},{9,11},{10,... | collective-permute-start | bytes 884744 | tf_op jit(solution)/shard_map/ppermute | solution.py:25
  56.4 20.2 %collective-permute-start.14 = (bf16[8,144,128]{2,1,0:T(8,128)(2,1)S(1)}, bf16[8,144,128]{2,1,0:T(8,128)(2,1)S(1)}, u32[]{:S(2)}, u32[]{:S(2)}) collective-permute-start(bf16[8,144,128]{2,1,0:T(8,128)(2,1)S(1)} %get-tuple-element.26.refs_0_), channel_id=1, source_target_pairs={{0,3},{1,0},{2,1},{3,2},{4,7},{5,4},{6,5},{7,6},{8,11},{9,8},{10,9... | collective-permute-start | bytes 884744 | tf_op jit(solution)/shard_map/ppermute | solution.py:25
  58.6 24.5 %collective-permute-start.13 = (bf16[8,144,128]{2,1,0:T(8,128)(2,1)S(1)}, bf16[8,144,128]{2,1,0:T(8,128)(2,1)S(1)}, u32[]{:S(2)}, u32[]{:S(2)}) collective-permute-start(bf16[8,144,128]{2,1,0:T(8,128)(2,1)S(1)} %get-tuple-element.26.refs_0_), channel_id=1, source_target_pairs={{0,1},{1,2},{2,3},{3,0},{4,5},{5,6},{6,7},{7,4},{8,9},{9,10},{10,1... | collective-permute-start | bytes 884744 | tf_op jit(solution)/shard_map/ppermute | solution.py:25
  59.8 12.4 %collective-permute-start.22 = (bf16[1,2,10,32,128]{4,3,2,1,0:T(8,128)(2,1)S(1)}, bf16[1,2,10,32,128]{4,3,2,1,0:T(8,128)(2,1)S(1)}, u32[]{:S(2)}, u32[]{:S(2)}) collective-permute-start(bf16[1,2,10,32,128]{4,3,2,1,0:T(8,128)(2,1)S(1)} %get-tuple-element.20), channel_id=1, source_target_pairs={{0,3},{1,0},{2,1},{3,2},{4,7},{5,4},{6,5},{7,6},{8,11},{9,8},{10,9... | collective-permute-start | bytes 491528 | tf_op jit(solution)/shard_map/ppermute | solution.py:25
  72.2 15.0 %collective-permute-start.23 = (bf16[1,2,10,32,128]{4,3,2,1,0:T(8,128)(2,1)S(1)}, bf16[1,2,10,32,128]{4,3,2,1,0:T(8,128)(2,1)S(1)}, u32[]{:S(2)}, u32[]{:S(2)}) collective-permute-start(bf16[1,2,10,32,128]{4,3,2,1,0:T(8,128)(2,1)S(1)} %get-tuple-element.21), channel_id=1, source_target_pairs={{0,2},{1,3},{2,0},{3,1},{4,6},{5,7},{6,4},{7,5},{8,10},{9,11},{10,... | collective-permute-start | bytes 491528 | tf_op jit(solution)/shard_map/ppermute | solution.py:25
  74.4 14.0 %collective-permute-start.12 = (bf16[1,2,10,32,128]{4,3,2,1,0:T(8,128)(2,1)S(1)}, bf16[1,2,10,32,128]{4,3,2,1,0:T(8,128)(2,1)S(1)}, u32[]{:S(2)}, u32[]{:S(2)}) collective-permute-start(bf16[1,2,10,32,128]{4,3,2,1,0:T(8,128)(2,1)S(1)} %get-tuple-element.16), channel_id=1, source_target_pairs={{0,4},{1,5},{2,6},{3,7},{4,8},{5,9},{6,10},{7,11},{8,12},{9,13},{1... | collective-permute-start | bytes 491528 | tf_op jit(solution)/shard_map/ppermute | solution.py:25
  76.7 11.7 %collective-permute-start.17 = (bf16[1,2,10,32,128]{4,3,2,1,0:T(8,128)(2,1)S(1)}, bf16[1,2,10,32,128]{4,3,2,1,0:T(8,128)(2,1)S(1)}, u32[]{:S(2)}, u32[]{:S(2)}) collective-permute-start(bf16[1,2,10,32,128]{4,3,2,1,0:T(8,128)(2,1)S(1)} %get-tuple-element.17), channel_id=1, source_target_pairs={{0,12},{1,13},{2,14},{3,15},{4,0},{5,1},{6,2},{7,3},{8,4},{9,5},{1... | collective-permute-start | bytes 491528 | tf_op jit(solution)/shard_map/ppermute | solution.py:25
  87.2 16.7 %collective-permute-start.16 = (bf16[3,2,10,32,128]{4,3,2,1,0:T(8,128)(2,1)S(1)}, bf16[3,2,10,32,128]{4,3,2,1,0:T(8,128)(2,1)S(1)}, u32[]{:S(2)}, u32[]{:S(2)}) collective-permute-start(bf16[3,2,10,32,128]{4,3,2,1,0:T(8,128)(2,1)S(1)} %shard_map.74), channel_id=1, source_target_pairs={{0,4},{1,5},{2,6},{3,7},{4,8},{5,9},{6,10},{7,11},{8,12},{9,13},{1... | collective-permute-start | bytes 1474568 | tf_op jit(solution)/shard_map/ppermute | solution.py:25
  88.4 14.1 %collective-permute-start.6 = (bf16[3,2,10,32,128]{4,3,2,1,0:T(8,128)(2,1)S(1)}, bf16[3,2,10,32,128]{4,3,2,1,0:T(8,128)(2,1)S(1)}, u32[]{:S(2)}, u32[]{:S(2)}) collective-permute-start(bf16[3,2,10,32,128]{4,3,2,1,0:T(8,128)(2,1)S(1)} %shard_map.71), channel_id=1, source_target_pairs={{0,3},{1,0},{2,1},{3,2},{4,7},{5,4},{6,5},{7,6},{8,11},{9,8},{10,9... | collective-permute-start | bytes 1474568 | tf_op jit(solution)/shard_map/ppermute | solution.py:25
  88.4 14.1 %collective-permute-start.8 = (bf16[3,2,10,32,128]{4,3,2,1,0:T(8,128)(2,1)S(1)}, bf16[3,2,10,32,128]{4,3,2,1,0:T(8,128)(2,1)S(1)}, u32[]{:S(2)}, u32[]{:S(2)}) collective-permute-start(bf16[3,2,10,32,128]{4,3,2,1,0:T(8,128)(2,1)S(1)} %shard_map.72), channel_id=1, source_target_pairs={{0,2},{1,3},{2,0},{3,1},{4,6},{5,7},{6,4},{7,5},{8,10},{9,11},{10,... | collective-permute-start | bytes 1474568 | tf_op jit(solution)/shard_map/ppermute | solution.py:25
  90.0 21.7 %collective-permute-start.18 = (bf16[3,2,10,32,128]{4,3,2,1,0:T(8,128)(2,1)S(1)}, bf16[3,2,10,32,128]{4,3,2,1,0:T(8,128)(2,1)S(1)}, u32[]{:S(2)}, u32[]{:S(2)}) collective-permute-start(bf16[3,2,10,32,128]{4,3,2,1,0:T(8,128)(2,1)S(1)} %shard_map.75), channel_id=1, source_target_pairs={{0,12},{1,13},{2,14},{3,15},{4,0},{5,1},{6,2},{7,3},{8,4},{9,5},{1... | collective-permute-start | bytes 1474568 | tf_op jit(solution)/shard_map/ppermute | solution.py:25
  92.0 19.7 %collective-permute-start.20 = (bf16[3,2,10,32,128]{4,3,2,1,0:T(8,128)(2,1)S(1)}, bf16[3,2,10,32,128]{4,3,2,1,0:T(8,128)(2,1)S(1)}, u32[]{:S(2)}, u32[]{:S(2)}) collective-permute-start(bf16[3,2,10,32,128]{4,3,2,1,0:T(8,128)(2,1)S(1)} %shard_map.76), channel_id=1, source_target_pairs={{0,8},{1,9},{2,10},{3,11},{4,12},{5,13},{6,14},{7,15},{8,0},{9,1},... | collective-permute-start | bytes 1474568 | tf_op jit(solution)/shard_map/ppermute | solution.py:25
  (2 other events, 17.1 us)
